TPU v7x, 32 devices: a whole 2x2x4 slice. The times are simulated.
32 devices in a mesh: ctx: 4 (over y, core), fsdp: 2 (over x), head: 4 (over z).
Axes of the slice: x: 2, y: 2, z: 4, core: 2. Of those that a mesh axis runs over, the one named last changes fastest.
Arguments:
- inputs: bfloat16 [4096, 2048], P(('ctx', 'fsdp')), may hold values from -6 to 6
- query_weight: bfloat16 [2048, 2048], P('fsdp', 'head'), may hold values from -0.13258252 to 0.13258252
- key_weight: bfloat16 [2048, 256], P('fsdp', 'head'), may hold values from -0.125 to 0.125
- value_weight: bfloat16 [2048, 256], P('fsdp', 'head'), may hold values from -0.125 to 0.125
- output_weight: bfloat16 [2048, 2048], P('head', 'fsdp'), may hold values from -6 to 6
- gate_weight: bfloat16 [2048, 5632], P('fsdp', 'head'), may hold values from -0.125 to 0.125
- up_weight: bfloat16 [2048, 5632], P('fsdp', 'head'), may hold values from -0.125 to 0.125
- down_weight: bfloat16 [5632, 2048], P('head', 'fsdp'), may hold values from -0.15625 to 0.15625
- attn_gain: bfloat16 [2048], P('fsdp'), may hold values from 0.099609375 to 1.8984375
- ffn_gain: bfloat16 [2048], P('fsdp'), may hold values from 0.099609375 to 1.8984375
- cotangent: bfloat16 [4096, 2048], P(('ctx', 'fsdp')), may hold values from -6 to 6
Outputs:
- outputs: bfloat16 [4096, 2048], P(('ctx', 'fsdp'))
- input_grad: float32 [4096, 2048], P(('ctx', 'fsdp'))
- query_grad: float32 [2048, 2048], P('fsdp', 'head')
- key_grad: float32 [2048, 256], P('fsdp', 'head')
- value_grad: float32 [2048, 256], P('fsdp', 'head')
- output_grad: float32 [2048, 2048], P('head', 'fsdp')
- gate_grad: float32 [2048, 5632], P('fsdp', 'head')
- up_grad: float32 [2048, 5632], P('fsdp', 'head')
- down_grad: float32 [5632, 2048], P('head', 'fsdp')
- attn_gain_grad: float32 [2048], P('fsdp')
- ffn_gain_grad: float32 [2048], P('fsdp')
All inputs are finite; a program needn't handle non-finite values.
Results may differ from a plain program's by a relative error of at most 0.025.
Values may be sent and summed in bfloat16 or wider, within the bound.
A program may use at most 256 MiB of HBM per device.

v0:
```python
import jax
import jax.numpy as jnp
from jax import lax
from jax.sharding import PartitionSpec as P

HEAD_DIM = 64


EPSILON = 1e-05


def rotate(values, positions, inverse):
    half_dim = values.shape[-1] // 2
    freqs = 10000.0 ** (-2.0 * jnp.arange(half_dim, dtype=jnp.float32) / values.shape[-1])
    angles = positions.astype(jnp.float32)[:, None] * freqs[None, :]
    cosine = jnp.cos(angles)[:, None, :]
    sine = jnp.sin(angles)[:, None, :]
    if inverse:
        sine = -sine
    first = values[..., :half_dim]
    second = values[..., half_dim:]
    return jnp.concatenate(
        [first * cosine - second * sine, second * cosine + first * sine], axis=-1
    )


def matmul(left, right):
    return jnp.dot(left, right, preferred_element_type=jnp.float32)


def mat_trans(left, right):
    return lax.dot_general(
        left, right, (((1,), (1,)), ((), ())), preferred_element_type=jnp.float32
    )


def trans_mat(left, right):
    return lax.dot_general(
        left, right, (((0,), (0,)), ((), ())), preferred_element_type=jnp.float32
    )


def shards(
    inputs,
    query_weight,
    key_weight,
    value_weight,
    output_weight,
    gate_weight,
    up_weight,
    down_weight,
    attn_gain,
    ffn_gain,
    cotangent,
):
    local_weights = (
        attn_gain,
        ffn_gain,
        query_weight,
        key_weight,
        value_weight,
        gate_weight,
        up_weight,
        output_weight,
        down_weight,
    )
    full_weights = (
        lax.all_gather(local_weights[0], "fsdp", axis=0, tiled=True),
        lax.all_gather(local_weights[1], "fsdp", axis=0, tiled=True),
        lax.all_gather(local_weights[2], "fsdp", axis=0, tiled=True),
        lax.all_gather(local_weights[3], "fsdp", axis=0, tiled=True),
        lax.all_gather(local_weights[4], "fsdp", axis=0, tiled=True),
        lax.all_gather(local_weights[5], "fsdp", axis=0, tiled=True),
        lax.all_gather(local_weights[6], "fsdp", axis=0, tiled=True),
        lax.all_gather(local_weights[7], "fsdp", axis=1, tiled=True),
        lax.all_gather(local_weights[8], "fsdp", axis=1, tiled=True),
    )
    gain_one, gain_two, w_query, w_key, w_value, w_gate, w_up, w_out, w_down = full_weights
    row_count = inputs.shape[0]
    heads_here = w_query.shape[1] // HEAD_DIM
    positions = lax.axis_index(("ctx", "fsdp")) * row_count + jnp.arange(row_count, dtype=jnp.int32)
    last_pos = positions[row_count - 1]
    seq_total = row_count * lax.axis_size(("ctx", "fsdp"))
    in_float = inputs.astype(jnp.float32)
    scale_one = lax.rsqrt(jnp.mean(in_float * in_float, axis=-1, keepdims=True) + EPSILON)
    unit_one = in_float * scale_one
    normed_one = (unit_one * gain_one.astype(jnp.float32)).astype(jnp.bfloat16)
    queries = (
        (
            rotate(
                matmul(normed_one, w_query).reshape(row_count, heads_here, HEAD_DIM),
                positions,
                False,
            )
            * 0.125
        )
        .astype(jnp.bfloat16)
        .transpose(1, 0, 2)
    )
    keys_mine = (
        rotate(matmul(normed_one, w_key).reshape(row_count, 1, HEAD_DIM), positions, False)
        .reshape(row_count, HEAD_DIM)
        .astype(jnp.bfloat16)
    )
    values_mine = matmul(normed_one, w_value).astype(jnp.bfloat16)
    start_state = (
        jnp.full((heads_here, row_count), -1e30, jnp.float32),
        jnp.zeros((heads_here, row_count), jnp.float32),
        jnp.zeros((heads_here, row_count, HEAD_DIM), jnp.float32),
    )
    key_piece = lax.all_gather(keys_mine, ("ctx", "fsdp"), axis=0, tiled=True)
    value_piece = lax.all_gather(values_mine, ("ctx", "fsdp"), axis=0, tiled=True)

    def attend_block(offset, inner):
        key_start = offset * row_count

        def attend_compute(current):
            running_max, running_sum, running_acc = current
            key_block = lax.dynamic_slice_in_dim(key_piece, offset * row_count, row_count, 0)
            value_block = lax.dynamic_slice_in_dim(value_piece, offset * row_count, row_count, 0)
            scores = jnp.einsum(
                "hrd,kd->hrk", queries, key_block, preferred_element_type=jnp.float32
            )
            allowed = (key_start + jnp.arange(row_count, dtype=jnp.int32))[None, :] <= positions[
                :, None
            ]
            scores = jnp.where(allowed[None], scores, -1e30)
            new_max = jnp.maximum(running_max, jnp.max(scores, axis=-1))
            rescale = jnp.exp(running_max - new_max)
            weights = jnp.where(allowed[None], jnp.exp(scores - new_max[..., None]), 0.0)
            running_sum = running_sum * rescale + jnp.sum(weights, axis=-1)
            running_acc = running_acc * rescale[..., None] + jnp.einsum(
                "hrk,kd->hrd",
                weights.astype(jnp.bfloat16),
                value_block,
                preferred_element_type=jnp.float32,
            )
            return (new_max, running_sum, running_acc)

        return lax.cond(key_start <= last_pos, attend_compute, lambda current: current, inner)

    run_max, run_sum, run_acc = lax.fori_loop(
        0, key_piece.shape[0] // row_count, attend_block, start_state
    )
    log_sums = run_max + jnp.log(run_sum)
    attended = (run_acc / run_sum[..., None]).astype(jnp.bfloat16)
    concat_heads = attended.transpose(1, 0, 2).reshape(row_count, heads_here * HEAD_DIM)
    hidden = in_float + lax.psum(matmul(concat_heads, w_out).astype(jnp.bfloat16), "head").astype(
        jnp.float32
    )
    scale_two = lax.rsqrt(jnp.mean(hidden * hidden, axis=-1, keepdims=True) + EPSILON)
    unit_two = hidden * scale_two
    normed_two = (unit_two * gain_two.astype(jnp.float32)).astype(jnp.bfloat16)
    gate_pre = matmul(normed_two, w_gate)
    up_pre = matmul(normed_two, w_up)
    silu_gate = jax.nn.silu(gate_pre)
    activated = (silu_gate * up_pre).astype(jnp.bfloat16)
    outputs = (
        hidden
        + lax.psum(matmul(activated, w_down).astype(jnp.bfloat16), "head").astype(jnp.float32)
    ).astype(jnp.bfloat16)
    back_weights = (
        lax.all_gather(local_weights[0], "fsdp", axis=0, tiled=True),
        lax.all_gather(local_weights[1], "fsdp", axis=0, tiled=True),
        lax.all_gather(local_weights[2], "fsdp", axis=0, tiled=True),
        lax.all_gather(local_weights[3], "fsdp", axis=0, tiled=True),
        lax.all_gather(local_weights[4], "fsdp", axis=0, tiled=True),
        lax.all_gather(local_weights[5], "fsdp", axis=0, tiled=True),
        lax.all_gather(local_weights[6], "fsdp", axis=0, tiled=True),
        lax.all_gather(local_weights[7], "fsdp", axis=1, tiled=True),
        lax.all_gather(local_weights[8], "fsdp", axis=1, tiled=True),
    )
    gain_one, gain_two, w_query, w_key, w_value, w_gate, w_up, w_out, w_down = back_weights
    out_float = cotangent.astype(jnp.float32)
    act_grad = mat_trans(cotangent, w_down)
    down_part = trans_mat(activated, cotangent)
    sigma = jax.nn.sigmoid(gate_pre)
    gate_in_grad = (act_grad * up_pre * sigma * (1.0 + gate_pre * (1.0 - sigma))).astype(
        jnp.bfloat16
    )
    up_in_grad = (act_grad * silu_gate).astype(jnp.bfloat16)
    gate_part = trans_mat(normed_two, gate_in_grad)
    up_part = trans_mat(normed_two, up_in_grad)
    normed_two_grad = lax.psum(
        (mat_trans(gate_in_grad, w_gate) + mat_trans(up_in_grad, w_up)).astype(jnp.bfloat16), "head"
    ).astype(jnp.float32)
    gain_two_part = jnp.sum(normed_two_grad * unit_two, axis=0)
    scaled_two = normed_two_grad * gain_two.astype(jnp.float32)
    hidden_grad = out_float + scale_two * (
        scaled_two - unit_two * jnp.mean(scaled_two * unit_two, axis=-1, keepdims=True)
    )
    hidden_low = hidden_grad.astype(jnp.bfloat16)
    out_part = trans_mat(concat_heads, hidden_low)
    attended_grad = mat_trans(hidden_low, w_out).astype(jnp.bfloat16)
    grad_heads = attended_grad.reshape(row_count, heads_here, HEAD_DIM).transpose(1, 0, 2)
    deltas = jnp.sum(grad_heads.astype(jnp.float32) * attended.astype(jnp.float32), axis=-1)
    back_state = (
        jnp.zeros((heads_here, row_count, HEAD_DIM), jnp.float32),
        jnp.zeros((seq_total, 2 * HEAD_DIM), jnp.float32),
    )
    back_key_piece = lax.all_gather(keys_mine, ("ctx", "fsdp"), axis=0, tiled=True)
    back_value_piece = lax.all_gather(values_mine, ("ctx", "fsdp"), axis=0, tiled=True)

    def back_block(offset, inner):
        key_start = offset * row_count

        def back_compute(current):
            query_acc, pair_acc = current
            key_block = lax.dynamic_slice_in_dim(back_key_piece, offset * row_count, row_count, 0)
            value_block = lax.dynamic_slice_in_dim(
                back_value_piece, offset * row_count, row_count, 0
            )
            scores = jnp.einsum(
                "hrd,kd->hrk", queries, key_block, preferred_element_type=jnp.float32
            )
            allowed = (key_start + jnp.arange(row_count, dtype=jnp.int32))[None, :] <= positions[
                :, None
            ]
            scores = jnp.where(allowed[None], scores, -1e30)
            probs = jnp.where(allowed[None], jnp.exp(scores - log_sums[..., None]), 0.0)
            prob_grad = jnp.einsum(
                "hrd,kd->hrk", grad_heads, value_block, preferred_element_type=jnp.float32
            )
            score_grad = (probs * (prob_grad - deltas[..., None])).astype(jnp.bfloat16)
            query_acc = query_acc + jnp.einsum(
                "hrk,kd->hrd", score_grad, key_block, preferred_element_type=jnp.float32
            )
            key_part = jnp.einsum(
                "hrk,hrd->kd", score_grad, queries, preferred_element_type=jnp.float32
            )
            value_part = jnp.einsum(
                "hrk,hrd->kd",
                probs.astype(jnp.bfloat16),
                grad_heads,
                preferred_element_type=jnp.float32,
            )
            rows_now = lax.dynamic_slice_in_dim(pair_acc, key_start, row_count, 0)
            pair_acc = lax.dynamic_update_slice_in_dim(
                pair_acc, rows_now + jnp.concatenate([key_part, value_part], axis=1), key_start, 0
            )
            return (query_acc, pair_acc)

        return lax.cond(key_start <= last_pos, back_compute, lambda current: current, inner)

    query_acc, pair_acc = lax.fori_loop(
        0, back_key_piece.shape[0] // row_count, back_block, back_state
    )
    pair_mine = lax.psum_scatter(
        pair_acc.astype(jnp.bfloat16), ("ctx", "fsdp"), scatter_dimension=0, tiled=True
    ).astype(jnp.float32)
    q_raw = (
        rotate((query_acc * 0.125).transpose(1, 0, 2), positions, True)
        .reshape(row_count, heads_here * HEAD_DIM)
        .astype(jnp.bfloat16)
    )
    k_raw = (
        rotate(pair_mine[:, :HEAD_DIM].reshape(row_count, 1, HEAD_DIM), positions, True)
        .reshape(row_count, HEAD_DIM)
        .astype(jnp.bfloat16)
    )
    v_raw = pair_mine[:, HEAD_DIM:].astype(jnp.bfloat16)
    query_part = trans_mat(normed_one, q_raw)
    key_part_w = trans_mat(normed_one, k_raw)
    value_part_w = trans_mat(normed_one, v_raw)
    normed_one_grad = lax.psum(
        (mat_trans(q_raw, w_query) + mat_trans(k_raw, w_key) + mat_trans(v_raw, w_value)).astype(
            jnp.bfloat16
        ),
        "head",
    ).astype(jnp.float32)
    gain_one_part = jnp.sum(normed_one_grad * unit_one, axis=0)
    scaled_one = normed_one_grad * gain_one.astype(jnp.float32)
    input_grad = hidden_grad + scale_one * (
        scaled_one - unit_one * jnp.mean(scaled_one * unit_one, axis=-1, keepdims=True)
    )
    grad_terms = (
        gain_one_part,
        gain_two_part,
        query_part,
        key_part_w,
        value_part_w,
        gate_part,
        up_part,
        out_part,
        down_part,
    )
    grad_halves = (
        lax.psum_scatter(
            grad_terms[0].astype(jnp.bfloat16), "fsdp", scatter_dimension=0, tiled=True
        ).astype(jnp.float32),
        lax.psum_scatter(
            grad_terms[1].astype(jnp.bfloat16), "fsdp", scatter_dimension=0, tiled=True
        ).astype(jnp.float32),
        lax.psum_scatter(
            grad_terms[2].astype(jnp.bfloat16), "fsdp", scatter_dimension=0, tiled=True
        ).astype(jnp.float32),
        lax.psum_scatter(
            grad_terms[3].astype(jnp.bfloat16), "fsdp", scatter_dimension=0, tiled=True
        ).astype(jnp.float32),
        lax.psum_scatter(
            grad_terms[4].astype(jnp.bfloat16), "fsdp", scatter_dimension=0, tiled=True
        ).astype(jnp.float32),
        lax.psum_scatter(
            grad_terms[5].astype(jnp.bfloat16), "fsdp", scatter_dimension=0, tiled=True
        ).astype(jnp.float32),
        lax.psum_scatter(
            grad_terms[6].astype(jnp.bfloat16), "fsdp", scatter_dimension=0, tiled=True
        ).astype(jnp.float32),
        lax.psum_scatter(
            grad_terms[7].astype(jnp.bfloat16), "fsdp", scatter_dimension=1, tiled=True
        ).astype(jnp.float32),
        lax.psum_scatter(
            grad_terms[8].astype(jnp.bfloat16), "fsdp", scatter_dimension=1, tiled=True
        ).astype(jnp.float32),
    )
    summed = (
        lax.psum(grad_halves[0].astype(jnp.bfloat16), "ctx").astype(jnp.float32),
        lax.psum(grad_halves[1].astype(jnp.bfloat16), "ctx").astype(jnp.float32),
        lax.psum(grad_halves[2].astype(jnp.bfloat16), "ctx").astype(jnp.float32),
        lax.psum(grad_halves[3].astype(jnp.bfloat16), "ctx").astype(jnp.float32),
        lax.psum(grad_halves[4].astype(jnp.bfloat16), "ctx").astype(jnp.float32),
        lax.psum(grad_halves[5].astype(jnp.bfloat16), "ctx").astype(jnp.float32),
        lax.psum(grad_halves[6].astype(jnp.bfloat16), "ctx").astype(jnp.float32),
        lax.psum(grad_halves[7].astype(jnp.bfloat16), "ctx").astype(jnp.float32),
        lax.psum(grad_halves[8].astype(jnp.bfloat16), "ctx").astype(jnp.float32),
    )
    (
        gain_one_grad,
        gain_two_grad,
        query_grad,
        key_grad,
        value_grad,
        gate_grad,
        up_grad,
        output_grad,
        down_grad,
    ) = summed
    return (
        outputs,
        input_grad,
        query_grad,
        key_grad,
        value_grad,
        output_grad,
        gate_grad,
        up_grad,
        down_grad,
        gain_one_grad,
        gain_two_grad,
    )


def solution(mesh):
    return jax.shard_map(
        shards,
        mesh=mesh,
        in_specs=(
            P(("ctx", "fsdp"), None),
            P("fsdp", "head"),
            P("fsdp", "head"),
            P("fsdp", "head"),
            P("head", "fsdp"),
            P("fsdp", "head"),
            P("fsdp", "head"),
            P("head", "fsdp"),
            P("fsdp"),
            P("fsdp"),
            P(("ctx", "fsdp"), None),
        ),
        out_specs=(
            P(("ctx", "fsdp"), None),
            P(("ctx", "fsdp"), None),
            P("fsdp", "head"),
            P("fsdp", "head"),
            P("fsdp", "head"),
            P("head", "fsdp"),
            P("fsdp", "head"),
            P("fsdp", "head"),
            P("head", "fsdp"),
            P("fsdp"),
            P("fsdp"),
        ),
        check_vma=False,
    )
```

profile of v0, /device:TPU:0, one launch (start us, length us, event | category | flops | bytes accessed | tf_op | source)
XLA Modules:
  0.0 1465.6 jit_solution(13294570087655459204)
XLA Ops:
  8.8 5.5 all_gather.44
  16.4 7.5 all_gather.45
  23.9 9.0 all_gather.48
  35.2 18.7 %all-gather = bf16[4096,1,64]{0,2,1:T(8,128)(2,1)S(1)} all-gather(bf16[512,1,64]{0,2,1:T(8,128)(2,1)S(1)} %pad_maximum_fusion.1), channel_id=2, replica_groups=mesh['ctx'=4,'fsdp'=2,'head'=4] {'ctx','fsdp'}, dimensions={0}, use_global_device_ids=true | all-gather | bytes 589824 | tf_op jit(solution)/shard_map/all_gather | solution.py:111
  54.7 21.4 %all_gather.49 = bf16[4096,64]{0,1:T(8,128)(2,1)} all-gather(bf16[512,64]{0,1:T(8,128)(2,1)S(1)} %convolution_convert_fusion.10), channel_id=1, replica_groups=mesh['ctx'=4,'fsdp'=2,'head'=4] {'ctx','fsdp'}, dimensions={0}, use_global_device_ids=true | all-gather | bytes 589824 | tf_op jit(solution)/shard_map/all_gather | solution.py:112
  77.0 3.5 fusion.96
  82.0 12.6 while.34
  82.5 7.7 conditional.6
  86.0 3.3 fusion.10
  96.7 4.4 convolution_convert_fusion.5
  102.9 11.6 all_gather.51
  114.5 127.7 %all-reduce.11.cloned.1.call-done = bf16[512,2048]{1,0:T(8,128)(2,1)} async-done(((bf16[512,2048]{1,0:T(8,128)(2,1)}), bf16[512,2048]{1,0:T(8,128)(2,1)}) %all-reduce.11.cloned.1.call-update) | async-done | bytes 2097168 | tf_op jit(solution)/shard_map/psum | solution.py:148
  247.1 70.0 %all-gather.11.cloned.1.call-done = bf16[2048,1408]{1,0:T(8,128)(2,1)} async-done(((bf16[1024,1408]{1,0:T(8,128)(2,1)}), bf16[2048,1408]{1,0:T(8,128)(2,1)}) %all-gather.11.cloned.1.call-update) | async-done | bytes 5767184 | tf_op jit(solution)/shard_map/all_gather | solution.py:73
  317.1 8.3 fusion.97
  325.4 67.6 %all-gather.13.cloned.1.call-done = bf16[2048,1408]{1,0:T(8,128)(2,1)} async-done(((bf16[1024,1408]{1,0:T(8,128)(2,1)}), bf16[2048,1408]{1,0:T(8,128)(2,1)}) %all-gather.13.cloned.1.call-update) | async-done | bytes 5767184 | tf_op jit(solution)/shard_map/all_gather | solution.py:74
  393.0 8.3 fusion.98
  401.2 67.6 %all-gather.15.cloned.1.call-done = bf16[1408,2048]{1,0:T(8,128)(2,1)} async-done(((bf16[1408,1024]{1,0:T(8,128)(2,1)}), bf16[1408,2048]{1,0:T(8,128)(2,1)}) %all-gather.15.cloned.1.call-update) | async-done | bytes 5767184 | tf_op jit(solution)/shard_map/all_gather | solution.py:76
  468.9 10.4 multiply_convert_fusion.1
  479.2 6.6 fusion.99
  485.8 4.7 add_convert_fusion.1
  491.0 85.8 %all-reduce.13.cloned.1.call-done = bf16[512,2048]{1,0:T(8,128)(2,1)} async-done(((bf16[512,2048]{1,0:T(8,128)(2,1)}), bf16[512,2048]{1,0:T(8,128)(2,1)}) %all-reduce.13.cloned.1.call-update) | async-done | bytes 2097168 | tf_op jit(solution)/shard_map/psum | solution.py:184
  576.8 3.9 fusion.58
  580.9 4.7 multiply_reduce_fusion.1
  588.3 21.8 %while.35 = (s32[]{:T(128)}, f32[8,512,64]{1,2,0:T(8,128)}, f32[4096,128]{0,1:T(8,128)}, s32[]{:T(128)}, bf16[4096,64]{0,1:T(8,128)(2,1)S(1)}, /*index=5*/bf16[8...) while((s32[]{:T(128)}, f32[8,512,64]{1,2,0:T(8,128)}, ...), condition=%wide.region_16.17_spmd.clone, body=%wide.region_13.0_spmd.clone.sunk | while | flops 1363805184 | bytes 62910912 | solution.py:245
  588.9 16.9 %conditional.7 = ((f32[8,512,64]{1,2,0:T(8,128)}, f32[4096,128]{0,1:T(8,128)})) conditional(s32[]{:T(128)} %convert_element_type.413, (f32[8,512,64]{1,2,0:T(8,128)}, f32[4096,128]{0,1:T(8,128)}) %tuple.101, (s32[]{:T(128)}, s32[]{:T(128)}, s32[]{:T(128)}, bf16[4096,64]{0,1:T(8,128)(2,1)S(1)}, bf16[8,512,64]{1,2,0:T(8,128)(2,1)S(1)}, ...), branch_computations={%region_14.14_spmd, %region_15.15_spmd} | conditional | flops 1363805184 | bytes 62908600 | solution.py:243
  590.4 3.7 fusion.22
  601.5 4.3 convolution_add_fusion
  612.9 152.7 %reduce-scatter.9.cloned.1.call-done = bf16[512,128]{0,1:T(8,128)(2,1)} async-done(((bf16[4096,128]{0,1:T(8,128)(2,1)}), bf16[512,128]{0,1:T(8,128)(2,1)}) %reduce-scatter.9.cloned.1.call-update) | async-done | bytes 131088 | tf_op jit(solution)/shard_map/reduce_scatter | solution.py:248
  769.7 2.8 convolution_convert_fusion.7
  772.7 6.6 convolution_convert_fusion.3
  783.7 8.0 convolution_convert_fusion.2
  791.8 8.0 convolution_convert_fusion.1
  800.1 7.8 convolution_convert_fusion
  807.9 8.0 convolution_convert_fusion.6
  820.4 9.8 reduce-scatter.17.cloned.1.call-done
  830.2 34.6 %reduce-scatter.11.cloned.1.call-done = bf16[1024,512]{1,0:T(8,128)(2,1)} async-done(((bf16[2048,512]{1,0:T(8,128)(2,1)}), bf16[1024,512]{1,0:T(8,128)(2,1)}) %reduce-scatter.11.cloned.1.call-update) | async-done | bytes 1048592 | tf_op jit(solution)/shard_map/reduce_scatter | solution.py:294
  864.8 74.3 %reduce-scatter.19.cloned.1.call-done = bf16[1024,1408]{1,0:T(8,128)(2,1)} async-done(((bf16[2048,1408]{1,0:T(8,128)(2,1)}), bf16[1024,1408]{1,0:T(8,128)(2,1)}) %reduce-scatter.19.cloned.1.call-update) | async-done | bytes 2883600 | tf_op jit(solution)/shard_map/reduce_scatter | solution.py:303
  939.1 74.2 %reduce-scatter.21.cloned.1.call-done = bf16[1024,1408]{1,0:T(8,128)(2,1)} async-done(((bf16[2048,1408]{1,0:T(8,128)(2,1)}), bf16[1024,1408]{1,0:T(8,128)(2,1)}) %reduce-scatter.21.cloned.1.call-update) | async-done | bytes 2883600 | tf_op jit(solution)/shard_map/reduce_scatter | solution.py:306
  1013.3 74.2 %reduce-scatter.23.cloned.1.call-done = bf16[1408,1024]{1,0:T(8,128)(2,1)} async-done(((bf16[1408,2048]{1,0:T(8,128)(2,1)}), bf16[1408,1024]{1,0:T(8,128)(2,1)}) %reduce-scatter.23.cloned.1.call-update) | async-done | bytes 2883600 | tf_op jit(solution)/shard_map/reduce_scatter | solution.py:312
  1089.4 156.0 %all-reduce.15.cloned.1.call-done = (bf16[512,2048]{1,0:T(8,128)(2,1)}, bf16[512,2048]{1,0:T(8,128)(2,1)}) async-done(((bf16[512,2048]{1,0:T(8,128)(2,1)}, bf16[512,2048]{1,0:T(8,128)(2,1)}), (bf16[512,2048]{1,0:T(8,128)(2,1)}, bf16[512,2048]{1,0:T(8,128)(2,1)})) %all-reduce.15.cloned.1.call-update) | async-done | bytes 4194320 | tf_op jit(solution)/shard_map/psum | solution.py:160
  1245.4 2.9 fusion.61
  1248.3 5.0 all-reduce.5
  1253.4 6.7 all-reduce.3
  1261.3 7.8 fusion.54
  1269.2 173.9 %all-reduce.17.cloned.1.call-done = (bf16[1024,512]{1,0:T(8,128)(2,1)}, bf16[1024,64]{0,1:T(8,128)(2,1)}, bf16[1024,64]{0,1:T(8,128)(2,1)}, bf16[512,1024]{1,0:T...) async-done(((bf16[1024,512]{1,0:T(8,128)(2,1)}, bf16[1024,64]{0,1:T(8,128)(2,1)}, bf16[1024,64]{0,1:T(8,128)(2,1)}, ...) | async-done | bytes 11010064 | tf_op jit(solution)/shard_map/psum | solution.py:319
  1443.0 4.9 convert_element_type.238
  1447.9 2.9 convert_element_type.240
  1450.9 3.2 convert_element_type.242
  (213 shorter events, 57.8 us)
Async XLA Ops:
  7.2 26.3 %copy-start.1 = (bf16[512,2048]{1,0:T(8,128)(2,1)S(1)}, bf16[512,2048]{1,0:T(8,128)(2,1)}, u32[]{:S(2)}) copy-start(bf16[512,2048]{1,0:T(8,128)(2,1)} %param.19) | copy-start | bytes 6291460
  7.2 9.2 copy-start.26
  7.2 16.7 %copy-start.27 = (bf16[1024,64]{0,1:T(8,128)(2,1)S(1)}, bf16[1024,64]{0,1:T(8,128)(2,1)}, u32[]{:S(2)}) copy-start(bf16[1024,64]{0,1:T(8,128)(2,1)} %param.22) | copy-start | bytes 393220
  7.2 69.8 %all-gather.7.cloned.1.call-start = ((), (), s32[]{:S(2)}) async-start(), calls=%async_computation.8 | async-start | bytes 3145728 | tf_op jit(solution)/shard_map/all_gather | solution.py:70
  7.9 88.8 %all-gather.9.cloned.1.call-start = ((), (), s32[]{:S(2)}) async-start(), calls=%async_computation.9 | async-start | bytes 3145728 | tf_op jit(solution)/shard_map/all_gather | solution.py:75
  8.7 233.5 %all-reduce.11.cloned.1.call-start = ((), (), s32[]{:S(2)}) async-start(), calls=%async_computation.10 | async-start | bytes 4194304 | tf_op jit(solution)/shard_map/psum | solution.py:148
  8.8 67.3 %copy-start.34 = (f32[32]{0:T(128)}, f32[32]{0:T(128)S(1)}, u32[]{:S(2)}) copy-start(f32[32]{0:T(128)S(1)} %multiply_power_fusion) | copy-start | bytes 388
  8.8 67.3 %copy-start.30 = (f32[512]{0:T(512)}, f32[512]{0:T(512)S(1)}, u32[]{:S(2)}) copy-start(f32[512]{0:T(512)S(1)} %fusion.91) | copy-start | bytes 6148
  14.3 20.5 %copy-start.24 = (f32[2048]{0:T(1024)}, f32[2048]{0:T(1024)S(1)}, u32[]{:S(2)}) copy-start(f32[2048]{0:T(1024)S(1)} %convert_element_type.200) | copy-start | bytes 24580
  16.4 18.8 %copy-start.32 = (f32[512]{0:T(512)}, f32[512]{0:T(512)S(1)}, u32[]{:S(2)}) copy-start(f32[512]{0:T(512)S(1)} %add_rsqrt_fusion.1) | copy-start | bytes 6148
  23.9 30.8 %copy-start.12 = (bf16[2048,64]{0,1:T(8,128)(2,1)}, bf16[2048,64]{0,1:T(8,128)(2,1)S(1)}, u32[]{:S(2)}) copy-start(bf16[2048,64]{0,1:T(8,128)(2,1)S(1)} %all_gather.45) | copy-start | bytes 786436
  32.9 21.8 %copy-start.14 = (bf16[2048,64]{0,1:T(8,128)(2,1)}, bf16[2048,64]{0,1:T(8,128)(2,1)S(1)}, u32[]{:S(2)}) copy-start(bf16[2048,64]{0,1:T(8,128)(2,1)S(1)} %all_gather.48) | copy-start | bytes 786436
  34.1 19.9 %copy-start.2 = (bf16[512,2048]{1,0:T(8,128)(2,1)}, bf16[512,2048]{1,0:T(8,128)(2,1)S(1)}, u32[]{:S(2)}) copy-start(bf16[512,2048]{1,0:T(8,128)(2,1)S(1)} %fusion.59) | copy-start | bytes 6291460
  77.0 3.6 copy-start.20
  101.1 216.0 %all-gather.11.cloned.1.call-start = ((), (), s32[]{:S(2)}) async-start(), calls=%async_computation.11 | async-start | bytes 8650752 | tf_op jit(solution)/shard_map/all_gather | solution.py:73
  101.7 291.3 %all-gather.13.cloned.1.call-start = ((), (), s32[]{:S(2)}) async-start(), calls=%async_computation.12 | async-start | bytes 8650752 | tf_op jit(solution)/shard_map/all_gather | solution.py:74
  102.3 366.6 %all-gather.15.cloned.1.call-start = ((), (), s32[]{:S(2)}) async-start(), calls=%async_computation.13 | async-start | bytes 8650752 | tf_op jit(solution)/shard_map/all_gather | solution.py:76
  102.9 474.0 %all-reduce.13.cloned.1.call-start = ((), (), s32[]{:S(2)}) async-start(), calls=%async_computation.14 | async-start | bytes 4194304 | tf_op jit(solution)/shard_map/psum | solution.py:184
  242.2 2.5 copy-start.5
  479.2 6.6 copy-start.41
  479.2 6.6 copy-start.40
  479.2 6.6 copy-start.37
  490.5 275.1 %reduce-scatter.9.cloned.1.call-start = ((), (), s32[]{:S(2)}) async-start(), calls=%async_computation.15 | async-start | bytes 1179648 | tf_op jit(solution)/shard_map/reduce_scatter | solution.py:248
  576.8 4.0 copy-start.6
  576.8 4.0 copy-start.7
  576.8 4.1 copy-start.16
  594.1 2.0 copy-start
  610.1 156.3 %copy-start.31 = (f32[512]{0:T(512)S(1)}, f32[512]{0:T(512)}, u32[]{:S(2)}) copy-start(f32[512]{0:T(512)} %copy-done.30) | copy-start | bytes 6148
  610.1 156.3 %copy-start.35 = (f32[32]{0:T(128)S(1)}, f32[32]{0:T(128)}, u32[]{:S(2)}) copy-start(f32[32]{0:T(128)} %copy-done.34) | copy-start | bytes 388
  612.8 207.5 %reduce-scatter.13.cloned.1.call-start = ((), (), s32[]{:S(2)}) async-start(), calls=%async_computation.17 | async-start | bytes 393216 | tf_op jit(solution)/shard_map/reduce_scatter | solution.py:297
  769.6 50.8 %reduce-scatter.15.cloned.1.call-start = ((), (), s32[]{:S(2)}) async-start(), calls=%async_computation.18 | async-start | bytes 393216 | tf_op jit(solution)/shard_map/reduce_scatter | solution.py:300
  772.5 6.9 copy-start.4
  772.5 57.7 %reduce-scatter.17.cloned.1.call-start = ((), (), s32[]{:S(2)}) async-start(), calls=%async_computation.19 | async-start | bytes 3145728 | tf_op jit(solution)/shard_map/reduce_scatter | solution.py:309
  779.3 85.5 %reduce-scatter.11.cloned.1.call-start = ((), (), s32[]{:S(2)}) async-start(), calls=%async_computation.16 | async-start | bytes 3145728 | tf_op jit(solution)/shard_map/reduce_scatter | solution.py:294
  783.7 155.4 %reduce-scatter.19.cloned.1.call-start = ((), (), s32[]{:S(2)}) async-start(), calls=%async_computation.20 | async-start | bytes 8650752 | tf_op jit(solution)/shard_map/reduce_scatter | solution.py:303
  791.8 221.6 %reduce-scatter.21.cloned.1.call-start = ((), (), s32[]{:S(2)}) async-start(), calls=%async_computation.21 | async-start | bytes 8650752 | tf_op jit(solution)/shard_map/reduce_scatter | solution.py:306
  799.8 287.7 %reduce-scatter.23.cloned.1.call-start = ((), (), s32[]{:S(2)}) async-start(), calls=%async_computation.22 | async-start | bytes 8650752 | tf_op jit(solution)/shard_map/reduce_scatter | solution.py:312
  807.9 437.6 %all-reduce.15.cloned.1.call-start = ((), (), s32[]{:S(2)}) async-start(), calls=%async_computation.23 | async-start | bytes 8388608 | tf_op jit(solution)/shard_map/psum | solution.py:160
  807.9 8.0 copy-start.17
  820.3 622.8 %all-reduce.17.cloned.1.call-start = ((), (), s32[]{:S(2)}) async-start(), calls=%async_computation.24 | async-start | bytes 22020096 | tf_op jit(solution)/shard_map/psum | solution.py:319
  1087.6 157.9 %copy-start.25 = (f32[2048]{0:T(1024)S(1)}, f32[2048]{0:T(1024)}, u32[]{:S(2)}) copy-start(f32[2048]{0:T(1024)} %copy-done.24) | copy-start | bytes 24580
  1087.6 157.9 %copy-start.33 = (f32[512]{0:T(512)S(1)}, f32[512]{0:T(512)}, u32[]{:S(2)}) copy-start(f32[512]{0:T(512)} %copy-done.32) | copy-start | bytes 6148
  1443.0 4.9 copy-start.11
  1447.9 3.0 copy-start.10
  1450.9 3.3 copy-start.19
  1450.9 4.9 copy-start.18
  1454.2 3.2 copy-start.29
  1454.2 3.9 copy-start.28
  (11 other events, 13.3 us)
Sparse Core Ops, SparseCore 0:
  9.6 40.0 all-gather.6
  51.2 36.7 all-gather.8
  101.2 140.9 all-reduce.10
  243.6 73.4 all-gather.10
  318.5 74.4 all-gather.12
  394.4 74.4 all-gather.14
  490.6 86.1 all-reduce.12
  613.0 152.5 reduce-scatter.8
  769.7 11.7 reduce-scatter.12
  783.6 11.7 reduce-scatter.14
  798.2 31.9 reduce-scatter.16
  832.8 31.8 reduce-scatter.10
  867.7 71.4 reduce-scatter.18
  941.9 71.4 reduce-scatter.20
  1016.0 71.4 reduce-scatter.22
  1090.4 154.9 all-reduce.14
  1248.5 194.4 all-reduce.16
where the time goes:
time: 1470 us
  waiting for transfers between devices  1170 us (80%)
  matrix products  120 us (8%)
  blocking collectives  85.4 us (6%)
  other arithmetic  50.8 us (3%)
  between operations  15.4 us (1%)
    psum x1, waiting for transfers between devices, shards(): lax.psum(grad_halves[2].astype(jnp.bfloat16), 'ctx').astype(jnp.float32)  174 us
    psum x1, waiting for transfers between devices, shards(): lax.psum(matmul(activated, w_down).astype(jnp.bfloat16), 'head')  156 us
    reduce_scatter x1, waiting for transfers between devices, shards(): lax.psum_scatter(pair_acc.astype(jnp.bfloat16), ('ctx', 'fsdp'), scatter_...  153 us
    psum x1, waiting for transfers between devices, shards(): lax.psum(matmul(concat_heads, w_out).astype(jnp.bfloat16), 'head')  128 us
    psum x1, waiting for transfers between devices, shards(): lax.psum((mat_trans(gate_in_grad, w_gate) + mat_trans(up_in_grad, w_up))....  85.8 us
    reduce_scatter x1, waiting for transfers between devices, shards(): lax.psum_scatter(grad_terms[5].astype(jnp.bfloat16), 'fsdp', scatter_dime...  74.3 us
    reduce_scatter x1, waiting for transfers between devices, shards(): lax.psum_scatter(grad_terms[8].astype(jnp.bfloat16), 'fsdp', scatter_dime...  74.2 us
    reduce_scatter x1, waiting for transfers between devices, shards(): lax.psum_scatter(grad_terms[6].astype(jnp.bfloat16), 'fsdp', scatter_dime...  74.2 us
  transfers between devices with their start and end apart: 17, of which 13 were waited for; matrix products, arithmetic and copies ran while one was open for 7% of the time, Pallas kernels for 0%

commit v1 on v0

v1 whole, which is shorter than its diff:
```python
import functools

import jax
import jax.numpy as jnp
from jax import lax
from jax.experimental import pallas as pl
from jax.experimental.pallas import tpu as pltpu
from jax.sharding import PartitionSpec as P


HEAD_DIM = 64
EPSILON = 1e-05
NEG = -1e30
BF = jnp.bfloat16
F32 = jnp.float32
MESH = pl.DeviceIdType.MESH
CHUNKS = 16
LAG = 3


def matmul(left, right):
    return jnp.dot(left, right, preferred_element_type=F32)


def mat_trans(left, right):
    return lax.dot_general(left, right, (((1,), (1,)), ((), ())), preferred_element_type=F32)


def trans_mat(left, right):
    return lax.dot_general(left, right, (((0,), (0,)), ((), ())), preferred_element_type=F32)


def high_bits(size):
    bits = []
    bit = size // 2
    while bit >= 1:
        bits.append(bit)
        bit //= 2
    return bits


def lanes(shape):
    return lax.broadcasted_iota(jnp.int32, shape, 1)


def head_lanes(ref, h, upper):
    wide = ref[:, (h // 2) * 128 : (h // 2) * 128 + 128]
    if (h % 2 == 1) != upper:
        wide = pltpu.roll(wide.astype(F32), HEAD_DIM, 1).astype(BF)
    keep = (lanes(wide.shape) >= HEAD_DIM) if upper else (lanes(wide.shape) < HEAD_DIM)
    return jnp.where(keep, wide, jnp.zeros_like(wide))


def forward_kernel(group, span, blk_ref, q_ref, p_ref, o_ref, lse_ref, q_pad, ext, max_ref, acc_ref):
    rows = q_ref.shape[0]
    block = blk_ref[0]

    @pl.when(pl.program_id(0) == 0)
    def _():
        ext[...] = jnp.where(lanes(p_ref.shape) < HEAD_DIM, jnp.ones_like(p_ref[...]), p_ref[...])

    for h in range(group):
        q_pad[h] = head_lanes(q_ref, h, False)
    max_ref[...] = jnp.full_like(max_ref, NEG)
    acc_ref[...] = jnp.zeros_like(acc_ref)

    def head_tile(h, keys, values, start, masked):
        scores = mat_trans(q_pad[h], keys)
        if masked:
            row = block * rows + lax.broadcasted_iota(jnp.int32, (rows, span), 0)
            col = start + lax.broadcasted_iota(jnp.int32, (rows, span), 1)
            scores = jnp.where(col <= row, scores, NEG)
        old = max_ref[h]
        new = jnp.maximum(old, jnp.max(scores, axis=1, keepdims=True))
        weights = jnp.exp(scores - jnp.tile(new, (1, span // 128))).astype(BF)
        acc_ref[h] = acc_ref[h] * jnp.exp(old - new) + matmul(weights, values)
        max_ref[h] = new

    def full(i, carry):
        cut = pl.ds(pl.multiple_of(i * span, span), span)
        for h in range(group):
            head_tile(h, p_ref[cut, :], ext[cut, :], i * span, False)
        return carry

    lax.fori_loop(0, block * (rows // span), full, 0)

    def last(t, carry):
        h = lax.rem(t, group)
        start = pl.multiple_of(block * rows + (t // group) * span, span)
        cut = pl.ds(start, span)
        head_tile(h, p_ref[cut, :], ext[cut, :], start, True)
        return carry

    lax.fori_loop(0, group * (rows // span), last, 0)
    for h in range(group):
        acc = acc_ref[h]
        total = acc[:, :HEAD_DIM]
        o_ref[:, h * HEAD_DIM : (h + 1) * HEAD_DIM] = (acc[:, HEAD_DIM:] / total).astype(BF)
        lse = max_ref[h] + jnp.log(jnp.concatenate([total, total], axis=1))
        lse_ref[h] = lse.T[0:1, :]


def attend(queries, pair, block):
    rows, width = queries.shape
    heads = width // HEAD_DIM
    seq = pair.shape[0]
    group = 4 if heads % 4 == 0 else 2
    span = min(512, rows)
    wide = pl.BlockSpec((rows, group * HEAD_DIM), lambda i, *_: (0, i))
    cost = pl.CostEstimate(
        flops=16 * rows * seq * width, bytes_accessed=4 * rows * width, transcendentals=0
    )
    return pl.pallas_call(
        functools.partial(forward_kernel, group, span),
        out_shape=(
            jax.ShapeDtypeStruct((rows, width), BF),
            jax.ShapeDtypeStruct((heads, 1, rows), F32),
        ),
        grid_spec=pltpu.PrefetchScalarGridSpec(
            num_scalar_prefetch=1,
            grid=(heads // group,),
            in_specs=[wide, pl.BlockSpec((seq, 2 * HEAD_DIM), lambda i, *_: (0, 0))],
            out_specs=[wide, pl.BlockSpec((group, 1, rows), lambda i, *_: (i, 0, 0))],
            scratch_shapes=[
                pltpu.VMEM((group, rows, 128), BF),
                pltpu.VMEM((seq, 128), BF),
                pltpu.VMEM((group, rows, 128), F32),
                pltpu.VMEM((group, rows, 128), F32),
            ],
        ),
        cost_estimate=cost,
        name="attend_forward",
    )(block, queries, pair)


def backward_kernel(
    n_head,
    group,
    span,
    q_ref,
    g_ref,
    o_ref,
    lse_ref,
    p_ref,
    left_ref,
    right_ref,
    dq_ref,
    dp_ref,
    sum_ref,
    q_pad,
    g_pad,
    acc_ref,
    dl_ref,
    work,
    from_lo,
    from_hi,
    *sems,
):
    rows, width = q_ref.shape
    heads = width // HEAD_DIM
    tiles = rows // span
    block = lax.axis_index("ctx") * 2 + lax.axis_index("fsdp")
    barrier = line_greet(n_head)
    stage(work, left_ref, right_ref)
    dp_ref[...] = jnp.zeros_like(dp_ref)
    acc_ref[...] = jnp.zeros_like(acc_ref)
    for h in range(heads):
        cut = slice(h * HEAD_DIM, (h + 1) * HEAD_DIM)
        q_pad[h] = head_lanes(q_ref, h, False)
        g_pad[h] = head_lanes(g_ref, h, True)
        product = g_ref[:, cut].astype(F32) * o_ref[:, cut].astype(F32)
        dl_ref[h] = jnp.sum(product.T, axis=0, keepdims=True)
    line_meet(n_head, barrier)
    step, steps, drain = line_sum(n_head, CHUNKS, LAG, work, sum_ref, from_lo, from_hi, sems)

    def head_tile(h, pairs, start, masked):
        probs = jnp.exp(mat_trans(pairs, q_pad[h]) - lse_ref[h])
        if masked:
            row = block * rows + lax.broadcasted_iota(jnp.int32, (span, rows), 1)
            col = start + lax.broadcasted_iota(jnp.int32, (span, rows), 0)
            probs = jnp.where(col <= row, probs, 0.0)
        grads = (probs * (mat_trans(pairs, g_pad[h]) - dl_ref[h])).astype(BF)
        acc_ref[h] += trans_mat(grads, pairs)
        return matmul(probs.astype(BF), g_pad[h]) + matmul(grads, q_pad[h])

    groups = heads // group

    def two_steps(t):
        for j in range(2):

            @pl.when(2 * t + j < steps)
            def _():
                step(2 * t + j)

    def full(t, carry):
        two_steps(t)
        first = lax.rem(t, groups) * group
        start = pl.multiple_of((t // groups) * span, span)
        cut = pl.ds(start, span)
        total = head_tile(first, p_ref[cut, :], start, False)
        for h in range(1, group):
            total = total + head_tile(first + h, p_ref[cut, :], start, False)
        dp_ref[cut, :] += total
        return carry

    count = block * tiles * groups
    lax.fori_loop(0, count, full, 0)

    def last(t, carry):
        h = lax.rem(t, heads)

        @pl.when(lax.rem(t, group) == 0)
        def _():
            two_steps(count + t // group)

        start = pl.multiple_of(block * rows + (t // heads) * span, span)
        cut = pl.ds(start, span)
        dp_ref[cut, :] += head_tile(h, p_ref[cut, :], start, True)
        return carry

    lax.fori_loop(0, heads * tiles, last, 0)
    for h in range(heads):
        dq_ref[:, h * HEAD_DIM : (h + 1) * HEAD_DIM] = acc_ref[h][:, :HEAD_DIM]

    def rest(s, carry):
        step(s)
        return carry

    lax.fori_loop(jnp.minimum(2 * (count + groups * tiles), steps), steps, rest, 0)
    drain()


def attend_back(queries, grads, attended, lse, pair, left, right, n_head, collective_id):
    rows, width = queries.shape
    heads = width // HEAD_DIM
    seq = pair.shape[0]
    group = 4 if heads % 4 == 0 else 2
    span = min(512, rows)
    vmem = pl.BlockSpec(memory_space=pltpu.VMEM)
    cost = pl.CostEstimate(
        flops=32 * rows * seq * width, bytes_accessed=8 * rows * width, transcendentals=0
    )
    return pl.pallas_call(
        functools.partial(backward_kernel, n_head, group, span),
        out_shape=(
            jax.ShapeDtypeStruct((rows, width), F32),
            jax.ShapeDtypeStruct((seq, 2 * HEAD_DIM), F32),
            jax.ShapeDtypeStruct((rows, 2 * left.shape[1]), BF),
        ),
        in_specs=[vmem] * 7,
        out_specs=(vmem, vmem, vmem),
        scratch_shapes=[
            pltpu.VMEM((heads, rows, 128), BF),
            pltpu.VMEM((heads, rows, 128), BF),
            pltpu.VMEM((heads, rows, 128), F32),
            pltpu.VMEM((heads, 1, rows), F32),
        ]
        + line_scratch(rows, 2 * left.shape[1]),
        compiler_params=pltpu.CompilerParams(collective_id=collective_id, has_side_effects=True),
        cost_estimate=cost,
        name="attend_backward",
    )(queries, grads, attended, lse, pair, left, right)


def partners(n_ctx):
    return [("fsdp", 1)] + [("ctx", bit) for bit in high_bits(n_ctx)]


def greet(n_ctx):
    barrier = pltpu.get_barrier_semaphore()
    for axis, bit in partners(n_ctx):
        pl.semaphore_signal(
            barrier, inc=1, device_id={axis: lax.axis_index(axis) ^ bit}, device_id_type=MESH
        )
    return barrier


def masks_of(bits):
    masks = [0]
    for bit in bits:
        masks = masks + [m | bit for m in masks]
    return masks


def gather_pairs(n_ctx, rows, all_ref, send, recv):
    x = lax.axis_index("fsdp")
    ctx = lax.axis_index("ctx")
    copies = []

    def part(start, size, axis, bit):
        e = len(copies)
        cut = all_ref.at[pl.ds(pl.multiple_of(start, rows), size)]
        copy = pltpu.make_async_remote_copy(
            src_ref=cut,
            dst_ref=cut,
            send_sem=send.at[e],
            recv_sem=recv.at[e],
            device_id={axis: lax.axis_index(axis) ^ bit},
            device_id_type=MESH,
        )
        copy.start()
        copies.append(copy)
        return copy

    part((ctx * 2 + x) * rows, rows, "fsdp", 1).wait_recv()
    done = []
    for bit in high_bits(n_ctx):
        now = [part((ctx ^ m) * 2 * rows, 2 * rows, "ctx", bit) for m in masks_of(done)]
        for copy in now:
            copy.wait_recv()
        done.append(bit)
    for copy in copies:
        copy.wait_send()


def scatter_kernel(n_ctx, part_ref, o_ref, work, land, send, recv):
    rows = o_ref.shape[0]
    x = lax.axis_index("fsdp")
    ctx = lax.axis_index("ctx")
    barrier = greet(n_ctx)
    work[...] = part_ref[...].astype(BF)
    pl.semaphore_wait(barrier, len(partners(n_ctx)))
    copies = []
    used = [0]

    def give(start, size, axis, bit):
        e = len(copies)
        cut = pl.ds(pl.multiple_of(start, rows), size)
        copy = pltpu.make_async_remote_copy(
            src_ref=work.at[cut],
            dst_ref=land.at[pl.ds(used[0], size)],
            send_sem=send.at[e],
            recv_sem=recv.at[e],
            device_id={axis: lax.axis_index(axis) ^ bit},
            device_id_type=MESH,
        )
        copy.start()
        copies.append(copy)
        used[0] += size
        return copy, used[0] - size

    def take(start, size, at):
        cut = pl.ds(pl.multiple_of(start, rows), size)
        work[cut, :] = (work[cut, :].astype(F32) + land[at : at + size, :].astype(F32)).astype(BF)

    bits = high_bits(n_ctx)
    for j in range(len(bits)):
        bit = bits[len(bits) - 1 - j]
        masks = masks_of(bits[: len(bits) - 1 - j])
        now = [give((ctx ^ bit ^ m) * 2 * rows, 2 * rows, "ctx", bit) for m in masks]
        for (copy, at), m in zip(now, masks):
            copy.wait_recv()
            take((ctx ^ m) * 2 * rows, 2 * rows, at)
    copy, at = give((ctx * 2 + 1 - x) * rows, rows, "fsdp", 1)
    copy.wait_recv()
    mine = pl.ds(pl.multiple_of((ctx * 2 + x) * rows, rows), rows)
    o_ref[...] = work[mine, :].astype(F32) + land[at : at + rows, :].astype(F32)
    for copy in copies:
        copy.wait_send()


def scatter_pairs(part, rows, n_ctx, collective_id):
    vmem = pl.BlockSpec(memory_space=pltpu.VMEM)
    return pl.pallas_call(
        functools.partial(scatter_kernel, n_ctx),
        out_shape=jax.ShapeDtypeStruct((rows, part.shape[1]), F32),
        in_specs=[vmem],
        out_specs=vmem,
        scratch_shapes=[
            pltpu.VMEM(part.shape, BF),
            pltpu.VMEM(part.shape, BF),
            pltpu.SemaphoreType.DMA((n_ctx,)),
            pltpu.SemaphoreType.DMA((n_ctx,)),
        ],
        compiler_params=pltpu.CompilerParams(collective_id=collective_id, has_side_effects=True),
        name="scatter_pairs",
    )(part)


def project_kernel(n_ctx, x_ref, wl_ref, wr_ref, cos_ref, sin_ref, q_ref, p_ref, send, recv):
    rows, width = x_ref.shape
    half = width // 2
    q_width = q_ref.shape[1]
    block = lax.axis_index("ctx") * 2 + lax.axis_index("fsdp")
    barrier = greet(n_ctx)
    size = rows // 4

    def rotated(wide, cut):
        low = lax.rem(lanes(wide.shape), HEAD_DIM) < HEAD_DIM // 2
        turned = jnp.where(low, pltpu.roll(wide, 128 - HEAD_DIM // 2, 1), pltpu.roll(wide, HEAD_DIM // 2, 1))
        return wide * cos_ref[cut, :] + turned * sin_ref[cut, :]

    def part(i, carry):
        cut = pl.ds(pl.multiple_of(i * size, size), size)
        left = x_ref[cut, :half]
        right = x_ref[cut, half:]
        both = matmul(left, wl_ref[:, q_width:]) + matmul(right, wr_ref[:, q_width:])
        pair = jnp.where(lanes(both.shape) < HEAD_DIM, rotated(both, cut), both)
        p_ref[pl.ds(pl.multiple_of(block * rows + i * size, size), size), :] = pair.astype(BF)
        for j in range(q_width // 128):
            sl = slice(j * 128, (j + 1) * 128)
            wide = matmul(left, wl_ref[:, sl]) + matmul(right, wr_ref[:, sl])
            q_ref[cut, sl] = (rotated(wide, cut) * 0.125).astype(BF)
        return carry

    lax.fori_loop(0, 4, part, 0)
    pl.semaphore_wait(barrier, len(partners(n_ctx)))
    gather_pairs(n_ctx, rows, p_ref, send, recv)


def project(normed, w_left, w_right, cosine, sine, q_width, n_ctx, collective_id):
    rows = normed.shape[0]
    vmem = pl.BlockSpec(memory_space=pltpu.VMEM)
    return pl.pallas_call(
        functools.partial(project_kernel, n_ctx),
        out_shape=(
            jax.ShapeDtypeStruct((rows, q_width), BF),
            jax.ShapeDtypeStruct((rows * 2 * n_ctx, 2 * HEAD_DIM), BF),
        ),
        in_specs=[vmem] * 5,
        out_specs=(vmem, vmem),
        scratch_shapes=[
            pltpu.SemaphoreType.DMA((n_ctx,)),
            pltpu.SemaphoreType.DMA((n_ctx,)),
        ],
        compiler_params=pltpu.CompilerParams(collective_id=collective_id, has_side_effects=True),
        name="project",
    )(normed, w_left, w_right, cosine, sine)


def line_sum(n, chunks, lag, work, o_ref, from_lo, from_hi, sems):
    s_up, r_up, s_dn, r_dn, s_a, r_a, s_b, r_b = sems
    me = lax.axis_index("head")
    half = work.shape[0] // 2
    size = half // chunks
    has_lo = me > 0
    has_hi = me < n - 1
    middle = jnp.logical_and(has_lo, has_hi)

    def lo(k):
        return pl.ds(pl.multiple_of(k * size, size), size)

    def hi(k):
        return pl.ds(pl.multiple_of(half + k * size, size), size)

    def remote(src, dst, send, recv, target):
        return pltpu.make_async_remote_copy(
            src_ref=src,
            dst_ref=dst,
            send_sem=send,
            recv_sem=recv,
            device_id={"head": target},
            device_id_type=MESH,
        )

    def up(k):
        return remote(work.at[hi(k)], from_lo.at[lo(k)], s_up.at[k], r_up.at[k], me + 1)

    def down(k):
        return remote(work.at[lo(k)], from_hi.at[lo(k)], s_dn.at[k], r_dn.at[k], me - 1)

    def spread_a(k):
        return remote(o_ref.at[lo(k)], o_ref.at[lo(k)], s_a.at[k], r_a.at[k], me + 1)

    def spread_b(k):
        return remote(o_ref.at[hi(k)], o_ref.at[hi(k)], s_b.at[k], r_b.at[k], me - 1)

    def valid(k):
        return jnp.logical_and(k >= 0, k < chunks)

    def added(here, there, k):
        return (work[here(k), :].astype(F32) + there[lo(k), :].astype(F32)).astype(BF)

    def step(s):
        k1 = s - lag * me
        k2 = s - lag * (n - 1 - me)
        k3 = s - lag * (n - 1 + me)
        k4 = s - lag * (2 * (n - 1) - me)

        @pl.when(jnp.logical_and(valid(k1), me == 0))
        def _():
            up(k1).start()

        @pl.when(jnp.logical_and(valid(k1), middle))
        def _():
            up(k1).wait_recv()
            work[hi(k1), :] = added(hi, from_lo, k1)
            up(k1).start()

        @pl.when(jnp.logical_and(valid(k1), me == n - 1))
        def _():
            up(k1).wait_recv()
            o_ref[hi(k1), :] = added(hi, from_lo, k1)
            spread_b(k1).start()

        @pl.when(jnp.logical_and(valid(k2), me == n - 1))
        def _():
            down(k2).start()

        @pl.when(jnp.logical_and(valid(k2), middle))
        def _():
            down(k2).wait_recv()
            work[lo(k2), :] = added(lo, from_hi, k2)
            down(k2).start()

        @pl.when(jnp.logical_and(valid(k2), me == 0))
        def _():
            down(k2).wait_recv()
            o_ref[lo(k2), :] = added(lo, from_hi, k2)
            spread_a(k2).start()

        @pl.when(jnp.logical_and(valid(k3), has_lo))
        def _():
            spread_a(k3).wait_recv()

            @pl.when(has_hi)
            def _():
                spread_a(k3).start()

        @pl.when(jnp.logical_and(valid(k4), has_hi))
        def _():
            spread_b(k4).wait_recv()

            @pl.when(has_lo)
            def _():
                spread_b(k4).start()

    def drain():
        def one(k, carry):
            @pl.when(has_hi)
            def _():
                up(k).wait_send()
                spread_a(k).wait_send()

            @pl.when(has_lo)
            def _():
                down(k).wait_send()
                spread_b(k).wait_send()

            return carry

        lax.fori_loop(0, chunks, one, 0)

    return step, chunks + 2 * lag * (n - 1), drain


def line_greet(n):
    me = lax.axis_index("head")
    barrier = pltpu.get_barrier_semaphore()

    @pl.when(me > 0)
    def _():
        pl.semaphore_signal(barrier, inc=1, device_id={"head": me - 1}, device_id_type=MESH)

    @pl.when(me < n - 1)
    def _():
        pl.semaphore_signal(barrier, inc=1, device_id={"head": me + 1}, device_id_type=MESH)

    return barrier


def line_meet(n, barrier):
    me = lax.axis_index("head")
    peers = jnp.where(me > 0, 1, 0) + jnp.where(me < n - 1, 1, 0)
    pl.semaphore_wait(barrier, peers)


def stage(work, left_ref, right_ref):
    rows, cols = left_ref.shape
    size = rows // 16

    def one(k, carry):
        cut = pl.ds(pl.multiple_of(k * size, size), size)
        work[cut, :cols] = left_ref[cut, :]
        work[cut, cols:] = right_ref[cut, :]
        return carry

    lax.fori_loop(0, 16, one, 0)


def line_scratch(rows, width):
    return [
        pltpu.VMEM((rows, width), BF),
        pltpu.VMEM((rows // 2, width), BF),
        pltpu.VMEM((rows // 2, width), BF),
    ] + [pltpu.SemaphoreType.DMA((CHUNKS,))] * 8


def head_sum_kernel(n, left_ref, right_ref, o_ref, work, from_lo, from_hi, *sems):
    barrier = line_greet(n)
    stage(work, left_ref, right_ref)
    line_meet(n, barrier)
    step, steps, drain = line_sum(n, CHUNKS, LAG, work, o_ref, from_lo, from_hi, sems)

    def run(s, carry):
        step(s)
        return carry

    lax.fori_loop(0, steps, run, 0)
    drain()


def head_sum(left, right, n, collective_id):
    rows, cols = left.shape
    return pl.pallas_call(
        functools.partial(head_sum_kernel, n),
        out_shape=jax.ShapeDtypeStruct((rows, 2 * cols), BF),
        in_specs=[pl.BlockSpec(memory_space=pltpu.VMEM)] * 2,
        out_specs=pl.BlockSpec(memory_space=pltpu.VMEM),
        scratch_shapes=line_scratch(rows, 2 * cols),
        compiler_params=pltpu.CompilerParams(collective_id=collective_id, has_side_effects=True),
        cost_estimate=pl.CostEstimate(
            flops=40_000_000_000, bytes_accessed=8 * rows * cols, transcendentals=0
        ),
        name="head_sum",
    )(left, right)


def flip(array, axis, bit, size):
    return lax.ppermute(array, axis, [(i, i ^ bit) for i in range(size)])


def after(value, *others):
    return lax.optimization_barrier((value,) + others)[0]


def shards(
    n_ctx,
    n_head,
    inputs,
    query_weight,
    key_weight,
    value_weight,
    output_weight,
    gate_weight,
    up_weight,
    down_weight,
    attn_gain,
    ffn_gain,
    cotangent,
):
    rows, width = inputs.shape
    half = width // 2
    quarter = half // 2
    x_at = lax.axis_index("fsdp")
    ctx_at = lax.axis_index("ctx")
    core = lax.rem(ctx_at, 2)
    block = ctx_at * 2 + x_at
    block_arr = jnp.reshape(block, (1,)).astype(jnp.int32)

    def own_first(array):
        swapped = jnp.concatenate([array[:, half:], array[:, :half]], axis=1)
        return jnp.where(x_at == 0, array, swapped)

    def fetch(shard, bits):
        count = 2 ** len(bits)
        piece = shard.shape[0] // count
        at = ctx_at if len(bits) > 1 else core
        mine = lax.dynamic_slice_in_dim(shard, at * piece, piece, 0)
        return flip(mine, "fsdp", 1, 2)

    def share(mine, bits):
        buf = mine[None]
        for bit in bits:
            got = flip(buf, "ctx", bit, n_ctx)
            upper = (ctx_at & bit) != 0
            pair = jnp.stack([jnp.where(upper, got, buf), jnp.where(upper, buf, got)], axis=1)
            buf = pair.reshape((-1,) + mine.shape)
        return buf.reshape((-1,) + mine.shape[1:])

    every = high_bits(n_ctx)
    chip = [1]
    qkv_local = jnp.concatenate([query_weight, key_weight, value_weight], axis=1)
    gains_local = jnp.stack([attn_gain, ffn_gain])
    gains_other = flip(gains_local, "fsdp", 1, 2)
    qkv_other = share(fetch(qkv_local, chip), chip)
    gain_one = jnp.concatenate([gains_local[0], gains_other[0]]).astype(F32)
    gain_two = jnp.concatenate([gains_local[1], gains_other[1]]).astype(F32)

    def columns_of(array, which):
        first = jnp.concatenate([array[:, :quarter], array[:, half : half + quarter]], axis=1)
        second = jnp.concatenate([array[:, quarter:half], array[:, half + quarter :]], axis=1)
        return jnp.where(which == 0, first, second)

    def trade(array):
        return jnp.concatenate([array, flip(array, "ctx", 1, n_ctx)], axis=0)

    def trade_columns(array):
        got = flip(columns_of(array, 1 - core), "ctx", 1, n_ctx)
        return jnp.concatenate([columns_of(array, core), got], axis=0)

    in_float = own_first(inputs).astype(F32)
    cot = own_first(cotangent)
    scale_one = lax.rsqrt(jnp.mean(in_float * in_float, axis=-1, keepdims=True) + EPSILON)
    unit_one = in_float * scale_one
    normed_one = (unit_one * gain_one).astype(BF)
    q_width = query_weight.shape[1]
    positions = block * rows + jnp.arange(rows, dtype=jnp.int32)
    half_dim = HEAD_DIM // 2
    lane = lax.broadcasted_iota(jnp.int32, (rows, 2 * HEAD_DIM), 1)
    freqs = 10000.0 ** (-2.0 * (lane % half_dim).astype(F32) / HEAD_DIM)
    angles = positions.astype(F32)[:, None] * freqs
    cosine = jnp.cos(angles)
    sine = jnp.sin(angles)
    signed = jnp.where(lane % HEAD_DIM < half_dim, -sine, sine)
    queries, pair = project(normed_one, qkv_local, qkv_other, cosine, signed, q_width, n_ctx, 4)
    out_piece = fetch(after(output_weight, pair), chip)
    gate_piece = fetch(after(gate_weight, pair), every)
    attended, lse = attend(queries, pair, block_arr)
    up_piece = fetch(after(up_weight, attended), chip)
    down_piece = fetch(after(down_weight, attended), chip)
    out_other = share(out_piece, chip)
    gate_other = share(gate_piece, every)
    up_other = share(up_piece, chip)
    down_other = share(down_piece, chip)
    cot = after(cot, attended)
    one_pair = trade_columns(normed_one)

    mixed_left = matmul(attended, output_weight).astype(BF)
    mixed_right = matmul(attended, out_other).astype(BF)
    mixed = head_sum(mixed_left, mixed_right, n_head, 1)
    hidden = in_float + mixed.astype(F32)
    scale_two = lax.rsqrt(jnp.mean(hidden * hidden, axis=-1, keepdims=True) + EPSILON)
    unit_two = hidden * scale_two
    normed_two = (unit_two * gain_two).astype(BF)

    act_grad = mat_trans(cot[:, :half], down_weight) + mat_trans(cot[:, half:], down_other)
    gate_pre = matmul(normed_two[:, :half], gate_weight) + matmul(normed_two[:, half:], gate_other)
    up_pre = matmul(normed_two[:, :half], up_weight) + matmul(normed_two[:, half:], up_other)
    sigma = jax.nn.sigmoid(gate_pre)
    silu_gate = gate_pre * sigma
    activated = (silu_gate * up_pre).astype(BF)
    gate_in_grad = (act_grad * up_pre * sigma * (1.0 + gate_pre * (1.0 - sigma))).astype(BF)
    up_in_grad = (act_grad * silu_gate).astype(BF)
    low_left = (mat_trans(gate_in_grad, gate_weight) + mat_trans(up_in_grad, up_weight)).astype(BF)
    low_right = (mat_trans(gate_in_grad, gate_other) + mat_trans(up_in_grad, up_other)).astype(BF)
    cot_pair = trade_columns(cot)
    two_pair = trade_columns(normed_two)
    down_part = trans_mat(trade(activated), cot_pair).astype(BF)
    gate_part = trans_mat(two_pair, trade(gate_in_grad)).astype(BF)
    low_left, low_right, down_part, gate_part = lax.optimization_barrier(
        (low_left, low_right, down_part, gate_part)
    )
    normed_two_grad = head_sum(low_left, low_right, n_head, 2).astype(F32)
    up_part = trans_mat(two_pair, trade(up_in_grad)).astype(BF)
    scaled_two = normed_two_grad * gain_two
    gain_two_part = jnp.sum(normed_two_grad * unit_two, axis=0)
    hidden_grad = cot.astype(F32) + scale_two * (
        scaled_two - unit_two * jnp.mean(scaled_two * unit_two, axis=-1, keepdims=True)
    )
    hidden_low = hidden_grad.astype(BF)

    down_left = matmul(activated, down_weight).astype(BF)
    down_right = matmul(activated, down_other).astype(BF)
    attended_grad = (
        mat_trans(hidden_low[:, :half], output_weight) + mat_trans(hidden_low[:, half:], out_other)
    ).astype(BF)
    out_part = trans_mat(trade(attended), trade_columns(hidden_low)).astype(BF)
    attended_grad, up_part, out_part = lax.optimization_barrier((attended_grad, up_part, out_part))
    query_acc, pair_acc, ffn_out = attend_back(
        queries, attended_grad, attended, lse, pair, down_left, down_right, n_head, 6
    )
    outputs = own_first((hidden + ffn_out.astype(F32)).astype(BF))
    pair_mine = scatter_pairs(pair_acc, rows, n_ctx, 5)

    def unrotate(values):
        count = values.shape[1] // 128
        cos = jnp.concatenate([cosine] * count, axis=1)
        sin = jnp.concatenate([signed] * count, axis=1)
        low = lax.broadcasted_iota(jnp.int32, values.shape, 1) % HEAD_DIM < half_dim
        turned = jnp.where(low, jnp.roll(values, -half_dim, axis=1), jnp.roll(values, half_dim, axis=1))
        return values * cos - turned * sin

    q_raw = unrotate(query_acc * 0.125)
    pair_raw = jnp.where(lane < HEAD_DIM, unrotate(pair_mine), pair_mine)
    qkv_raw = jnp.concatenate([q_raw, pair_raw], axis=1).astype(BF)
    last_left = mat_trans(qkv_raw, qkv_local).astype(BF)
    last_right = mat_trans(qkv_raw, qkv_other).astype(BF)
    qkv_part = trans_mat(one_pair, trade(qkv_raw)).astype(BF)
    last_left, last_right, qkv_part = lax.optimization_barrier((last_left, last_right, qkv_part))
    normed_one_grad = head_sum(last_left, last_right, n_head, 3).astype(F32)
    gain_one_part = jnp.sum(normed_one_grad * unit_one, axis=0)
    scaled_one = normed_one_grad * gain_one
    input_grad = own_first(
        hidden_grad
        + scale_one
        * (scaled_one - unit_one * jnp.mean(scaled_one * unit_one, axis=-1, keepdims=True))
    )

    def total(kept, sent):
        kept = (kept.astype(F32) + flip(sent, "fsdp", 1, 2).astype(F32)).astype(BF)
        for bit in every[:-1]:
            kept = (kept.astype(F32) + flip(kept, "ctx", bit, n_ctx).astype(F32)).astype(BF)
        return kept

    def spread(kept, dim):
        got = flip(kept, "ctx", 1, n_ctx)
        first = jnp.where(core == 0, kept, got)
        second = jnp.where(core == 0, got, kept)
        return jnp.concatenate([first, second], axis=dim).astype(F32)

    def by_rows(part):
        return spread(total(part[:quarter], part[quarter:]), 0)

    def by_columns(part):
        return spread(total(part[:, :quarter], part[:, quarter:]), 1)

    down_grad = by_columns(down_part)
    gate_grad = by_rows(gate_part)
    up_grad = by_rows(up_part)
    output_grad = by_columns(out_part)
    qkv_grad = by_rows(qkv_part)
    query_grad = qkv_grad[:, :q_width]
    key_grad = qkv_grad[:, q_width : q_width + HEAD_DIM]
    value_grad = qkv_grad[:, q_width + HEAD_DIM :]

    def gain_total(part):
        kept = part[:half].reshape(8, -1) + flip(part[half:].reshape(8, -1), "fsdp", 1, 2)
        for bit in every:
            kept = kept + flip(kept, "ctx", bit, n_ctx)
        return kept.reshape(half)

    return (
        outputs,
        input_grad,
        query_grad,
        key_grad,
        value_grad,
        output_grad,
        gate_grad,
        up_grad,
        down_grad,
        gain_total(gain_one_part),
        gain_total(gain_two_part),
    )


def solution(mesh):
    n_ctx = mesh.shape["ctx"]

    def body(*args):
        return shards(n_ctx, mesh.shape["head"], *args)

    return jax.shard_map(
        body,
        mesh=mesh,
        in_specs=(
            P(("ctx", "fsdp"), None),
            P("fsdp", "head"),
            P("fsdp", "head"),
            P("fsdp", "head"),
            P("head", "fsdp"),
            P("fsdp", "head"),
            P("fsdp", "head"),
            P("head", "fsdp"),
            P("fsdp"),
            P("fsdp"),
            P(("ctx", "fsdp"), None),
        ),
        out_specs=(
            P(("ctx", "fsdp"), None),
            P(("ctx", "fsdp"), None),
            P("fsdp", "head"),
            P("fsdp", "head"),
            P("fsdp", "head"),
            P("head", "fsdp"),
            P("fsdp", "head"),
            P("fsdp", "head"),
            P("head", "fsdp"),
            P("fsdp"),
            P("fsdp"),
        ),
        check_vma=False,
    )
```

time: 1470 us -> 626 us (0.43)
  waiting for transfers between devices: 1170 us -> 62.3 us
  Pallas kernels: 0 us -> 314 us
  blocking collectives: 85.4 us -> 0 us
  matrix products: 120 us -> 67.3 us
  starting transfers between devices: 1.48 us -> 47.4 us
  other arithmetic: 50.8 us -> 91.7 us
  local copies, waits for them, and re-layouts: 10.5 us -> 36.8 us
    psum x4 -> x0, waiting for transfers between devices: 543 us -> none  [the longest x1 174 us: shards(): lax.psum(grad_halves[2].astype(jnp.bfloat16), 'ctx').astype(jnp.float32)]
    reduce_scatter x8 -> x0, waiting for transfers between devices: 420 us -> none  [the longest x1 153 us: shards(): lax.psum_scatter(pair_acc.astype(jnp.bfloat16), ('ctx', 'fsdp'), scatter_...]
    pallas_call x0 -> x7, Pallas kernels: none -> 314 us  [the longest x3 191 us: head_sum(): pl.pallas_call(functools.partial(head_sum_kernel, n), out_shape=jax.Shape...]
    all_gather x5 -> x0, waiting for transfers between devices: 205 us -> none  [the longest x1 70 us: shards(): lax.all_gather(local_weights[5], 'fsdp', axis=0, tiled=True)]
    all_gather x6 -> x0, blocking collectives: 73.7 us -> none  [the longest x1 21.4 us: shards(): lax.all_gather(values_mine, ('ctx', 'fsdp'), axis=0, tiled=True)]
    ppermute x0 -> x42, waiting for transfers between devices: none -> 62.3 us  [flip(): return lax.ppermute(array, axis, [(i, i ^ bit) for i in range(size)])]
    ppermute x0 -> x42, starting transfers between devices: none -> 47.4 us  [flip(): return lax.ppermute(array, axis, [(i, i ^ bit) for i in range(size)])]
    dot_general x14 -> x8, matrix products: 51.5 us -> 18.5 us  [matmul(): return jnp.dot(left, right, preferred_element_type=F32)]
  transfers between devices with their start and end apart: 17 -> 42, of which waited for: 13 -> 6; matrix products, arithmetic and copies ran while one was open for 7% -> 29% of each run, Pallas kernels for 0% -> 51%
where the time goes in v1:
time: 626 us; the launch traced here: 622 us
  Pallas kernels  314 us (50%)
  other arithmetic  91.7 us (15%)
  matrix products  67.3 us (11%)
  waiting for transfers between devices  62.3 us (10%)
  starting transfers between devices  47.4 us (8%)
  local copies, waits for them, and re-layouts  36.8 us (6%)
    pallas_call x3, Pallas kernels, head_sum(): pl.pallas_call(functools.partial(head_sum_kernel, n), out_shape=jax.Shape...  191 us
    pallas_call x1, Pallas kernels, attend_back(): pl.pallas_call(functools.partial(backward_kernel, n_head, group, span), o...  69.8 us
    ppermute x42, waiting for transfers between devices, flip(): return lax.ppermute(array, axis, [(i, i ^ bit) for i in range(size)])  62.3 us
    ppermute x42, starting transfers between devices, flip(): return lax.ppermute(array, axis, [(i, i ^ bit) for i in range(size)])  47.4 us
    dot_general x5, matrix products, trans_mat(): lax.dot_general(left, right, (((0,), (0,)), ((), ())), preferred_element_...  25.1 us
    dot_general x10, matrix products, mat_trans(): lax.dot_general(left, right, (((1,), (1,)), ((), ())), preferred_element_...  23.7 us
    pallas_call x1, Pallas kernels, scatter_pairs(): pl.pallas_call(functools.partial(scatter_kernel, n_ctx), out_shape=jax.Sh...  22.4 us
    pallas_call x1, Pallas kernels, project(): pl.pallas_call(functools.partial(project_kernel, n_ctx), out_shape=(jax.S...  22.3 us
  transfers between devices with their start and end apart: 42, of which 6 were waited for; matrix products, arithmetic and copies ran while one was open for 29% of the time, Pallas kernels for 51%

profile of v1, /device:TPU:0, one launch (start us, length us, event | category | flops | bytes accessed | tf_op | source)
XLA Modules:
  0.0 622.0 jit_solution(11996608613881897333)
XLA Ops:
  2.8 3.0 collective-permute-start
  14.5 4.5 fusion.16
  21.3 2.2 maximum_select_fusion.2
  24.1 2.3 negate_select_fusion
  28.2 2.1 fusion.13.x_ref
  36.0 22.3 %project.1 = (bf16[512,512]{1,0:T(8,128)(2,1)}, bf16[4096,128]{1,0:T(8,128)(2,1)}) custom-call(bf16[512,2048]{1,0:T(8,128)(2,1)} %copy-done.12, bf16[1024,640]{1,0:T(8,128)(2,1)} %copy-done.16, bf16[1024,640]{1,0:T(8,128)(2,1)} %bitcast.99, f32[512,128]{1,0:T(8,128)} %get-tuple-element.155.cos_ref, f32[512,128]{1,0:T(8,128)} %get-tuple-element.154.sin_ref), custom_call_target="tpu_custom_call" | custom-call | tf_op jit(solution)/shard_map/project/pallas_call | solution.py:414
  61.3 2.0 constant_dynamic-slice_fusion
  64.2 8.8 %attend_forward.1 = (bf16[512,512]{1,0:T(8,128)(2,1)}, f32[8,1,512]{2,1,0:T(1,128)}) custom-call(s32[1]{0:T(128)} %bitcast.blk_ref, bf16[512,512]{1,0:T(8,128)(2,1)} %get-tuple-element.33.q_ref, bf16[4096,128]{1,0:T(8,128)(2,1)} %get-tuple-element.34.p_ref), custom_call_target="tpu_custom_call" | custom-call | flops 17179869184 | bytes 1048576 | tf_op jit(solution)/shard_map/attend_forward/pallas_call | solution.py:113
  73.0 2.6 constant_dynamic-slice_fusion.2
  75.6 4.7 collective-permute-start.5
  83.3 6.7 %collective-permute-start.4 = (bf16[1,256,1024]{2,1,0:T(8,128)(2,1)S(1)}, bf16[1,256,1024]{2,1,0:T(8,128)(2,1)S(1)}, u32[]{:S(2)}, u32[]{:S(2)}) collective-permute-start(bf16[1,256,1024]{2,1,0:T(8,128)(2,1)S(1)} %bitcast.109), channel_id=1, source_target_pairs={{0,8},{8,0},{16,24},{24,16},{1,9},{9,1},{17,25},{25,17},{2,10},{10... | collective-permute-start | bytes 1572872 | tf_op jit(solution)/shard_map/ppermute | solution.py:620
  92.6 3.4 fusion.61
  96.1 14.3 %collective-permute-start.10 = (bf16[1,256,1408]{2,1,0:T(8,128)(2,1)}, bf16[1,256,1408]{2,1,0:T(8,128)(2,1)}, u32[]{:S(2)}, u32[]{:S(2)}) collective-permute-start(bf16[1,256,1408]{2,1,0:T(8,128)(2,1)} %bitcast.17), channel_id=1, source_target_pairs={{0,16},{8,24},{16,0},{24,8},{1,17},{9,25},{17,1},{25,9},{2,18},{10... | collective-permute-start | bytes 2162696 | tf_op jit(solution)/shard_map/ppermute | solution.py:620
  113.3 64.7 %head_sum.3 = bf16[512,2048]{1,0:T(8,128)(2,1)} custom-call(bf16[512,1024]{1,0:T(8,128)(2,1)} %convolution_convert_fusion.8.left_ref, bf16[512,1024]{1,0:T(8,128)(2,1)} %convolution_convert_fusion.7.right_ref), custom_call_target="tpu_custom_call" | custom-call | flops 40000000000 | bytes 4194304 | tf_op jit(solution)/shard_map/head_sum/pallas_call | solution.py:605
  178.1 3.1 multiply_reduce_fusion
  200.1 4.1 multiply_convert_fusion.1
  206.3 3.2 fusion.99
  209.5 4.3 add_convert_fusion.8.left_ref
  214.2 2.8 convolution_convert_fusion.6.left_ref
  217.0 2.8 convolution_convert_fusion.5.right_ref
  219.8 2.8 add_convert_fusion.7.right_ref
  223.1 6.0 convolution_convert_fusion.2
  230.1 4.8 convolution_convert_fusion.1
  234.9 63.7 %head_sum.4 = bf16[512,2048]{1,0:T(8,128)(2,1)} custom-call(bf16[512,1024]{1,0:T(8,128)(2,1)} %add_convert_fusion.8.left_ref, bf16[512,1024]{1,0:T(8,128)(2,1)} %add_convert_fusion.7.right_ref), custom_call_target="tpu_custom_call" | custom-call | flops 40000000000 | bytes 4194304 | tf_op jit(solution)/shard_map/head_sum/pallas_call | solution.py:605
  298.7 3.9 fusion.12
  302.8 2.4 fusion.85
  314.3 6.8 %convolution_convert_fusion = bf16[1024,1408]{1,0:T(8,128)(2,1)} fusion(bf16[512,1408]{1,0:T(8,128)(2,1)} %collective-permute-done.16, bf16[512,1408]{1,0:T(8,128)(2,1)} %get-tuple-element.87, bf16[512,1024]{1,0:T(8,128)(2,1)S(1)} %copy-done.66, bf16[512,1024]{1,0:T(8,128)(2,1)S(1)} %copy-done.32), kind=kOutput, calls=%fused_computation.27 | convolution fusion | flops 2964193280 | bytes 7864320 | tf_op jit(solution)/shard_map/dot_general | solution.py:30
  323.4 3.3 fusion.42
  326.7 69.8 %attend_backward.1 = (f32[512,512]{1,0:T(8,128)}, f32[4096,128]{1,0:T(8,128)}, bf16[512,2048]{1,0:T(8,128)(2,1)}) custom-call(bf16[512,512]{1,0:T(8,128)(2,1)} %get-tuple-element.33.q_ref, bf16[512,512]{1,0:T(8,128)(2,1)} %fusion.50.g_ref, bf16[512,512]{1,0:T(8,128)(2,1)} %get-tuple-element.35.o_ref, f32[8,1,512]{2,1,0:T(1,128)} %get-tuple-element.44.lse_ref, ...), custom_call_target="tpu_custom_call" | custom-call | flops 34359738368 | bytes 2097152 | tf_op jit(solution)/shard_map/attend_backward/pallas_call | solution.py:243
  396.5 22.4 %scatter_pairs.1 = f32[512,128]{1,0:T(8,128)} custom-call(f32[4096,128]{1,0:T(8,128)} %get-tuple-element.47.part_ref), custom_call_target="tpu_custom_call" | custom-call | tf_op jit(solution)/shard_map/scatter_pairs/pallas_call | solution.py:364
  432.4 2.8 add_convert_fusion.6
  435.2 3.1 add_convert_fusion.2
  440.5 4.1 fusion.39
  444.6 62.7 %head_sum.5 = bf16[512,2048]{1,0:T(8,128)(2,1)} custom-call(bf16[512,1024]{1,0:T(8,128)(2,1)} %convolution_convert_fusion.4.left_ref, bf16[512,1024]{1,0:T(8,128)(2,1)} %convolution_convert_fusion.3.right_ref), custom_call_target="tpu_custom_call" | custom-call | flops 40000000000 | bytes 4194304 | tf_op jit(solution)/shard_map/head_sum/pallas_call | solution.py:605
  507.4 3.1 fusion.15
  510.5 5.7 fusion.8
  517.4 3.1 maximum_select_fusion
  524.8 2.2 maximum_select_fusion.3
  529.9 8.3 %collective-permute-done.21 = bf16[512,640]{1,0:T(8,128)(2,1)S(1)} collective-permute-done((bf16[512,640]{1,0:T(8,128)(2,1)S(1)}, bf16[512,640]{1,0:T(8,128)(2,1)S(1)}, u32[]{:S(2)}, u32[]{:S(2)}) %collective-permute-start.21) | collective-permute-done | bytes 655392 | tf_op jit(solution)/shard_map/ppermute | solution.py:620
  539.0 2.8 add_convert_fusion.4
  544.9 30.6 %collective-permute-done.22 = bf16[512,640]{1,0:T(8,128)(2,1)S(1)} collective-permute-done((bf16[512,640]{1,0:T(8,128)(2,1)S(1)}, bf16[512,640]{1,0:T(8,128)(2,1)S(1)}, u32[]{:S(2)}, u32[]{:S(2)}) %collective-permute-start.22) | collective-permute-done | bytes 655392 | tf_op jit(solution)/shard_map/ppermute | solution.py:620
  575.8 3.2 add_convert_fusion.5
  584.9 21.2 %collective-permute-done.31 = bf16[512,1408]{1,0:T(8,128)(2,1)} collective-permute-done((bf16[512,1408]{1,0:T(8,128)(2,1)}, bf16[512,1408]{1,0:T(8,128)(2,1)}, u32[]{:S(2)}, u32[]{:S(2)}) %collective-permute-start.31) | collective-permute-done | bytes 1441824 | tf_op jit(solution)/shard_map/ppermute | solution.py:620
  606.0 2.1 add_convert_fusion.3
  608.3 2.1 broadcast_select_fusion.5
  610.3 2.9 maximum_convert_fusion
  615.2 3.3 maximum_convert_fusion.2
  618.9 2.9 maximum_convert_fusion.1
  (311 shorter events, 103.8 us)
Async XLA Ops:
  0.6 79.6 %copy-start = (bf16[1024,1408]{1,0:T(8,128)(2,1)S(1)}, bf16[1024,1408]{1,0:T(8,128)(2,1)}, u32[]{:S(2)}) copy-start(bf16[1024,1408]{1,0:T(8,128)(2,1)} %param.17) | copy-start | bytes 8650756
  2.8 24.1 %collective-permute-start = (bf16[2,1024]{1,0:T(2,128)(2,1)}, bf16[2,1024]{1,0:T(2,128)(2,1)S(1)}, u32[]{:S(2)}, u32[]{:S(2)}) collective-permute-start(bf16[2,1024]{1,0:T(2,128)(2,1)} %pad_maximum_fusion.18), channel_id=1, source_target_pairs={{0,4},{4,0},{1,5},{5,1},{2,6},{6,2},{3,7},{7,3},{8,12},{12,8},{9,1... | collective-permute-start | bytes 12296 | tf_op jit(solution)/shard_map/ppermute | solution.py:620
  10.7 16.9 %collective-permute-start.1 = (bf16[512,640]{1,0:T(8,128)(2,1)S(1)}, bf16[512,640]{1,0:T(8,128)(2,1)}, u32[]{:S(2)}, u32[]{:S(2)}) collective-permute-start(bf16[512,640]{1,0:T(8,128)(2,1)S(1)} %constant_dynamic-slice_fusion.4), channel_id=1, source_target_pairs={{0,4},{4,0},{1,5},{5,1},{2,6},{6,2},{3,7},{7,3},{8,12},{12,8},{9,1... | collective-permute-start | bytes 1966088 | tf_op jit(solution)/shard_map/ppermute | solution.py:620
  27.6 5.9 collective-permute-start.2
  33.5 406.9 %collective-permute-start.19 = (bf16[512,1024]{1,0:T(8,128)(2,1)}, bf16[512,1024]{1,0:T(8,128)(2,1)}, u32[]{:S(2)}, u32[]{:S(2)}) collective-permute-start(bf16[512,1024]{1,0:T(8,128)(2,1)} %get-tuple-element.105), channel_id=1, source_target_pairs={{0,8},{8,0},{16,24},{24,16},{1,9},{9,1},{17,25},{25,17},{2,10},{10... | collective-permute-start | bytes 3145736 | tf_op jit(solution)/shard_map/ppermute | solution.py:620
  60.2 23.2 %collective-permute-start.3 = (bf16[256,1024]{1,0:T(8,128)(2,1)}, bf16[256,1024]{1,0:T(8,128)(2,1)S(1)}, u32[]{:S(2)}, u32[]{:S(2)}) collective-permute-start(bf16[256,1024]{1,0:T(8,128)(2,1)} %constant_dynamic-slice_fusion.3), channel_id=1, source_target_pairs={{0,4},{4,0},{1,5},{5,1},{2,6},{6,2},{3,7},{7,3},{8,12},{12,8},{9,1... | collective-permute-start | bytes 1572872 | tf_op jit(solution)/shard_map/ppermute | solution.py:620
  63.3 32.7 %collective-permute-start.9 = (bf16[256,1408]{1,0:T(8,128)(2,1)}, bf16[256,1408]{1,0:T(8,128)(2,1)}, u32[]{:S(2)}, u32[]{:S(2)}) collective-permute-start(bf16[256,1408]{1,0:T(8,128)(2,1)} %constant_dynamic-slice_fusion), channel_id=1, source_target_pairs={{0,4},{4,0},{1,5},{5,1},{2,6},{6,2},{3,7},{7,3},{8,12},{12,8},{9,1... | collective-permute-start | bytes 2162696 | tf_op jit(solution)/shard_map/ppermute | solution.py:620
  75.6 107.7 %collective-permute-start.5 = (bf16[704,1024]{1,0:T(8,128)(2,1)}, bf16[704,1024]{1,0:T(8,128)(2,1)}, u32[]{:S(2)}, u32[]{:S(2)}) collective-permute-start(bf16[704,1024]{1,0:T(8,128)(2,1)} %constant_dynamic-slice_fusion.2), channel_id=1, source_target_pairs={{0,4},{4,0},{1,5},{5,1},{2,6},{6,2},{3,7},{7,3},{8,12},{12,8},{9,1... | collective-permute-start | bytes 4325384 | tf_op jit(solution)/shard_map/ppermute | solution.py:620
  81.5 109.1 %collective-permute-start.7 = (bf16[512,1408]{1,0:T(8,128)(2,1)}, bf16[512,1408]{1,0:T(8,128)(2,1)}, u32[]{:S(2)}, u32[]{:S(2)}) collective-permute-start(bf16[512,1408]{1,0:T(8,128)(2,1)} %constant_dynamic-slice_fusion.1), channel_id=1, source_target_pairs={{0,4},{4,0},{1,5},{5,1},{2,6},{6,2},{3,7},{7,3},{8,12},{12,8},{9,1... | collective-permute-start | bytes 4325384 | tf_op jit(solution)/shard_map/ppermute | solution.py:620
  83.3 12.7 %collective-permute-start.4 = (bf16[1,256,1024]{2,1,0:T(8,128)(2,1)S(1)}, bf16[1,256,1024]{2,1,0:T(8,128)(2,1)S(1)}, u32[]{:S(2)}, u32[]{:S(2)}) collective-permute-start(bf16[1,256,1024]{2,1,0:T(8,128)(2,1)S(1)} %bitcast.109), channel_id=1, source_target_pairs={{0,8},{8,0},{16,24},{24,16},{1,9},{9,1},{17,25},{25,17},{2,10},{10... | collective-permute-start | bytes 1572872 | tf_op jit(solution)/shard_map/ppermute | solution.py:620
  96.0 126.5 %collective-permute-start.13 = (bf16[512,1024]{1,0:T(8,128)(2,1)}, bf16[512,1024]{1,0:T(8,128)(2,1)}, u32[]{:S(2)}, u32[]{:S(2)}) collective-permute-start(bf16[512,1024]{1,0:T(8,128)(2,1)} %get-tuple-element.125), channel_id=1, source_target_pairs={{0,8},{8,0},{16,24},{24,16},{1,9},{9,1},{17,25},{25,17},{2,10},{10... | collective-permute-start | bytes 3145736 | tf_op jit(solution)/shard_map/ppermute | solution.py:620
  96.1 87.3 %collective-permute-start.10 = (bf16[1,256,1408]{2,1,0:T(8,128)(2,1)}, bf16[1,256,1408]{2,1,0:T(8,128)(2,1)}, u32[]{:S(2)}, u32[]{:S(2)}) collective-permute-start(bf16[1,256,1408]{2,1,0:T(8,128)(2,1)} %bitcast.17), channel_id=1, source_target_pairs={{0,16},{8,24},{16,0},{24,8},{1,17},{9,25},{17,1},{25,9},{2,18},{10... | collective-permute-start | bytes 2162696 | tf_op jit(solution)/shard_map/ppermute | solution.py:620
  183.3 45.8 %copy-start.31 = (bf16[512,1024]{1,0:T(8,128)(2,1)}, bf16[512,1024]{1,0:T(8,128)(2,1)S(1)}, u32[]{:S(2)}) copy-start(bf16[512,1024]{1,0:T(8,128)(2,1)S(1)} %get-tuple-element.118) | copy-start | bytes 3145732
  183.3 7.5 %collective-permute-start.6 = (bf16[1,704,1024]{2,1,0:T(8,128)(2,1)}, bf16[1,704,1024]{2,1,0:T(8,128)(2,1)S(1)}, u32[]{:S(2)}, u32[]{:S(2)}) collective-permute-start(bf16[1,704,1024]{2,1,0:T(8,128)(2,1)} %bitcast.9), channel_id=1, source_target_pairs={{0,8},{8,0},{16,24},{24,16},{1,9},{9,1},{17,25},{25,17},{2,10},{10... | collective-permute-start | bytes 4325384 | tf_op jit(solution)/shard_map/ppermute | solution.py:620
  185.3 7.8 %collective-permute-start.11 = (bf16[2,256,1408]{2,1,0:T(8,128)(2,1)S(1)}, bf16[2,256,1408]{2,1,0:T(8,128)(2,1)S(1)}, u32[]{:S(2)}, u32[]{:S(2)}) collective-permute-start(bf16[2,256,1408]{2,1,0:T(8,128)(2,1)S(1)} %maximum_bitcast_fusion), channel_id=1, source_target_pairs={{0,8},{8,0},{16,24},{24,16},{1,9},{9,1},{17,25},{25,17},{2,10},{10... | collective-permute-start | bytes 4325384 | tf_op jit(solution)/shard_map/ppermute | solution.py:620
  190.6 38.5 %collective-permute-start.14 = (bf16[512,1024]{1,0:T(8,128)(2,1)S(1)}, bf16[512,1024]{1,0:T(8,128)(2,1)S(1)}, u32[]{:S(2)}, u32[]{:S(2)}) collective-permute-start(bf16[512,1024]{1,0:T(8,128)(2,1)S(1)} %get-tuple-element.119), channel_id=1, source_target_pairs={{0,8},{8,0},{16,24},{24,16},{1,9},{9,1},{17,25},{25,17},{2,10},{10... | collective-permute-start | bytes 3145736 | tf_op jit(solution)/shard_map/ppermute | solution.py:620
  190.8 7.3 %collective-permute-start.8 = (bf16[1,512,1408]{2,1,0:T(8,128)(2,1)}, bf16[1,512,1408]{2,1,0:T(8,128)(2,1)S(1)}, u32[]{:S(2)}, u32[]{:S(2)}) collective-permute-start(bf16[1,512,1408]{2,1,0:T(8,128)(2,1)} %bitcast.13), channel_id=1, source_target_pairs={{0,8},{8,0},{16,24},{24,16},{1,9},{9,1},{17,25},{25,17},{2,10},{10... | collective-permute-start | bytes 4325384 | tf_op jit(solution)/shard_map/ppermute | solution.py:620
  206.1 23.0 %collective-permute-start.15 = (bf16[512,1408]{1,0:T(8,128)(2,1)S(1)}, bf16[512,1408]{1,0:T(8,128)(2,1)S(1)}, u32[]{:S(2)}, u32[]{:S(2)}) collective-permute-start(bf16[512,1408]{1,0:T(8,128)(2,1)S(1)} %get-tuple-element.86), channel_id=1, source_target_pairs={{0,8},{8,0},{16,24},{24,16},{1,9},{9,1},{17,25},{25,17},{2,10},{10... | collective-permute-start | bytes 4325384 | tf_op jit(solution)/shard_map/ppermute | solution.py:620
  213.9 8.9 %collective-permute-start.12 = (bf16[512,1408]{1,0:T(8,128)(2,1)S(1)}, bf16[512,1408]{1,0:T(8,128)(2,1)S(1)}, u32[]{:S(2)}, u32[]{:S(2)}) collective-permute-start(bf16[512,1408]{1,0:T(8,128)(2,1)S(1)} %get-tuple-element.85), channel_id=1, source_target_pairs={{0,8},{8,0},{16,24},{24,16},{1,9},{9,1},{17,25},{25,17},{2,10},{10... | collective-permute-start | bytes 4325384 | tf_op jit(solution)/shard_map/ppermute | solution.py:620
  222.5 100.9 %collective-permute-start.17 = (bf16[512,512]{1,0:T(8,128)(2,1)S(1)}, bf16[512,512]{1,0:T(8,128)(2,1)}, u32[]{:S(2)}, u32[]{:S(2)}) collective-permute-start(bf16[512,512]{1,0:T(8,128)(2,1)S(1)} %copy-done.68), channel_id=1, source_target_pairs={{0,8},{8,0},{16,24},{24,16},{1,9},{9,1},{17,25},{25,17},{2,10},{10... | collective-permute-start | bytes 1572872 | tf_op jit(solution)/shard_map/ppermute | solution.py:620
  222.8 91.4 %collective-permute-start.16 = (bf16[512,1408]{1,0:T(8,128)(2,1)}, bf16[512,1408]{1,0:T(8,128)(2,1)}, u32[]{:S(2)}, u32[]{:S(2)}) collective-permute-start(bf16[512,1408]{1,0:T(8,128)(2,1)} %get-tuple-element.87), channel_id=1, source_target_pairs={{0,8},{8,0},{16,24},{24,16},{1,9},{9,1},{17,25},{25,17},{2,10},{10... | collective-permute-start | bytes 4325384 | tf_op jit(solution)/shard_map/ppermute | solution.py:620
  234.9 63.7 %copy-start.3 = (bf16[512,2048]{1,0:T(8,128)(2,1)S(1)}, bf16[512,2048]{1,0:T(8,128)(2,1)}, u32[]{:S(2)}) copy-start(bf16[512,2048]{1,0:T(8,128)(2,1)} %get-tuple-element.84) | copy-start | bytes 6291460
  305.2 3.7 collective-permute-start.39
  308.4 15.0 %collective-permute-start.18 = (bf16[512,1024]{1,0:T(8,128)(2,1)S(1)}, bf16[512,1024]{1,0:T(8,128)(2,1)S(1)}, u32[]{:S(2)}, u32[]{:S(2)}) collective-permute-start(bf16[512,1024]{1,0:T(8,128)(2,1)S(1)} %get-tuple-element.113), channel_id=1, source_target_pairs={{0,8},{8,0},{16,24},{24,16},{1,9},{9,1},{17,25},{25,17},{2,10},{10... | collective-permute-start | bytes 3145736 | tf_op jit(solution)/shard_map/ppermute | solution.py:620
  308.9 3.6 collective-permute-start.40
  312.5 118.0 %collective-permute-start.27 = (bf16[512,1408]{1,0:T(8,128)(2,1)}, bf16[512,1408]{1,0:T(8,128)(2,1)}, u32[]{:S(2)}, u32[]{:S(2)}) collective-permute-start(bf16[512,1408]{1,0:T(8,128)(2,1)} %slice.285), channel_id=1, source_target_pairs={{0,4},{4,0},{1,5},{5,1},{2,6},{6,2},{3,7},{7,3},{8,12},{12,8},{9,1... | collective-permute-start | bytes 4325384 | tf_op jit(solution)/shard_map/ppermute | solution.py:620
  314.2 8.2 %collective-permute-start.41 = (f32[8,128]{1,0:T(8,128)S(1)}, f32[8,128]{1,0:T(8,128)S(1)}, u32[]{:S(2)}, u32[]{:S(2)}) collective-permute-start(f32[8,128]{1,0:T(8,128)S(1)} %fusion.126), channel_id=1, source_target_pairs={{0,8},{8,0},{16,24},{24,16},{1,9},{9,1},{17,25},{25,17},{2,10},{10... | collective-permute-start | bytes 12296 | tf_op jit(solution)/shard_map/ppermute | solution.py:620
  322.4 112.8 %collective-permute-start.33 = (bf16[1408,512]{1,0:T(8,128)(2,1)}, bf16[1408,512]{1,0:T(8,128)(2,1)}, u32[]{:S(2)}, u32[]{:S(2)}) collective-permute-start(bf16[1408,512]{1,0:T(8,128)(2,1)} %slice.289), channel_id=1, source_target_pairs={{0,4},{4,0},{1,5},{5,1},{2,6},{6,2},{3,7},{7,3},{8,12},{12,8},{9,1... | collective-permute-start | bytes 4325384 | tf_op jit(solution)/shard_map/ppermute | solution.py:620
  424.9 15.6 %collective-permute-start.20 = (bf16[512,640]{1,0:T(8,128)(2,1)S(1)}, bf16[512,640]{1,0:T(8,128)(2,1)S(1)}, u32[]{:S(2)}, u32[]{:S(2)}) collective-permute-start(bf16[512,640]{1,0:T(8,128)(2,1)S(1)} %pad_maximum_fusion.17), channel_id=1, source_target_pairs={{0,8},{8,0},{16,24},{24,16},{1,9},{9,1},{17,25},{25,17},{2,10},{10... | collective-permute-start | bytes 1966088 | tf_op jit(solution)/shard_map/ppermute | solution.py:620
  425.0 14.9 %collective-permute-start.24 = (bf16[512,512]{1,0:T(8,128)(2,1)S(1)}, bf16[512,512]{1,0:T(8,128)(2,1)S(1)}, u32[]{:S(2)}, u32[]{:S(2)}) collective-permute-start(bf16[512,512]{1,0:T(8,128)(2,1)S(1)} %slice.283), channel_id=1, source_target_pairs={{0,4},{4,0},{1,5},{5,1},{2,6},{6,2},{3,7},{7,3},{8,12},{12,8},{9,1... | collective-permute-start | bytes 1572872 | tf_op jit(solution)/shard_map/ppermute | solution.py:620
  430.4 108.6 %collective-permute-start.30 = (bf16[512,1408]{1,0:T(8,128)(2,1)}, bf16[512,1408]{1,0:T(8,128)(2,1)}, u32[]{:S(2)}, u32[]{:S(2)}) collective-permute-start(bf16[512,1408]{1,0:T(8,128)(2,1)} %slice.287), channel_id=1, source_target_pairs={{0,4},{4,0},{1,5},{5,1},{2,6},{6,2},{3,7},{7,3},{8,12},{12,8},{9,1... | collective-permute-start | bytes 4325384 | tf_op jit(solution)/shard_map/ppermute | solution.py:620
  435.2 140.6 %collective-permute-start.28 = (bf16[512,1408]{1,0:T(8,128)(2,1)}, bf16[512,1408]{1,0:T(8,128)(2,1)}, u32[]{:S(2)}, u32[]{:S(2)}) collective-permute-start(bf16[512,1408]{1,0:T(8,128)(2,1)} %add_convert_fusion.6), channel_id=1, source_target_pairs={{0,16},{8,24},{16,0},{24,8},{1,17},{9,25},{17,1},{25,9},{2,18},{10... | collective-permute-start | bytes 4325384 | tf_op jit(solution)/shard_map/ppermute | solution.py:620
  440.1 88.4 %collective-permute-start.25 = (bf16[512,512]{1,0:T(8,128)(2,1)S(1)}, bf16[512,512]{1,0:T(8,128)(2,1)}, u32[]{:S(2)}, u32[]{:S(2)}) collective-permute-start(bf16[512,512]{1,0:T(8,128)(2,1)S(1)} %add_convert_fusion.12), channel_id=1, source_target_pairs={{0,16},{8,24},{16,0},{24,8},{1,17},{9,25},{17,1},{25,9},{2,18},{10... | collective-permute-start | bytes 1572872 | tf_op jit(solution)/shard_map/ppermute | solution.py:620
  444.6 62.7 %copy-start.43 = (f32[2048]{0:T(1024)S(1)}, f32[2048]{0:T(1024)}, u32[]{:S(2)}) copy-start(f32[2048]{0:T(1024)} %copy-done.42) | copy-start | bytes 24580
  444.6 62.8 %copy-start.45 = (f32[512]{0:T(512)S(1)}, f32[512]{0:T(512)}, u32[]{:S(2)}) copy-start(f32[512]{0:T(512)} %copy-done.44) | copy-start | bytes 6148
  516.8 3.7 collective-permute-start.36
  520.6 4.2 collective-permute-start.37
  523.4 14.8 %collective-permute-start.21 = (bf16[512,640]{1,0:T(8,128)(2,1)S(1)}, bf16[512,640]{1,0:T(8,128)(2,1)S(1)}, u32[]{:S(2)}, u32[]{:S(2)}) collective-permute-start(bf16[512,640]{1,0:T(8,128)(2,1)S(1)} %slice.278), channel_id=1, source_target_pairs={{0,4},{4,0},{1,5},{5,1},{2,6},{6,2},{3,7},{7,3},{8,12},{12,8},{9,1... | collective-permute-start | bytes 1966088 | tf_op jit(solution)/shard_map/ppermute | solution.py:620
  524.8 2.2 collective-permute-start.38
  526.9 12.1 %copy-start.22 = (bf16[1024,1408]{1,0:T(8,128)(2,1)S(1)}, bf16[1024,1408]{1,0:T(8,128)(2,1)}, u32[]{:S(2)}) copy-start(bf16[1024,1408]{1,0:T(8,128)(2,1)} %convolution_convert_fusion) | copy-start | bytes 8650756
  526.9 52.5 %collective-permute-start.34 = (bf16[1408,512]{1,0:T(8,128)(2,1)S(1)}, bf16[1408,512]{1,0:T(8,128)(2,1)S(1)}, u32[]{:S(2)}, u32[]{:S(2)}) collective-permute-start(bf16[1408,512]{1,0:T(8,128)(2,1)S(1)} %copy-done.18), channel_id=1, source_target_pairs={{0,16},{8,24},{16,0},{24,8},{1,17},{9,25},{17,1},{25,9},{2,18},{10... | collective-permute-start | bytes 4325384 | tf_op jit(solution)/shard_map/ppermute | solution.py:620
  529.6 13.7 %collective-permute-start.26 = (bf16[512,512]{1,0:T(8,128)(2,1)S(1)}, bf16[512,512]{1,0:T(8,128)(2,1)S(1)}, u32[]{:S(2)}, u32[]{:S(2)}) collective-permute-start(bf16[512,512]{1,0:T(8,128)(2,1)S(1)} %add_convert_fusion.11), channel_id=1, source_target_pairs={{0,8},{8,0},{16,24},{24,16},{1,9},{9,1},{17,25},{25,17},{2,10},{10... | collective-permute-start | bytes 1572872 | tf_op jit(solution)/shard_map/ppermute | solution.py:620
  538.4 37.1 %collective-permute-start.22 = (bf16[512,640]{1,0:T(8,128)(2,1)S(1)}, bf16[512,640]{1,0:T(8,128)(2,1)S(1)}, u32[]{:S(2)}, u32[]{:S(2)}) collective-permute-start(bf16[512,640]{1,0:T(8,128)(2,1)S(1)} %add_convert_fusion.10), channel_id=1, source_target_pairs={{0,16},{8,24},{16,0},{24,8},{1,17},{9,25},{17,1},{25,9},{2,18},{10... | collective-permute-start | bytes 1966088 | tf_op jit(solution)/shard_map/ppermute | solution.py:620
  541.9 64.2 %collective-permute-start.31 = (bf16[512,1408]{1,0:T(8,128)(2,1)}, bf16[512,1408]{1,0:T(8,128)(2,1)}, u32[]{:S(2)}, u32[]{:S(2)}) collective-permute-start(bf16[512,1408]{1,0:T(8,128)(2,1)} %add_convert_fusion.4), channel_id=1, source_target_pairs={{0,16},{8,24},{16,0},{24,8},{1,17},{9,25},{17,1},{25,9},{2,18},{10... | collective-permute-start | bytes 4325384 | tf_op jit(solution)/shard_map/ppermute | solution.py:620
  575.7 5.4 collective-permute-start.23
  579.0 29.3 %collective-permute-start.29 = (bf16[512,1408]{1,0:T(8,128)(2,1)}, bf16[512,1408]{1,0:T(8,128)(2,1)}, u32[]{:S(2)}, u32[]{:S(2)}) collective-permute-start(bf16[512,1408]{1,0:T(8,128)(2,1)} %add_convert_fusion.5), channel_id=1, source_target_pairs={{0,8},{8,0},{16,24},{24,16},{1,9},{9,1},{17,25},{25,17},{2,10},{10... | collective-permute-start | bytes 4325384 | tf_op jit(solution)/shard_map/ppermute | solution.py:620
  581.0 32.2 %collective-permute-start.35 = (bf16[1408,512]{1,0:T(8,128)(2,1)}, bf16[1408,512]{1,0:T(8,128)(2,1)}, u32[]{:S(2)}, u32[]{:S(2)}) collective-permute-start(bf16[1408,512]{1,0:T(8,128)(2,1)} %add_convert_fusion.1), channel_id=1, source_target_pairs={{0,8},{8,0},{16,24},{24,16},{1,9},{9,1},{17,25},{25,17},{2,10},{10... | collective-permute-start | bytes 4325384 | tf_op jit(solution)/shard_map/ppermute | solution.py:620
  608.2 10.4 %collective-permute-start.32 = (bf16[512,1408]{1,0:T(8,128)(2,1)S(1)}, bf16[512,1408]{1,0:T(8,128)(2,1)S(1)}, u32[]{:S(2)}, u32[]{:S(2)}) collective-permute-start(bf16[512,1408]{1,0:T(8,128)(2,1)S(1)} %add_convert_fusion.3), channel_id=1, source_target_pairs={{0,8},{8,0},{16,24},{24,16},{1,9},{9,1},{17,25},{25,17},{2,10},{10... | collective-permute-start | bytes 4325384 | tf_op jit(solution)/shard_map/ppermute | solution.py:620
  (64 other events, 170.2 us)

commit v2 on v1

--- a/solution.py
+++ b/solution.py
@@ -16,6 +16,7 @@
 MESH = pl.DeviceIdType.MESH
 CHUNKS = 16
 LAG = 3
+GROUPS = 4
 
 
 def matmul(left, right):
@@ -51,86 +52,213 @@
     return jnp.where(keep, wide, jnp.zeros_like(wide))
 
 
-def forward_kernel(group, span, blk_ref, q_ref, p_ref, o_ref, lse_ref, q_pad, ext, max_ref, acc_ref):
-    rows = q_ref.shape[0]
-    block = blk_ref[0]
-
-    @pl.when(pl.program_id(0) == 0)
-    def _():
-        ext[...] = jnp.where(lanes(p_ref.shape) < HEAD_DIM, jnp.ones_like(p_ref[...]), p_ref[...])
-
-    for h in range(group):
-        q_pad[h] = head_lanes(q_ref, h, False)
-    max_ref[...] = jnp.full_like(max_ref, NEG)
-    acc_ref[...] = jnp.zeros_like(acc_ref)
-
-    def head_tile(h, keys, values, start, masked):
-        scores = mat_trans(q_pad[h], keys)
-        if masked:
-            row = block * rows + lax.broadcasted_iota(jnp.int32, (rows, span), 0)
-            col = start + lax.broadcasted_iota(jnp.int32, (rows, span), 1)
-            scores = jnp.where(col <= row, scores, NEG)
-        old = max_ref[h]
-        new = jnp.maximum(old, jnp.max(scores, axis=1, keepdims=True))
-        weights = jnp.exp(scores - jnp.tile(new, (1, span // 128))).astype(BF)
-        acc_ref[h] = acc_ref[h] * jnp.exp(old - new) + matmul(weights, values)
-        max_ref[h] = new
-
-    def full(i, carry):
-        cut = pl.ds(pl.multiple_of(i * span, span), span)
-        for h in range(group):
-            head_tile(h, p_ref[cut, :], ext[cut, :], i * span, False)
+class Relay:
+    def __init__(self, n_ctx, src, dst, send, recv):
+        self.src, self.dst, self.send, self.recv = src, dst, send, recv
+        self.piece = src.shape[0] // n_ctx
+        self.ctx = lax.axis_index("ctx")
+        self.bits = high_bits(n_ctx)
+        self.count = 0
+        self.all = []
+        self.last = []
+
+    def _copy(self, src, dst, axis, bit):
+        e = self.count
+        self.count += 1
+        copy = pltpu.make_async_remote_copy(
+            src_ref=src,
+            dst_ref=dst,
+            send_sem=self.send.at[e],
+            recv_sem=self.recv.at[e],
+            device_id={axis: lax.axis_index(axis) ^ bit},
+            device_id_type=MESH,
+        )
+        copy.start()
+        self.all.append(copy)
+        return copy
+
+    def _cut(self, which):
+        return pl.ds(pl.multiple_of(which * self.piece, self.piece), self.piece)
+
+    def start(self):
+        mine = self._cut(self.ctx)
+        self.last = [self._copy(self.src.at[mine], self.dst.at[mine], "fsdp", 1)]
+
+    def hop(self, j):
+        self.landed()
+        bit = self.bits[j]
+        parts = [self.dst.at[self._cut(self.ctx ^ m)] for m in masks_of(self.bits[:j])]
+        self.last = [self._copy(part, part, "ctx", bit) for part in parts]
+
+    def landed(self):
+        for copy in self.last:
+            copy.wait_recv()
+        self.last = []
+
+    def drain(self):
+        for copy in self.all:
+            copy.wait_send()
+
+
+def forward_kernel(
+    n_ctx,
+    n_head,
+    span,
+    q_ref,
+    p_ref,
+    wl_ref,
+    wr_ref,
+    gate_ref,
+    up_ref,
+    down_ref,
+    o_ref,
+    lse_ref,
+    sum_ref,
+    gate_other,
+    up_other,
+    down_other,
+    q_pad,
+    ext,
+    max_ref,
+    acc_ref,
+    relay_send,
+    relay_recv,
+    left,
+    right,
+    from_lo,
+    from_hi,
+    *sems,
+):
+    rows, width = q_ref.shape
+    heads = width // HEAD_DIM
+    block = lax.axis_index("ctx") * 2 + lax.axis_index("fsdp")
+    barrier = line_greet(n_head)
+    greet(n_ctx)
+    ext[...] = jnp.where(lanes(p_ref.shape) < HEAD_DIM, jnp.ones_like(p_ref[...]), p_ref[...])
+    pl.semaphore_wait(barrier, line_peers(n_head) + len(partners(n_ctx)))
+    gate = Relay(n_ctx, gate_ref, gate_other, relay_send.at[0], relay_recv.at[0])
+    up = Relay(n_ctx, up_ref, up_other, relay_send.at[1], relay_recv.at[1])
+    down = Relay(n_ctx, down_ref, down_other, relay_send.at[2], relay_recv.at[2])
+    gate.start()
+    up.start()
+    down.hop(0)
+    step, steps, drain = line_sum(n_head, left, right, left, right, sum_ref, from_lo, from_hi, sems)
+    size = rows // GROUPS
+    stack = heads * size
+    sub = min(512, stack)
+    per_group = CHUNKS // GROUPS
+
+    def tile(start, first_row, masked):
+        cut = pl.ds(start, span)
+        for j in range(stack // sub):
+            part = pl.ds(j * sub, sub)
+            scores = mat_trans(q_pad[part, :], p_ref[cut, :])
+            if masked:
+                row = first_row + lax.rem(lax.broadcasted_iota(jnp.int32, (sub, span), 0), size)
+                col = start + lax.broadcasted_iota(jnp.int32, (sub, span), 1)
+                scores = jnp.where(col <= row, scores, NEG)
+            old = max_ref[part, :]
+            new = jnp.maximum(old, jnp.max(scores, axis=1, keepdims=True))
+            weights = jnp.exp(scores - jnp.tile(new, (1, span // 128))).astype(BF)
+            acc_ref[part, :] = acc_ref[part, :] * jnp.exp(old - new) + matmul(weights, ext[cut, :])
+            max_ref[part, :] = new
+
+    def run(s, carry):
+        step(s)
         return carry
 
-    lax.fori_loop(0, block * (rows // span), full, 0)
-
-    def last(t, carry):
-        h = lax.rem(t, group)
-        start = pl.multiple_of(block * rows + (t // group) * span, span)
-        cut = pl.ds(start, span)
-        head_tile(h, p_ref[cut, :], ext[cut, :], start, True)
+    def one_group(g, carry):
+        mine = pl.ds(pl.multiple_of(g * size, size), size)
+        first_row = block * rows + g * size
+        for h in range(heads):
+            q_pad[h * size : (h + 1) * size, :] = head_lanes(q_ref.at[mine], h, False)
+        max_ref[...] = jnp.full_like(max_ref, NEG)
+        acc_ref[...] = jnp.zeros_like(acc_ref)
+
+        tiles = (block + 1) * (rows // span)
+        base = (g - 1) * per_group
+
+        def sums(i):
+            lax.fori_loop((i * per_group) // tiles, ((i + 1) * per_group) // tiles, lambda j, c: run(base + j, c), 0)
+
+        def full(i, c):
+            sums(i)
+            tile(pl.multiple_of(i * span, span), first_row, False)
+            return c
+
+        lax.fori_loop(0, block * (rows // span), full, 0)
+        for j in range(rows // span):
+            sums(block * (rows // span) + j)
+            tile(pl.multiple_of(block * rows + j * span, span), first_row, True)
+        for h in range(heads):
+            acc = acc_ref[h * size : (h + 1) * size, :]
+            total = acc[:, :HEAD_DIM]
+            o_ref[mine, h * HEAD_DIM : (h + 1) * HEAD_DIM] = (acc[:, HEAD_DIM:] / total).astype(BF)
+            lse = max_ref[h * size : (h + 1) * size, :] + jnp.log(jnp.concatenate([total, total], axis=1))
+            lse_ref[h, :, mine] = lse.T[0:1, :]
+        att = o_ref[mine, :]
+        left[mine, :] = matmul(att, wl_ref[...]).astype(BF)
+        right[mine, :] = matmul(att, wr_ref[...]).astype(BF)
         return carry
 
-    lax.fori_loop(0, group * (rows // span), last, 0)
-    for h in range(group):
-        acc = acc_ref[h]
-        total = acc[:, :HEAD_DIM]
-        o_ref[:, h * HEAD_DIM : (h + 1) * HEAD_DIM] = (acc[:, HEAD_DIM:] / total).astype(BF)
-        lse = max_ref[h] + jnp.log(jnp.concatenate([total, total], axis=1))
-        lse_ref[h] = lse.T[0:1, :]
-
-
-def attend(queries, pair, block):
+    lax.fori_loop(0, GROUPS - 1, one_group, 0)
+    gate.hop(0)
+    down.hop(1)
+    lax.fori_loop(GROUPS - 1, GROUPS, one_group, 0)
+    hops = len(high_bits(n_ctx))
+    later = [(down, j) for j in range(2, hops)] + [(gate, 1), (up, 0)]
+    for j in range(1, hops):
+        later += [(up, j)] + ([(gate, j + 1)] if j + 1 < hops else [])
+    at = CHUNKS - per_group
+    rest = steps - at
+    for i, (relay, j) in enumerate(later):
+        to = CHUNKS - per_group + (rest * (2 * i + 1)) // (2 * len(later))
+        lax.fori_loop(at, to, run, 0)
+        at = to
+        relay.hop(j)
+    lax.fori_loop(at, steps, run, 0)
+    for relay in (gate, up, down):
+        relay.landed()
+        relay.drain()
+    drain()
+
+
+def attend_sum(queries, pair, out_left, out_right, gate, up, down, n_ctx, n_head, collective_id):
     rows, width = queries.shape
     heads = width // HEAD_DIM
     seq = pair.shape[0]
-    group = 4 if heads % 4 == 0 else 2
     span = min(512, rows)
-    wide = pl.BlockSpec((rows, group * HEAD_DIM), lambda i, *_: (0, i))
-    cost = pl.CostEstimate(
-        flops=16 * rows * seq * width, bytes_accessed=4 * rows * width, transcendentals=0
-    )
+    wide = 2 * out_left.shape[1]
+    vmem = pl.BlockSpec(memory_space=pltpu.VMEM)
+    anywhere = pl.BlockSpec(memory_space=pl.ANY)
+    stack = heads * rows // GROUPS
+    cost = pl.CostEstimate(flops=50_000_000_000, bytes_accessed=8 * rows * wide, transcendentals=0)
     return pl.pallas_call(
-        functools.partial(forward_kernel, group, span),
+        functools.partial(forward_kernel, n_ctx, n_head, span),
         out_shape=(
             jax.ShapeDtypeStruct((rows, width), BF),
             jax.ShapeDtypeStruct((heads, 1, rows), F32),
+            jax.ShapeDtypeStruct((rows, wide), BF),
+            jax.ShapeDtypeStruct(gate.shape, BF),
+            jax.ShapeDtypeStruct(up.shape, BF),
+            jax.ShapeDtypeStruct(down.shape, BF),
         ),
-        grid_spec=pltpu.PrefetchScalarGridSpec(
-            num_scalar_prefetch=1,
-            grid=(heads // group,),
-            in_specs=[wide, pl.BlockSpec((seq, 2 * HEAD_DIM), lambda i, *_: (0, 0))],
-            out_specs=[wide, pl.BlockSpec((group, 1, rows), lambda i, *_: (i, 0, 0))],
-            scratch_shapes=[
-                pltpu.VMEM((group, rows, 128), BF),
-                pltpu.VMEM((seq, 128), BF),
-                pltpu.VMEM((group, rows, 128), F32),
-                pltpu.VMEM((group, rows, 128), F32),
-            ],
-        ),
+        input_output_aliases={6: 5},
+        in_specs=[vmem] * 4 + [anywhere] * 3,
+        out_specs=(vmem, vmem, vmem, anywhere, anywhere, anywhere),
+        scratch_shapes=[
+            pltpu.VMEM((stack, 128), BF),
+            pltpu.VMEM((seq, 128), BF),
+            pltpu.VMEM((stack, 128), F32),
+            pltpu.VMEM((stack, 128), F32),
+            pltpu.SemaphoreType.DMA((3, n_ctx)),
+            pltpu.SemaphoreType.DMA((3, n_ctx)),
+        ]
+        + line_scratch(rows, wide),
+        compiler_params=pltpu.CompilerParams(collective_id=collective_id, has_side_effects=True),
         cost_estimate=cost,
-        name="attend_forward",
-    )(block, queries, pair)
+        name="attend_sum",
+    )(queries, pair, out_left, out_right, gate, up, down)
 
 
 def backward_kernel(
@@ -151,7 +279,8 @@
     g_pad,
     acc_ref,
     dl_ref,
-    work,
+    work_l,
+    work_r,
     from_lo,
     from_hi,
     *sems,
@@ -161,7 +290,6 @@
     tiles = rows // span
     block = lax.axis_index("ctx") * 2 + lax.axis_index("fsdp")
     barrier = line_greet(n_head)
-    stage(work, left_ref, right_ref)
     dp_ref[...] = jnp.zeros_like(dp_ref)
     acc_ref[...] = jnp.zeros_like(acc_ref)
     for h in range(heads):
@@ -170,8 +298,10 @@
         g_pad[h] = head_lanes(g_ref, h, True)
         product = g_ref[:, cut].astype(F32) * o_ref[:, cut].astype(F32)
         dl_ref[h] = jnp.sum(product.T, axis=0, keepdims=True)
-    line_meet(n_head, barrier)
-    step, steps, drain = line_sum(n_head, CHUNKS, LAG, work, sum_ref, from_lo, from_hi, sems)
+    pl.semaphore_wait(barrier, line_peers(n_head))
+    step, steps, drain = line_sum(
+        n_head, left_ref, right_ref, work_l, work_r, sum_ref, from_lo, from_hi, sems
+    )
 
     def head_tile(h, pairs, start, masked):
         probs = jnp.exp(mat_trans(pairs, q_pad[h]) - lse_ref[h])
@@ -302,15 +432,20 @@
         copies.append(copy)
         return copy
 
-    part((ctx * 2 + x) * rows, rows, "fsdp", 1).wait_recv()
-    done = []
-    for bit in high_bits(n_ctx):
-        now = [part((ctx ^ m) * 2 * rows, 2 * rows, "ctx", bit) for m in masks_of(done)]
-        for copy in now:
-            copy.wait_recv()
-        done.append(bit)
-    for copy in copies:
-        copy.wait_send()
+    opening = part((ctx * 2 + x) * rows, rows, "fsdp", 1)
+
+    def finish():
+        opening.wait_recv()
+        done = []
+        for bit in high_bits(n_ctx):
+            now = [part((ctx ^ m) * 2 * rows, 2 * rows, "ctx", bit) for m in masks_of(done)]
+            for copy in now:
+                copy.wait_recv()
+            done.append(bit)
+        for copy in copies:
+            copy.wait_send()
+
+    return finish
 
 
 def scatter_kernel(n_ctx, part_ref, o_ref, work, land, send, recv):
@@ -377,71 +512,174 @@
     )(part)
 
 
-def project_kernel(n_ctx, x_ref, wl_ref, wr_ref, cos_ref, sin_ref, q_ref, p_ref, send, recv):
+def project_kernel(
+    n_ctx,
+    x_ref,
+    w_ref,
+    gain_ref,
+    cos_ref,
+    sin_ref,
+    wo_ref,
+    down_ref,
+    q_ref,
+    p_ref,
+    n_ref,
+    w_other,
+    gain_other,
+    wo_other,
+    down_other,
+    acc_ref,
+    send,
+    recv,
+    relay_send,
+    relay_recv,
+    gain_send,
+    gain_recv,
+):
     rows, width = x_ref.shape
     half = width // 2
     q_width = q_ref.shape[1]
-    block = lax.axis_index("ctx") * 2 + lax.axis_index("fsdp")
+    x_at = lax.axis_index("fsdp")
+    block = lax.axis_index("ctx") * 2 + x_at
     barrier = greet(n_ctx)
-    size = rows // 4
+    pl.semaphore_wait(barrier, len(partners(n_ctx)))
+    gains = pltpu.make_async_remote_copy(
+        src_ref=gain_ref,
+        dst_ref=gain_other,
+        send_sem=gain_send,
+        recv_sem=gain_recv,
+        device_id={"fsdp": 1 - x_at},
+        device_id_type=MESH,
+    )
+    gains.start()
+    part = half // 2
+    first = [
+        Relay(
+            n_ctx,
+            w_ref.at[pl.ds(i * part, part)],
+            w_other.at[pl.ds(i * part, part)],
+            relay_send.at[i],
+            relay_recv.at[i],
+        )
+        for i in range(2)
+    ]
+    second = Relay(n_ctx, wo_ref, wo_other, relay_send.at[2], relay_recv.at[2])
+    third = Relay(n_ctx, down_ref, down_other, relay_send.at[3], relay_recv.at[3])
+    for relay in first:
+        relay.start()
+    second.start()
+    gains.wait_recv()
+    parts = 8
+    size = rows // parts
+    own = pl.ds(pl.multiple_of(x_at * half, half), half)
+    other = pl.ds(pl.multiple_of((1 - x_at) * half, half), half)
+
+    def cut_of(i):
+        return pl.ds(pl.multiple_of(i * size, size), size)
+
+    def norm(i, carry):
+        cut = cut_of(i)
+        left = x_ref[cut, own].astype(F32)
+        right = x_ref[cut, other].astype(F32)
+        total = jnp.sum(left * left, axis=1, keepdims=True) + jnp.sum(right * right, axis=1, keepdims=True)
+        scale = lax.rsqrt(total / width + EPSILON)
+        n_ref[cut, :half] = (left * scale * gain_ref[0:1, :]).astype(BF)
+        n_ref[cut, half:] = (right * scale * gain_other[0:1, :]).astype(BF)
+        return carry
+
+    lax.fori_loop(0, parts, norm, 0)
+    for relay in first:
+        relay.hop(0)
+    third.start()
+    second.hop(0)
+
+    def local(i, carry):
+        cut = cut_of(i)
+        acc_ref[cut, :] = matmul(n_ref[cut, :half], w_ref[...])
+        return carry
+
+    lax.fori_loop(0, parts, local, 0)
+    for j in range(1, len(high_bits(n_ctx))):
+        for relay in first:
+            relay.hop(j)
+    for relay in first:
+        relay.landed()
 
     def rotated(wide, cut):
         low = lax.rem(lanes(wide.shape), HEAD_DIM) < HEAD_DIM // 2
         turned = jnp.where(low, pltpu.roll(wide, 128 - HEAD_DIM // 2, 1), pltpu.roll(wide, HEAD_DIM // 2, 1))
         return wide * cos_ref[cut, :] + turned * sin_ref[cut, :]
 
-    def part(i, carry):
-        cut = pl.ds(pl.multiple_of(i * size, size), size)
-        left = x_ref[cut, :half]
-        right = x_ref[cut, half:]
-        both = matmul(left, wl_ref[:, q_width:]) + matmul(right, wr_ref[:, q_width:])
+    def pairs(i, carry):
+        cut = cut_of(i)
+        both = acc_ref[cut, q_width:] + matmul(n_ref[cut, half:], w_other[:, q_width:])
         pair = jnp.where(lanes(both.shape) < HEAD_DIM, rotated(both, cut), both)
         p_ref[pl.ds(pl.multiple_of(block * rows + i * size, size), size), :] = pair.astype(BF)
+        return carry
+
+    def queries(i, carry):
+        cut = cut_of(i)
+        whole = acc_ref[cut, :q_width] + matmul(n_ref[cut, half:], w_other[:, :q_width])
         for j in range(q_width // 128):
             sl = slice(j * 128, (j + 1) * 128)
-            wide = matmul(left, wl_ref[:, sl]) + matmul(right, wr_ref[:, sl])
-            q_ref[cut, sl] = (rotated(wide, cut) * 0.125).astype(BF)
+            q_ref[cut, sl] = (rotated(whole[:, sl], cut) * 0.125).astype(BF)
         return carry
 
-    lax.fori_loop(0, 4, part, 0)
-    pl.semaphore_wait(barrier, len(partners(n_ctx)))
-    gather_pairs(n_ctx, rows, p_ref, send, recv)
-
-
-def project(normed, w_left, w_right, cosine, sine, q_width, n_ctx, collective_id):
-    rows = normed.shape[0]
+    lax.fori_loop(0, parts, pairs, 0)
+    finish = gather_pairs(n_ctx, rows, p_ref, send, recv)
+    lax.fori_loop(0, parts, queries, 0)
+    finish()
+    for j in range(1, len(high_bits(n_ctx))):
+        second.hop(j)
+    second.landed()
+    third.landed()
+    for relay in first + [second, third]:
+        relay.drain()
+    gains.wait_send()
+
+
+def project(inputs, w_local, gains, cosine, sine, w_out, w_down, q_width, n_ctx, collective_id):
+    rows, width = inputs.shape
     vmem = pl.BlockSpec(memory_space=pltpu.VMEM)
+    anywhere = pl.BlockSpec(memory_space=pl.ANY)
     return pl.pallas_call(
         functools.partial(project_kernel, n_ctx),
         out_shape=(
             jax.ShapeDtypeStruct((rows, q_width), BF),
             jax.ShapeDtypeStruct((rows * 2 * n_ctx, 2 * HEAD_DIM), BF),
+            jax.ShapeDtypeStruct((rows, width), BF),
+            jax.ShapeDtypeStruct(w_local.shape, BF),
+            jax.ShapeDtypeStruct(gains.shape, F32),
+            jax.ShapeDtypeStruct(w_out.shape, BF),
+            jax.ShapeDtypeStruct(w_down.shape, BF),
         ),
-        in_specs=[vmem] * 5,
-        out_specs=(vmem, vmem),
+        in_specs=[vmem] * 5 + [anywhere] * 2,
+        out_specs=(vmem,) * 5 + (anywhere,) * 2,
         scratch_shapes=[
+            pltpu.VMEM((rows, w_local.shape[1]), F32),
             pltpu.SemaphoreType.DMA((n_ctx,)),
             pltpu.SemaphoreType.DMA((n_ctx,)),
+            pltpu.SemaphoreType.DMA((4, n_ctx)),
+            pltpu.SemaphoreType.DMA((4, n_ctx)),
+            pltpu.SemaphoreType.DMA,
+            pltpu.SemaphoreType.DMA,
         ],
         compiler_params=pltpu.CompilerParams(collective_id=collective_id, has_side_effects=True),
         name="project",
-    )(normed, w_left, w_right, cosine, sine)
-
-
-def line_sum(n, chunks, lag, work, o_ref, from_lo, from_hi, sems):
+    )(inputs, w_local, gains, cosine, sine, w_out, w_down)
+
+
+def line_sum(n, left, right, work_l, work_r, o_ref, from_lo, from_hi, sems):
     s_up, r_up, s_dn, r_dn, s_a, r_a, s_b, r_b = sems
     me = lax.axis_index("head")
-    half = work.shape[0] // 2
-    size = half // chunks
+    rows, cols = left.shape
+    size = rows // CHUNKS
     has_lo = me > 0
     has_hi = me < n - 1
     middle = jnp.logical_and(has_lo, has_hi)
 
-    def lo(k):
+    def at(k):
         return pl.ds(pl.multiple_of(k * size, size), size)
-
-    def hi(k):
-        return pl.ds(pl.multiple_of(half + k * size, size), size)
 
     def remote(src, dst, send, recv, target):
         return pltpu.make_async_remote_copy(
@@ -453,60 +691,62 @@
             device_id_type=MESH,
         )
 
-    def up(k):
-        return remote(work.at[hi(k)], from_lo.at[lo(k)], s_up.at[k], r_up.at[k], me + 1)
-
-    def down(k):
-        return remote(work.at[lo(k)], from_hi.at[lo(k)], s_dn.at[k], r_dn.at[k], me - 1)
+    def up(k, src):
+        return remote(src.at[at(k)], from_lo.at[at(k)], s_up.at[k], r_up.at[k], me + 1)
+
+    def down(k, src):
+        return remote(src.at[at(k)], from_hi.at[at(k)], s_dn.at[k], r_dn.at[k], me - 1)
 
     def spread_a(k):
-        return remote(o_ref.at[lo(k)], o_ref.at[lo(k)], s_a.at[k], r_a.at[k], me + 1)
+        part = o_ref.at[at(k), pl.ds(0, cols)]
+        return remote(part, part, s_a.at[k], r_a.at[k], me + 1)
 
     def spread_b(k):
-        return remote(o_ref.at[hi(k)], o_ref.at[hi(k)], s_b.at[k], r_b.at[k], me - 1)
+        part = o_ref.at[at(k), pl.ds(cols, cols)]
+        return remote(part, part, s_b.at[k], r_b.at[k], me - 1)
 
     def valid(k):
-        return jnp.logical_and(k >= 0, k < chunks)
-
-    def added(here, there, k):
-        return (work[here(k), :].astype(F32) + there[lo(k), :].astype(F32)).astype(BF)
+        return jnp.logical_and(k >= 0, k < CHUNKS)
+
+    def added(mine, there, k):
+        return (mine[at(k), :].astype(F32) + there[at(k), :].astype(F32)).astype(BF)
 
     def step(s):
-        k1 = s - lag * me
-        k2 = s - lag * (n - 1 - me)
-        k3 = s - lag * (n - 1 + me)
-        k4 = s - lag * (2 * (n - 1) - me)
+        k1 = s - LAG * me
+        k2 = s - LAG * (n - 1 - me)
+        k3 = s - LAG * (n - 1 + me)
+        k4 = s - LAG * (2 * (n - 1) - me)
 
         @pl.when(jnp.logical_and(valid(k1), me == 0))
         def _():
-            up(k1).start()
+            up(k1, right).start()
+
+        @pl.when(jnp.logical_and(valid(k2), me == n - 1))
+        def _():
+            down(k2, left).start()
 
         @pl.when(jnp.logical_and(valid(k1), middle))
         def _():
-            up(k1).wait_recv()
-            work[hi(k1), :] = added(hi, from_lo, k1)
-            up(k1).start()
+            up(k1, right).wait_recv()
+            work_r[at(k1), :] = added(right, from_lo, k1)
+            up(k1, work_r).start()
 
         @pl.when(jnp.logical_and(valid(k1), me == n - 1))
         def _():
-            up(k1).wait_recv()
-            o_ref[hi(k1), :] = added(hi, from_lo, k1)
+            up(k1, right).wait_recv()
+            o_ref[at(k1), cols:] = added(right, from_lo, k1)
             spread_b(k1).start()
-
-        @pl.when(jnp.logical_and(valid(k2), me == n - 1))
-        def _():
-            down(k2).start()
 
         @pl.when(jnp.logical_and(valid(k2), middle))
         def _():
-            down(k2).wait_recv()
-            work[lo(k2), :] = added(lo, from_hi, k2)
-            down(k2).start()
+            down(k2, left).wait_recv()
+            work_l[at(k2), :] = added(left, from_hi, k2)
+            down(k2, work_l).start()
 
         @pl.when(jnp.logical_and(valid(k2), me == 0))
         def _():
-            down(k2).wait_recv()
-            o_ref[lo(k2), :] = added(lo, from_hi, k2)
+            down(k2, left).wait_recv()
+            o_ref[at(k2), :cols] = added(left, from_hi, k2)
             spread_a(k2).start()
 
         @pl.when(jnp.logical_and(valid(k3), has_lo))
@@ -529,19 +769,19 @@
         def one(k, carry):
             @pl.when(has_hi)
             def _():
-                up(k).wait_send()
+                up(k, right).wait_send()
                 spread_a(k).wait_send()
 
             @pl.when(has_lo)
             def _():
-                down(k).wait_send()
+                down(k, left).wait_send()
                 spread_b(k).wait_send()
 
             return carry
 
-        lax.fori_loop(0, chunks, one, 0)
-
-    return step, chunks + 2 * lag * (n - 1), drain
+        lax.fori_loop(0, CHUNKS, one, 0)
+
+    return step, CHUNKS + 2 * LAG * (n - 1), drain
 
 
 def line_greet(n):
@@ -559,38 +799,19 @@
     return barrier
 
 
-def line_meet(n, barrier):
+def line_peers(n):
     me = lax.axis_index("head")
-    peers = jnp.where(me > 0, 1, 0) + jnp.where(me < n - 1, 1, 0)
-    pl.semaphore_wait(barrier, peers)
-
-
-def stage(work, left_ref, right_ref):
-    rows, cols = left_ref.shape
-    size = rows // 16
-
-    def one(k, carry):
-        cut = pl.ds(pl.multiple_of(k * size, size), size)
-        work[cut, :cols] = left_ref[cut, :]
-        work[cut, cols:] = right_ref[cut, :]
-        return carry
-
-    lax.fori_loop(0, 16, one, 0)
+    return jnp.where(me > 0, 1, 0) + jnp.where(me < n - 1, 1, 0)
 
 
 def line_scratch(rows, width):
-    return [
-        pltpu.VMEM((rows, width), BF),
-        pltpu.VMEM((rows // 2, width), BF),
-        pltpu.VMEM((rows // 2, width), BF),
-    ] + [pltpu.SemaphoreType.DMA((CHUNKS,))] * 8
-
-
-def head_sum_kernel(n, left_ref, right_ref, o_ref, work, from_lo, from_hi, *sems):
+    return [pltpu.VMEM((rows, width // 2), BF)] * 4 + [pltpu.SemaphoreType.DMA((CHUNKS,))] * 8
+
+
+def head_sum_kernel(n, left_ref, right_ref, o_ref, work_l, work_r, from_lo, from_hi, *sems):
     barrier = line_greet(n)
-    stage(work, left_ref, right_ref)
-    line_meet(n, barrier)
-    step, steps, drain = line_sum(n, CHUNKS, LAG, work, o_ref, from_lo, from_hi, sems)
+    pl.semaphore_wait(barrier, line_peers(n))
+    step, steps, drain = line_sum(n, left_ref, right_ref, work_l, work_r, o_ref, from_lo, from_hi, sems)
 
     def run(s, carry):
         step(s)
@@ -618,10 +839,6 @@
 
 def flip(array, axis, bit, size):
     return lax.ppermute(array, axis, [(i, i ^ bit) for i in range(size)])
-
-
-def after(value, *others):
-    return lax.optimization_barrier((value,) + others)[0]
 
 
 def shards(
@@ -652,30 +869,7 @@
         swapped = jnp.concatenate([array[:, half:], array[:, :half]], axis=1)
         return jnp.where(x_at == 0, array, swapped)
 
-    def fetch(shard, bits):
-        count = 2 ** len(bits)
-        piece = shard.shape[0] // count
-        at = ctx_at if len(bits) > 1 else core
-        mine = lax.dynamic_slice_in_dim(shard, at * piece, piece, 0)
-        return flip(mine, "fsdp", 1, 2)
-
-    def share(mine, bits):
-        buf = mine[None]
-        for bit in bits:
-            got = flip(buf, "ctx", bit, n_ctx)
-            upper = (ctx_at & bit) != 0
-            pair = jnp.stack([jnp.where(upper, got, buf), jnp.where(upper, buf, got)], axis=1)
-            buf = pair.reshape((-1,) + mine.shape)
-        return buf.reshape((-1,) + mine.shape[1:])
-
     every = high_bits(n_ctx)
-    chip = [1]
-    qkv_local = jnp.concatenate([query_weight, key_weight, value_weight], axis=1)
-    gains_local = jnp.stack([attn_gain, ffn_gain])
-    gains_other = flip(gains_local, "fsdp", 1, 2)
-    qkv_other = share(fetch(qkv_local, chip), chip)
-    gain_one = jnp.concatenate([gains_local[0], gains_other[0]]).astype(F32)
-    gain_two = jnp.concatenate([gains_local[1], gains_other[1]]).astype(F32)
 
     def columns_of(array, which):
         first = jnp.concatenate([array[:, :quarter], array[:, half : half + quarter]], axis=1)
@@ -689,36 +883,34 @@
         got = flip(columns_of(array, 1 - core), "ctx", 1, n_ctx)
         return jnp.concatenate([columns_of(array, core), got], axis=0)
 
-    in_float = own_first(inputs).astype(F32)
-    cot = own_first(cotangent)
-    scale_one = lax.rsqrt(jnp.mean(in_float * in_float, axis=-1, keepdims=True) + EPSILON)
-    unit_one = in_float * scale_one
-    normed_one = (unit_one * gain_one).astype(BF)
     q_width = query_weight.shape[1]
+    half_dim = HEAD_DIM // 2
     positions = block * rows + jnp.arange(rows, dtype=jnp.int32)
-    half_dim = HEAD_DIM // 2
     lane = lax.broadcasted_iota(jnp.int32, (rows, 2 * HEAD_DIM), 1)
     freqs = 10000.0 ** (-2.0 * (lane % half_dim).astype(F32) / HEAD_DIM)
     angles = positions.astype(F32)[:, None] * freqs
     cosine = jnp.cos(angles)
     sine = jnp.sin(angles)
     signed = jnp.where(lane % HEAD_DIM < half_dim, -sine, sine)
-    queries, pair = project(normed_one, qkv_local, qkv_other, cosine, signed, q_width, n_ctx, 4)
-    out_piece = fetch(after(output_weight, pair), chip)
-    gate_piece = fetch(after(gate_weight, pair), every)
-    attended, lse = attend(queries, pair, block_arr)
-    up_piece = fetch(after(up_weight, attended), chip)
-    down_piece = fetch(after(down_weight, attended), chip)
-    out_other = share(out_piece, chip)
-    gate_other = share(gate_piece, every)
-    up_other = share(up_piece, chip)
-    down_other = share(down_piece, chip)
-    cot = after(cot, attended)
+    qkv_local = jnp.concatenate([query_weight, key_weight, value_weight], axis=1)
+    gains_local = jnp.concatenate([attn_gain[None], ffn_gain[None], jnp.zeros((6, half), BF)]).astype(F32)
+    queries, pair, normed_one, qkv_other, gains_other, out_other, down_begun = project(
+        inputs, qkv_local, gains_local, cosine, signed, output_weight, down_weight, q_width, n_ctx, 4
+    )
+    attended, lse, mixed, gate_other, up_other, down_other = attend_sum(
+        queries, pair, output_weight, out_other, gate_weight, up_weight, down_begun, n_ctx, n_head, 1
+    )
+    gain_one = jnp.concatenate([gains_local[0], gains_other[0]])
+    gain_two = jnp.concatenate([gains_local[1], gains_other[1]])
+    late_inputs, late_cot, normed_one, mixed = lax.optimization_barrier(
+        (inputs, cotangent, normed_one, mixed)
+    )
+    in_float = own_first(late_inputs).astype(F32)
+    cot = own_first(late_cot)
+    scale_one = lax.rsqrt(jnp.mean(in_float * in_float, axis=-1, keepdims=True) + EPSILON)
+    unit_one = in_float * scale_one
     one_pair = trade_columns(normed_one)
 
-    mixed_left = matmul(attended, output_weight).astype(BF)
-    mixed_right = matmul(attended, out_other).astype(BF)
-    mixed = head_sum(mixed_left, mixed_right, n_head, 1)
     hidden = in_float + mixed.astype(F32)
     scale_two = lax.rsqrt(jnp.mean(hidden * hidden, axis=-1, keepdims=True) + EPSILON)
     unit_two = hidden * scale_two

time: 626 us -> 603 us (0.963)
  Pallas kernels: 314 us -> 347 us
  starting transfers between devices: 47.4 us -> 14.7 us
  other arithmetic: 91.7 us -> 69.9 us
    pallas_call x1, Pallas kernels: 8.78 us -> 77.6 us  [attend_sum(): pl.pallas_call(functools.partial(forward_kernel, n_ctx, n_head, span), ou...]
    pallas_call x3 -> x2, Pallas kernels: 191 us -> 127 us  [head_sum(): pl.pallas_call(functools.partial(head_sum_kernel, n), out_shape=jax.Shape...]
    ppermute x42 -> x30, starting transfers between devices: 47.4 us -> 14.7 us  [flip(): return lax.ppermute(array, axis, [(i, i ^ bit) for i in range(size)])]
    pallas_call x1, Pallas kernels: 22.3 us -> 51.8 us  [project(): pl.pallas_call(functools.partial(project_kernel, n_ctx), out_shape=(jax.S...]
    another operation x14 -> x2, other arithmetic: 11.5 us -> 1.9 us  [the longest x11 8.96 us: share(): jnp.stack([jnp.where(upper, got, buf), jnp.where(upper, buf, got)], axis=1)]
    dynamic_slice x5 -> x0, local copies, waits for them, and re-layouts: 7.72 us -> none  [fetch(): mine = lax.dynamic_slice_in_dim(shard, at * piece, piece, 0)]
    ppermute x42 -> x30, waiting for transfers between devices: 62.3 us -> 65.1 us  [flip(): return lax.ppermute(array, axis, [(i, i ^ bit) for i in range(size)])]
    unnamed x144 -> x136, local copies, waits for them, and re-layouts: 14.5 us -> 15.3 us
  transfers between devices with their start and end apart: 42 -> 30, of which waited for: 6 -> 6; matrix products, arithmetic and copies ran while one was open for 29% -> 21% of each run, Pallas kernels for 51% -> 36%
where the time goes in v2:
time: 603 us; the launch traced here: 596 us
  Pallas kernels  347 us (58%)
  other arithmetic  69.9 us (12%)
  matrix products  66.5 us (11%)
  waiting for transfers between devices  65.1 us (11%)
  local copies, waits for them, and re-layouts  31 us (5%)
  starting transfers between devices  14.7 us (2%)
    pallas_call x2, Pallas kernels, head_sum(): pl.pallas_call(functools.partial(head_sum_kernel, n), out_shape=jax.Shape...  127 us
    pallas_call x1, Pallas kernels, attend_sum(): pl.pallas_call(functools.partial(forward_kernel, n_ctx, n_head, span), ou...  77.6 us
    pallas_call x1, Pallas kernels, attend_back(): pl.pallas_call(functools.partial(backward_kernel, n_head, group, span), o...  68.8 us
    ppermute x30, waiting for transfers between devices, flip(): return lax.ppermute(array, axis, [(i, i ^ bit) for i in range(size)])  65.1 us
    pallas_call x1, Pallas kernels, project(): pl.pallas_call(functools.partial(project_kernel, n_ctx), out_shape=(jax.S...  51.8 us
    dot_general x5, matrix products, trans_mat(): lax.dot_general(left, right, (((0,), (0,)), ((), ())), preferred_element_...  26 us
    dot_general x10, matrix products, mat_trans(): lax.dot_general(left, right, (((1,), (1,)), ((), ())), preferred_element_...  22.1 us
    pallas_call x1, Pallas kernels, scatter_pairs(): pl.pallas_call(functools.partial(scatter_kernel, n_ctx), out_shape=jax.Sh...  21.5 us
  transfers between devices with their start and end apart: 30, of which 6 were waited for; matrix products, arithmetic and copies ran while one was open for 21% of the time, Pallas kernels for 36%

profile of v2, /device:TPU:0, one launch (start us, length us, event | category | flops | bytes accessed | tf_op | source)
XLA Modules:
  0.0 596.2 jit_solution(12979756858080252885)
XLA Ops:
  4.5 2.5 pad_maximum_fusion.3.w_ref
  7.0 1.8 negate_select_fusion
  8.8 51.8 %project.1 = (bf16[512,512]{1,0:T(8,128)(2,1)}, bf16[4096,128]{1,0:T(8,128)(2,1)}, bf16[512,2048]{1,0:T(8,128)(2,1)}, bf16[1024,640]{1,0:T(8,128)(2,1)}, f32[8,1...) custom-call(bf16[512,2048]{1,0:T(8,128)(2,1)} %x_ref.1, ...), custom_call_target="tpu_custom_call" | custom-call | tf_op jit(solution)/shard_map/project/pallas_call | solution.py:645
  60.6 77.6 %attend_sum.1 = (bf16[512,512]{1,0:T(8,128)(2,1)}, f32[8,1,512]{2,1,0:T(1,128)}, bf16[512,2048]{1,0:T(8,128)(2,1)}, bf16[1024,1408]{1,0:T(8,128)(2,1)}, bf16[102...) custom-call(bf16[512,512]{1,0:T(8,128)(2,1)} %get-tuple-element.42.q_ref, ...), custom_call_target="tpu_custom_call", output_to_operand_aliasing={{5}: (6, {})} | custom-call | flops 49999998976 | bytes 8388608 | tf_op jit(solution)/shard_map/attend_sum/pallas_call | solution.py:236
  140.2 3.9 multiply_reduce_fusion
  148.6 1.8 fusion.65
  152.4 1.8 fusion.53
  155.0 1.8 convolution_add_fusion
  156.9 1.9 convolution_add_fusion.2
  158.8 4.5 multiply_convert_fusion.1
  163.3 2.6 fusion.89
  170.3 1.8 fusion.98
  172.2 1.8 fusion.99
  174.0 4.3 convolution_convert_fusion.6.left_ref
  178.3 4.3 add_convert_fusion.8.left_ref
  184.5 4.2 convolution_convert_fusion.5.right_ref
  189.3 1.9 broadcast_select_fusion.10
  191.9 4.2 add_convert_fusion.7.right_ref
  196.6 6.3 %convolution_convert_fusion.2 = bf16[1408,1024]{1,0:T(8,128)(2,1)} fusion(bf16[512,1408]{1,0:T(8,128)(2,1)} %collective-permute-done, bf16[512,1408]{1,0:T(8,128)(2,1)} %get-tuple-element.89, bf16[512,1024]{1,0:T(8,128)(2,1)S(1)} %collective-permute-done.1, bf16[512,1024]{1,0:T(8,128)(2,1)S(1)} %get-tuple-element.122), kind=kOutput, calls=%fused_computation.27 | convolution fusion | flops 2964193280 | bytes 7864320 | tf_op jit(solution)/shard_map/dot_general | solution.py:31
  203.9 5.3 convolution_convert_fusion.1
  209.1 64.8 %head_sum.2 = bf16[512,2048]{1,0:T(8,128)(2,1)} custom-call(bf16[512,1024]{1,0:T(8,128)(2,1)} %add_convert_fusion.8.left_ref, bf16[512,1024]{1,0:T(8,128)(2,1)} %add_convert_fusion.7.right_ref), custom_call_target="tpu_custom_call" | custom-call | flops 40000000000 | bytes 4194304 | tf_op jit(solution)/shard_map/head_sum/pallas_call | solution.py:826
  274.0 4.3 fusion.11
  278.4 2.4 fusion.83
  289.8 6.8 %convolution_convert_fusion = bf16[1024,1408]{1,0:T(8,128)(2,1)} fusion(bf16[512,1408]{1,0:T(8,128)(2,1)} %collective-permute-done.4, bf16[512,1408]{1,0:T(8,128)(2,1)} %get-tuple-element.91, bf16[512,1024]{1,0:T(8,128)(2,1)S(1)} %copy-done.61, bf16[512,1024]{1,0:T(8,128)(2,1)S(1)} %get-tuple-element.116), kind=kOutput, calls=%fused_computation.25 | convolution fusion | flops 2964193280 | bytes 7864320 | tf_op jit(solution)/shard_map/dot_general | solution.py:31
  299.6 3.5 fusion.40
  303.1 68.8 %attend_backward.1 = (f32[512,512]{1,0:T(8,128)}, f32[4096,128]{1,0:T(8,128)}, bf16[512,2048]{1,0:T(8,128)(2,1)}) custom-call(bf16[512,512]{1,0:T(8,128)(2,1)} %get-tuple-element.42.q_ref, bf16[512,512]{1,0:T(8,128)(2,1)} %fusion.48.g_ref, bf16[512,512]{1,0:T(8,128)(2,1)} %get-tuple-element.56.o_ref, f32[8,1,512]{2,1,0:T(1,128)} %get-tuple-element.58.lse_ref, ...), custom_call_target="tpu_custom_call" | custom-call | flops 34359738368 | bytes 2097152 | tf_op jit(solution)/shard_map/attend_backward/pallas_call | solution.py:373
  372.0 21.5 %scatter_pairs.1 = f32[512,128]{1,0:T(8,128)} custom-call(f32[4096,128]{1,0:T(8,128)} %get-tuple-element.61.part_ref), custom_call_target="tpu_custom_call" | custom-call | tf_op jit(solution)/shard_map/scatter_pairs/pallas_call | solution.py:499
  400.8 2.0 convolution_convert_fusion.4.left_ref
  402.8 2.0 convolution_convert_fusion.3.right_ref
  404.8 1.9 collective-permute-start.18
  408.6 3.1 add_convert_fusion.2
  411.7 2.6 collective-permute-done.12
  415.3 4.1 fusion.37
  419.4 62.4 %head_sum.3 = bf16[512,2048]{1,0:T(8,128)(2,1)} custom-call(bf16[512,1024]{1,0:T(8,128)(2,1)} %convolution_convert_fusion.4.left_ref, bf16[512,1024]{1,0:T(8,128)(2,1)} %convolution_convert_fusion.3.right_ref), custom_call_target="tpu_custom_call" | custom-call | flops 40000000000 | bytes 4194304 | tf_op jit(solution)/shard_map/head_sum/pallas_call | solution.py:826
  481.9 3.1 fusion.13
  485.0 5.8 fusion.7
  492.2 3.1 maximum_select_fusion
  499.9 2.2 maximum_select_fusion.3
  505.2 8.2 %collective-permute-done.9 = bf16[512,640]{1,0:T(8,128)(2,1)S(1)} collective-permute-done((bf16[512,640]{1,0:T(8,128)(2,1)S(1)}, bf16[512,640]{1,0:T(8,128)(2,1)S(1)}, u32[]{:S(2)}, u32[]{:S(2)}) %collective-permute-start.9) | collective-permute-done | bytes 655392 | tf_op jit(solution)/shard_map/ppermute | solution.py:841
  515.6 1.8 collective-permute-start.19
  519.0 31.6 %collective-permute-done.10 = bf16[512,640]{1,0:T(8,128)(2,1)S(1)} collective-permute-done((bf16[512,640]{1,0:T(8,128)(2,1)S(1)}, bf16[512,640]{1,0:T(8,128)(2,1)S(1)}, u32[]{:S(2)}, u32[]{:S(2)}) %collective-permute-start.10) | collective-permute-done | bytes 655392 | tf_op jit(solution)/shard_map/ppermute | solution.py:841
  550.9 2.8 add_convert_fusion.5
  557.5 1.9 copy.25
  560.3 20.9 %collective-permute-done.19 = bf16[512,1408]{1,0:T(8,128)(2,1)} collective-permute-done((bf16[512,1408]{1,0:T(8,128)(2,1)S(1)}, bf16[512,1408]{1,0:T(8,128)(2,1)}, u32[]{:S(2)}, u32[]{:S(2)}) %collective-permute-start.19) | collective-permute-done | bytes 1441824 | tf_op jit(solution)/shard_map/ppermute | solution.py:841
  582.9 2.1 broadcast_select_fusion.5
  585.0 2.9 maximum_convert_fusion
  589.5 3.3 maximum_convert_fusion.2
  593.1 2.9 maximum_convert_fusion.1
  (261 shorter events, 65.3 us)
Async XLA Ops:
  0.7 8.1 %copy-start.39 = (s32[128]{0:T(128)}, s32[128]{0:T(128)S(1)}, u32[]{:S(2)}) copy-start(s32[128]{0:T(128)S(1)} %get-tuple-element.154) | copy-start | bytes 1540
  0.7 8.1 %copy-start.41 = (s32[128]{0:T(128)}, s32[128]{0:T(128)S(1)}, u32[]{:S(2)}) copy-start(s32[128]{0:T(128)S(1)} %get-tuple-element.155) | copy-start | bytes 1540
  0.7 8.1 %copy-start.43 = (s32[128]{0:T(128)}, s32[128]{0:T(128)S(1)}, u32[]{:S(2)}) copy-start(s32[128]{0:T(128)S(1)} %get-tuple-element.156) | copy-start | bytes 1540
  0.7 8.1 %copy-start.45 = (s32[128]{0:T(128)}, s32[128]{0:T(128)S(1)}, u32[]{:S(2)}) copy-start(s32[128]{0:T(128)S(1)} %get-tuple-element.157) | copy-start | bytes 1540
  0.7 8.1 %copy-start.47 = (pred[128]{0:T(512)(128)(4,1)}, pred[128]{0:T(512)(128)(4,1)S(1)}, u32[]{:S(2)}) copy-start(pred[128]{0:T(512)(128)(4,1)S(1)} %get-tuple-element.152) | copy-start | bytes 388
  0.7 8.1 %copy-start.49 = (pred[128]{0:T(512)(128)(4,1)}, pred[128]{0:T(512)(128)(4,1)S(1)}, u32[]{:S(2)}) copy-start(pred[128]{0:T(512)(128)(4,1)S(1)} %get-tuple-element.153) | copy-start | bytes 388
  60.6 77.6 %copy-start.7 = (bf16[512,2048]{1,0:T(8,128)(2,1)S(1)}, bf16[512,2048]{1,0:T(8,128)(2,1)}, u32[]{:S(2)}) copy-start(bf16[512,2048]{1,0:T(8,128)(2,1)} %x_ref.1) | copy-start | bytes 6291460
  144.2 134.2 %copy-start.32 = (f32[512]{0:T(512)}, f32[512]{0:T(512)S(1)}, u32[]{:S(2)}) copy-start(f32[512]{0:T(512)S(1)} %add_rsqrt_fusion.1) | copy-start | bytes 6148
  146.0 12.7 %copy-start.10 = (bf16[512,2048]{1,0:T(8,128)(2,1)}, bf16[512,2048]{1,0:T(8,128)(2,1)S(1)}, u32[]{:S(2)}) copy-start(bf16[512,2048]{1,0:T(8,128)(2,1)S(1)} %multiply_convert_fusion) | copy-start | bytes 6291460
  152.4 4.4 copy-start.3
  163.2 33.2 %collective-permute-start = (bf16[512,1408]{1,0:T(8,128)(2,1)}, bf16[512,1408]{1,0:T(8,128)(2,1)}, u32[]{:S(2)}, u32[]{:S(2)}) collective-permute-start(bf16[512,1408]{1,0:T(8,128)(2,1)} %get-tuple-element.89), channel_id=1, source_target_pairs={{0,8},{8,0},{16,24},{24,16},{1,9},{9,1},{17,25},{25,17},{2,10},{10... | collective-permute-start | bytes 4325384 | tf_op jit(solution)/shard_map/ppermute | solution.py:841
  167.7 28.3 %collective-permute-start.1 = (bf16[512,1024]{1,0:T(8,128)(2,1)S(1)}, bf16[512,1024]{1,0:T(8,128)(2,1)S(1)}, u32[]{:S(2)}, u32[]{:S(2)}) collective-permute-start(bf16[512,1024]{1,0:T(8,128)(2,1)S(1)} %get-tuple-element.123), channel_id=1, source_target_pairs={{0,8},{8,0},{16,24},{24,16},{1,9},{9,1},{17,25},{25,17},{2,10},{10... | collective-permute-start | bytes 3145736 | tf_op jit(solution)/shard_map/ppermute | solution.py:841
  168.2 34.7 %collective-permute-start.3 = (bf16[512,1408]{1,0:T(8,128)(2,1)S(1)}, bf16[512,1408]{1,0:T(8,128)(2,1)S(1)}, u32[]{:S(2)}, u32[]{:S(2)}) collective-permute-start(bf16[512,1408]{1,0:T(8,128)(2,1)S(1)} %copy-done.57), channel_id=1, source_target_pairs={{0,8},{8,0},{16,24},{24,16},{1,9},{9,1},{17,25},{25,17},{2,10},{10... | collective-permute-start | bytes 4325384 | tf_op jit(solution)/shard_map/ppermute | solution.py:841
  168.9 34.0 %collective-permute-start.2 = (bf16[512,1024]{1,0:T(8,128)(2,1)S(1)}, bf16[512,1024]{1,0:T(8,128)(2,1)S(1)}, u32[]{:S(2)}, u32[]{:S(2)}) collective-permute-start(bf16[512,1024]{1,0:T(8,128)(2,1)S(1)} %get-tuple-element.117), channel_id=1, source_target_pairs={{0,8},{8,0},{16,24},{24,16},{1,9},{9,1},{17,25},{25,17},{2,10},{10... | collective-permute-start | bytes 3145736 | tf_op jit(solution)/shard_map/ppermute | solution.py:841
  169.4 120.3 %collective-permute-start.4 = (bf16[512,1408]{1,0:T(8,128)(2,1)}, bf16[512,1408]{1,0:T(8,128)(2,1)}, u32[]{:S(2)}, u32[]{:S(2)}) collective-permute-start(bf16[512,1408]{1,0:T(8,128)(2,1)} %get-tuple-element.91), channel_id=1, source_target_pairs={{0,8},{8,0},{16,24},{24,16},{1,9},{9,1},{17,25},{25,17},{2,10},{10... | collective-permute-start | bytes 4325384 | tf_op jit(solution)/shard_map/ppermute | solution.py:841
  196.0 103.6 %collective-permute-start.5 = (bf16[512,512]{1,0:T(8,128)(2,1)}, bf16[512,512]{1,0:T(8,128)(2,1)}, u32[]{:S(2)}, u32[]{:S(2)}) collective-permute-start(bf16[512,512]{1,0:T(8,128)(2,1)} %get-tuple-element.56.o_ref), channel_id=1, source_target_pairs={{0,8},{8,0},{16,24},{24,16},{1,9},{9,1},{17,25},{25,17},{2,10},{10... | collective-permute-start | bytes 1572872 | tf_op jit(solution)/shard_map/ppermute | solution.py:841
  196.5 218.8 %collective-permute-start.7 = (bf16[512,1024]{1,0:T(8,128)(2,1)}, bf16[512,1024]{1,0:T(8,128)(2,1)}, u32[]{:S(2)}, u32[]{:S(2)}) collective-permute-start(bf16[512,1024]{1,0:T(8,128)(2,1)} %get-tuple-element.103), channel_id=1, source_target_pairs={{0,8},{8,0},{16,24},{24,16},{1,9},{9,1},{17,25},{25,17},{2,10},{10... | collective-permute-start | bytes 3145736 | tf_op jit(solution)/shard_map/ppermute | solution.py:841
  273.9 4.4 copy-start.1
  274.0 4.4 copy-start.4
  281.6 3.7 collective-permute-start.27
  284.8 4.9 copy-start.61
  284.8 14.8 %collective-permute-start.6 = (bf16[512,1024]{1,0:T(8,128)(2,1)S(1)}, bf16[512,1024]{1,0:T(8,128)(2,1)S(1)}, u32[]{:S(2)}, u32[]{:S(2)}) collective-permute-start(bf16[512,1024]{1,0:T(8,128)(2,1)S(1)} %get-tuple-element.111), channel_id=1, source_target_pairs={{0,8},{8,0},{16,24},{24,16},{1,9},{9,1},{17,25},{25,17},{2,10},{10... | collective-permute-start | bytes 3145736 | tf_op jit(solution)/shard_map/ppermute | solution.py:841
  285.2 3.6 collective-permute-start.28
  288.9 116.0 %collective-permute-start.15 = (bf16[512,1408]{1,0:T(8,128)(2,1)}, bf16[512,1408]{1,0:T(8,128)(2,1)}, u32[]{:S(2)}, u32[]{:S(2)}) collective-permute-start(bf16[512,1408]{1,0:T(8,128)(2,1)} %slice.293), channel_id=1, source_target_pairs={{0,4},{4,0},{1,5},{5,1},{2,6},{6,2},{3,7},{7,3},{8,12},{12,8},{9,1... | collective-permute-start | bytes 4325384 | tf_op jit(solution)/shard_map/ppermute | solution.py:841
  289.7 6.9 %copy-start.17 = (bf16[1408,1024]{1,0:T(8,128)(2,1)S(1)}, bf16[1408,1024]{1,0:T(8,128)(2,1)}, u32[]{:S(2)}) copy-start(bf16[1408,1024]{1,0:T(8,128)(2,1)} %convolution_convert_fusion.2) | copy-start | bytes 8650756
  289.7 8.1 %collective-permute-start.29 = (f32[8,128]{1,0:T(8,128)S(1)}, f32[8,128]{1,0:T(8,128)S(1)}, u32[]{:S(2)}, u32[]{:S(2)}) collective-permute-start(f32[8,128]{1,0:T(8,128)S(1)} %fusion.122), channel_id=1, source_target_pairs={{0,8},{8,0},{16,24},{24,16},{1,9},{9,1},{17,25},{25,17},{2,10},{10... | collective-permute-start | bytes 12296 | tf_op jit(solution)/shard_map/ppermute | solution.py:841
  297.8 110.7 %collective-permute-start.21 = (bf16[1408,512]{1,0:T(8,128)(2,1)}, bf16[1408,512]{1,0:T(8,128)(2,1)}, u32[]{:S(2)}, u32[]{:S(2)}) collective-permute-start(bf16[1408,512]{1,0:T(8,128)(2,1)} %slice.297), channel_id=1, source_target_pairs={{0,4},{4,0},{1,5},{5,1},{2,6},{6,2},{3,7},{7,3},{8,12},{12,8},{9,1... | collective-permute-start | bytes 4325384 | tf_op jit(solution)/shard_map/ppermute | solution.py:841
  371.9 23.9 %copy-start.14 = (f32[512,512]{1,0:T(8,128)S(1)}, f32[512,512]{1,0:T(8,128)}, u32[]{:S(2)}) copy-start(f32[512,512]{1,0:T(8,128)} %get-tuple-element.60) | copy-start | bytes 3145732
  399.3 16.0 %collective-permute-start.8 = (bf16[512,640]{1,0:T(8,128)(2,1)S(1)}, bf16[512,640]{1,0:T(8,128)(2,1)S(1)}, u32[]{:S(2)}, u32[]{:S(2)}) collective-permute-start(bf16[512,640]{1,0:T(8,128)(2,1)S(1)} %pad_maximum_fusion.12), channel_id=1, source_target_pairs={{0,8},{8,0},{16,24},{24,16},{1,9},{9,1},{17,25},{25,17},{2,10},{10... | collective-permute-start | bytes 1966088 | tf_op jit(solution)/shard_map/ppermute | solution.py:841
  399.4 14.9 %collective-permute-start.12 = (bf16[512,512]{1,0:T(8,128)(2,1)S(1)}, bf16[512,512]{1,0:T(8,128)(2,1)S(1)}, u32[]{:S(2)}, u32[]{:S(2)}) collective-permute-start(bf16[512,512]{1,0:T(8,128)(2,1)S(1)} %slice.291), channel_id=1, source_target_pairs={{0,4},{4,0},{1,5},{5,1},{2,6},{6,2},{3,7},{7,3},{8,12},{12,8},{9,1... | collective-permute-start | bytes 1572872 | tf_op jit(solution)/shard_map/ppermute | solution.py:841
  404.8 109.0 %collective-permute-start.18 = (bf16[512,1408]{1,0:T(8,128)(2,1)}, bf16[512,1408]{1,0:T(8,128)(2,1)}, u32[]{:S(2)}, u32[]{:S(2)}) collective-permute-start(bf16[512,1408]{1,0:T(8,128)(2,1)} %slice.295), channel_id=1, source_target_pairs={{0,4},{4,0},{1,5},{5,1},{2,6},{6,2},{3,7},{7,3},{8,12},{12,8},{9,1... | collective-permute-start | bytes 4325384 | tf_op jit(solution)/shard_map/ppermute | solution.py:841
  408.5 6.8 %copy-start.28 = (bf16[512,1024]{1,0:T(8,128)(2,1)S(1)}, bf16[512,1024]{1,0:T(8,128)(2,1)}, u32[]{:S(2)}) copy-start(bf16[512,1024]{1,0:T(8,128)(2,1)} %get-tuple-element.102) | copy-start | bytes 3145732
  408.5 142.4 %collective-permute-start.16 = (bf16[512,1408]{1,0:T(8,128)(2,1)S(1)}, bf16[512,1408]{1,0:T(8,128)(2,1)}, u32[]{:S(2)}, u32[]{:S(2)}) collective-permute-start(bf16[512,1408]{1,0:T(8,128)(2,1)S(1)} %add_convert_fusion.6), channel_id=1, source_target_pairs={{0,16},{8,24},{16,0},{24,8},{1,17},{9,25},{17,1},{25,9},{2,18},{10... | collective-permute-start | bytes 4325384 | tf_op jit(solution)/shard_map/ppermute | solution.py:841
  415.3 88.3 %collective-permute-start.13 = (bf16[512,512]{1,0:T(8,128)(2,1)}, bf16[512,512]{1,0:T(8,128)(2,1)}, u32[]{:S(2)}, u32[]{:S(2)}) collective-permute-start(bf16[512,512]{1,0:T(8,128)(2,1)} %add_convert_fusion.12), channel_id=1, source_target_pairs={{0,16},{8,24},{16,0},{24,8},{1,17},{9,25},{17,1},{25,9},{2,18},{10... | collective-permute-start | bytes 1572872 | tf_op jit(solution)/shard_map/ppermute | solution.py:841
  419.4 62.4 %copy-start.31 = (f32[2048]{0:T(1024)S(1)}, f32[2048]{0:T(1024)}, u32[]{:S(2)}) copy-start(f32[2048]{0:T(1024)} %pad_maximum_fusion.14) | copy-start | bytes 24580
  491.4 3.9 collective-permute-start.24
  495.3 4.6 collective-permute-start.25
  498.5 14.8 %collective-permute-start.9 = (bf16[512,640]{1,0:T(8,128)(2,1)S(1)}, bf16[512,640]{1,0:T(8,128)(2,1)S(1)}, u32[]{:S(2)}, u32[]{:S(2)}) collective-permute-start(bf16[512,640]{1,0:T(8,128)(2,1)S(1)} %slice.286), channel_id=1, source_target_pairs={{0,4},{4,0},{1,5},{5,1},{2,6},{6,2},{3,7},{7,3},{8,12},{12,8},{9,1... | collective-permute-start | bytes 1966088 | tf_op jit(solution)/shard_map/ppermute | solution.py:841
  499.9 2.2 collective-permute-start.26
  502.1 11.8 %copy-start.16 = (bf16[1024,1408]{1,0:T(8,128)(2,1)S(1)}, bf16[1024,1408]{1,0:T(8,128)(2,1)}, u32[]{:S(2)}) copy-start(bf16[1024,1408]{1,0:T(8,128)(2,1)} %convolution_convert_fusion) | copy-start | bytes 8650756
  502.1 52.1 %collective-permute-start.22 = (bf16[1408,512]{1,0:T(8,128)(2,1)S(1)}, bf16[1408,512]{1,0:T(8,128)(2,1)S(1)}, u32[]{:S(2)}, u32[]{:S(2)}) collective-permute-start(bf16[1408,512]{1,0:T(8,128)(2,1)S(1)} %copy-done.12), channel_id=1, source_target_pairs={{0,16},{8,24},{16,0},{24,8},{1,17},{9,25},{17,1},{25,9},{2,18},{10... | collective-permute-start | bytes 4325384 | tf_op jit(solution)/shard_map/ppermute | solution.py:841
  504.9 12.5 %collective-permute-start.14 = (bf16[512,512]{1,0:T(8,128)(2,1)S(1)}, bf16[512,512]{1,0:T(8,128)(2,1)S(1)}, u32[]{:S(2)}, u32[]{:S(2)}) collective-permute-start(bf16[512,512]{1,0:T(8,128)(2,1)S(1)} %add_convert_fusion.11), channel_id=1, source_target_pairs={{0,8},{8,0},{16,24},{24,16},{1,9},{9,1},{17,25},{25,17},{2,10},{10... | collective-permute-start | bytes 1572872 | tf_op jit(solution)/shard_map/ppermute | solution.py:841
  513.5 37.1 %collective-permute-start.10 = (bf16[512,640]{1,0:T(8,128)(2,1)S(1)}, bf16[512,640]{1,0:T(8,128)(2,1)S(1)}, u32[]{:S(2)}, u32[]{:S(2)}) collective-permute-start(bf16[512,640]{1,0:T(8,128)(2,1)S(1)} %add_convert_fusion.10), channel_id=1, source_target_pairs={{0,16},{8,24},{16,0},{24,8},{1,17},{9,25},{17,1},{25,9},{2,18},{10... | collective-permute-start | bytes 1966088 | tf_op jit(solution)/shard_map/ppermute | solution.py:841
  515.6 65.6 %collective-permute-start.19 = (bf16[512,1408]{1,0:T(8,128)(2,1)S(1)}, bf16[512,1408]{1,0:T(8,128)(2,1)}, u32[]{:S(2)}, u32[]{:S(2)}) collective-permute-start(bf16[512,1408]{1,0:T(8,128)(2,1)S(1)} %add_convert_fusion.4), channel_id=1, source_target_pairs={{0,16},{8,24},{16,0},{24,8},{1,17},{9,25},{17,1},{25,9},{2,18},{10... | collective-permute-start | bytes 4325384 | tf_op jit(solution)/shard_map/ppermute | solution.py:841
  550.8 3.9 collective-permute-start.11
  553.7 29.3 %collective-permute-start.17 = (bf16[512,1408]{1,0:T(8,128)(2,1)}, bf16[512,1408]{1,0:T(8,128)(2,1)}, u32[]{:S(2)}, u32[]{:S(2)}) collective-permute-start(bf16[512,1408]{1,0:T(8,128)(2,1)} %add_convert_fusion.5), channel_id=1, source_target_pairs={{0,8},{8,0},{16,24},{24,16},{1,9},{9,1},{17,25},{25,17},{2,10},{10... | collective-permute-start | bytes 4325384 | tf_op jit(solution)/shard_map/ppermute | solution.py:841
  554.6 33.3 %collective-permute-start.23 = (bf16[1408,512]{1,0:T(8,128)(2,1)S(1)}, bf16[1408,512]{1,0:T(8,128)(2,1)}, u32[]{:S(2)}, u32[]{:S(2)}) collective-permute-start(bf16[1408,512]{1,0:T(8,128)(2,1)S(1)} %add_convert_fusion.1), channel_id=1, source_target_pairs={{0,8},{8,0},{16,24},{24,16},{1,9},{9,1},{17,25},{25,17},{2,10},{10... | collective-permute-start | bytes 4325384 | tf_op jit(solution)/shard_map/ppermute | solution.py:841
  582.9 9.9 %collective-permute-start.20 = (bf16[512,1408]{1,0:T(8,128)(2,1)S(1)}, bf16[512,1408]{1,0:T(8,128)(2,1)S(1)}, u32[]{:S(2)}, u32[]{:S(2)}) collective-permute-start(bf16[512,1408]{1,0:T(8,128)(2,1)S(1)} %add_convert_fusion.3), channel_id=1, source_target_pairs={{0,8},{8,0},{16,24},{24,16},{1,9},{9,1},{17,25},{25,17},{2,10},{10... | collective-permute-start | bytes 4325384 | tf_op jit(solution)/shard_map/ppermute | solution.py:841
  (48 other events, 106.8 us)

commit v3 on v2

--- a/solution.py
+++ b/solution.py
@@ -17,6 +17,7 @@
 CHUNKS = 16
 LAG = 3
 GROUPS = 4
+FFN_GROUPS = 2
 
 
 def matmul(left, right):
@@ -837,6 +838,285 @@
     )(left, right)
 
 
+def ffn_kernel(
+    n_head,
+    x_ref,
+    mix_ref,
+    cot_ref,
+    gain_ref,
+    gain_other,
+    gate_l,
+    gate_r,
+    up_l,
+    up_r,
+    down_l,
+    down_r,
+    sum_ref,
+    n_ref,
+    ffn_left,
+    ffn_right,
+    down_kept,
+    gate_kept,
+    gate_sent,
+    up_kept,
+    up_sent,
+    act_ref,
+    gig_ref,
+    uig_ref,
+    cot_land,
+    n_land,
+    act_land,
+    gig_land,
+    uig_land,
+    down_sent,
+    down_land,
+    out_tile,
+    out_sem,
+    trade_send,
+    trade_recv,
+    cross_send,
+    cross_recv,
+    left,
+    right,
+    from_lo,
+    from_hi,
+    *sems,
+):
+    rows, width = x_ref.shape
+    half = width // 2
+    quarter = half // 2
+    units = act_ref.shape[1]
+    x_at = lax.axis_index("fsdp")
+    ctx_at = lax.axis_index("ctx")
+    core = lax.rem(ctx_at, 2)
+    own = pl.ds(pl.multiple_of(x_at * half, half), half)
+    other = pl.ds(pl.multiple_of((1 - x_at) * half, half), half)
+    barrier = line_greet(n_head)
+    pl.semaphore_signal(barrier, inc=1, device_id={"fsdp": 1 - x_at}, device_id_type=MESH)
+    pl.semaphore_signal(barrier, inc=1, device_id={"ctx": ctx_at ^ 1}, device_id_type=MESH)
+    pl.semaphore_wait(barrier, line_peers(n_head) + 2)
+
+    def trade(src, dst, at):
+        return pltpu.make_async_remote_copy(
+            src_ref=src,
+            dst_ref=dst,
+            send_sem=trade_send.at[at],
+            recv_sem=trade_recv.at[at],
+            device_id={"ctx": ctx_at ^ 1},
+            device_id_type=MESH,
+        )
+
+    def absolute(side, c):
+        start = (x_at if side == 0 else 1 - x_at) * half + c * quarter
+        return pl.ds(pl.multiple_of(start, quarter), quarter)
+
+    def relative(side, c):
+        return pl.ds(pl.multiple_of(side * half + c * quarter, quarter), quarter)
+
+    cot_trades = [
+        trade(cot_ref.at[:, absolute(j, 1 - core)], cot_land.at[:, pl.ds(j * quarter, quarter)], j)
+        for j in range(2)
+    ]
+    for copy in cot_trades:
+        copy.start()
+
+    def row_trades(g):
+        mine = pl.ds(pl.multiple_of(g * (rows // FFN_GROUPS), rows // FFN_GROUPS), rows // FFN_GROUPS)
+        at = 2 + g * 5
+        return [
+            trade(act_ref.at[mine], act_land.at[mine], at),
+            trade(gig_ref.at[mine], gig_land.at[mine], at + 1),
+            trade(uig_ref.at[mine], uig_land.at[mine], at + 2),
+            trade(n_ref.at[mine, relative(0, 1 - core)], n_land.at[mine, pl.ds(0, quarter)], at + 3),
+            trade(n_ref.at[mine, relative(1, 1 - core)], n_land.at[mine, pl.ds(quarter, quarter)], at + 4),
+        ]
+
+    step, steps, drain = line_sum(n_head, left, right, left, right, sum_ref, from_lo, from_hi, sems)
+
+    def run(s, carry):
+        step(s)
+        return carry
+
+    size = rows // FFN_GROUPS
+    per_group = CHUNKS // FFN_GROUPS
+
+    def one_group(g, carry):
+        mine = pl.ds(pl.multiple_of(g * size, size), size)
+        base = (g - 1) * per_group
+        stops = [base + (per_group * i) // 4 for i in range(5)]
+        hid_l = x_ref[mine, own].astype(F32) + mix_ref[mine, :half].astype(F32)
+        hid_r = x_ref[mine, other].astype(F32) + mix_ref[mine, half:].astype(F32)
+        total = jnp.sum(hid_l * hid_l, axis=1, keepdims=True) + jnp.sum(hid_r * hid_r, axis=1, keepdims=True)
+        scale = lax.rsqrt(total / width + EPSILON)
+        n_ref[mine, :half] = (hid_l * scale * gain_ref[1:2, :]).astype(BF)
+        n_ref[mine, half:] = (hid_r * scale * gain_other[1:2, :]).astype(BF)
+        lax.fori_loop(stops[0], stops[1], run, 0)
+        gate = matmul(n_ref[mine, :half], gate_l[...]) + matmul(n_ref[mine, half:], gate_r[...])
+        up = matmul(n_ref[mine, :half], up_l[...]) + matmul(n_ref[mine, half:], up_r[...])
+        lax.fori_loop(stops[1], stops[2], run, 0)
+        sigma = jax.nn.sigmoid(gate)
+        silu = gate * sigma
+        act_ref[mine, :] = (silu * up).astype(BF)
+        grad = mat_trans(cot_ref[mine, own], down_l[...]) + mat_trans(cot_ref[mine, other], down_r[...])
+        gig_ref[mine, :] = (grad * up * sigma * (1.0 + gate * (1.0 - sigma))).astype(BF)
+        uig_ref[mine, :] = (grad * silu).astype(BF)
+        lax.fori_loop(stops[2], stops[3], run, 0)
+        gig = gig_ref[mine, :]
+        uig = uig_ref[mine, :]
+        left[mine, :] = (mat_trans(gig, gate_l[...]) + mat_trans(uig, up_l[...])).astype(BF)
+        lax.fori_loop(stops[3], stops[4], run, 0)
+        right[mine, :] = (mat_trans(gig, gate_r[...]) + mat_trans(uig, up_r[...])).astype(BF)
+        for copy in row_trades(g):
+            copy.start()
+        return carry
+
+    lax.fori_loop(0, FFN_GROUPS, one_group, 0)
+    first = CHUNKS - per_group
+    rest = steps - first
+    tile = 128
+    down_tiles = units // tile
+    row_tiles = quarter // tile
+    total_work = down_tiles + 4 * row_tiles + 2 * FFN_GROUPS
+
+    def sums(i, weight=1):
+        lax.fori_loop(
+            first + (rest * i) // total_work, first + (rest * (i + weight)) // total_work, run, 0
+        )
+
+    for copy in cot_trades:
+        copy.wait_recv()
+
+    def landed(g, carry):
+        for copy in row_trades(g):
+            copy.wait_recv()
+        return carry
+
+    lax.fori_loop(0, FFN_GROUPS, landed, 0)
+
+    def down_tile(t, carry):
+        sums(t)
+        cut = pl.ds(pl.multiple_of(t * tile, tile), tile)
+        mine = act_ref[:, cut]
+        theirs = act_land[:, cut]
+        for dst, side in ((down_sent, 1), (down_kept, 0)):
+            dst[cut, :] = (
+                trans_mat(mine, cot_ref[:, absolute(side, core)])
+                + trans_mat(theirs, cot_land[:, side * quarter : (side + 1) * quarter])
+            ).astype(BF)
+        return carry
+
+    lax.fori_loop(0, down_tiles, down_tile, 0)
+    cross = pltpu.make_async_remote_copy(
+        src_ref=down_sent,
+        dst_ref=down_land,
+        send_sem=cross_send,
+        recv_sem=cross_recv,
+        device_id={"fsdp": 1 - x_at},
+        device_id_type=MESH,
+    )
+    cross.start()
+    done = down_tiles
+
+    def out_copy(dst, t, slot):
+        cut = pl.ds(pl.multiple_of(t * tile, tile), tile)
+        return pltpu.make_async_copy(out_tile.at[slot], dst.at[cut], out_sem.at[slot])
+
+    outs = (
+        (gate_sent, 1, gig_ref, gig_land),
+        (gate_kept, 0, gig_ref, gig_land),
+        (up_sent, 1, uig_ref, uig_land),
+        (up_kept, 0, uig_ref, uig_land),
+    )
+    for dst, side, own_grad, their_grad in outs:
+
+        def row_tile(t, carry):
+            sums(done + t)
+            slot = lax.rem(t, 2)
+            there = pl.ds(pl.multiple_of(side * half + core * quarter + t * tile, tile), tile)
+            landing = pl.ds(pl.multiple_of(side * quarter + t * tile, tile), tile)
+            value = (
+                trans_mat(n_ref[:, there], own_grad[...]) + trans_mat(n_land[:, landing], their_grad[...])
+            ).astype(BF)
+
+            @pl.when(t >= 2)
+            def _():
+                out_copy(dst, t - 2, slot).wait()
+
+            out_tile[slot] = value
+            out_copy(dst, t, slot).start()
+            return carry
+
+        lax.fori_loop(0, row_tiles, row_tile, 0)
+        for t in range(max(row_tiles - 2, 0), row_tiles):
+            out_copy(dst, t, t % 2).wait()
+        done += row_tiles
+
+    def project_down(g, carry):
+        mine = pl.ds(pl.multiple_of(g * size, size), size)
+        sums(done + 2 * g, 2)
+        ffn_left[mine, :] = matmul(act_ref[mine, :], down_l[...]).astype(BF)
+        ffn_right[mine, :] = matmul(act_ref[mine, :], down_r[...]).astype(BF)
+        return carry
+
+    lax.fori_loop(0, FFN_GROUPS, project_down, 0)
+    cross.wait_recv()
+
+    def finish(t, carry):
+        cut = pl.ds(pl.multiple_of(t * tile, tile), tile)
+        down_kept[cut, :] = (down_kept[cut, :].astype(F32) + down_land[cut, :].astype(F32)).astype(BF)
+        return carry
+
+    lax.fori_loop(0, down_tiles, finish, 0)
+    cross.wait_send()
+    for copy in cot_trades:
+        copy.wait_send()
+
+    def sent(g, carry):
+        for copy in row_trades(g):
+            copy.wait_send()
+        return carry
+
+    lax.fori_loop(0, FFN_GROUPS, sent, 0)
+    drain()
+
+
+def ffn_sum(inputs, mixed, cot, gains, gains_other, gate, gate_o, up, up_o, down, down_o, n_head, collective_id):
+    rows, width = inputs.shape
+    units = gate.shape[1]
+    vmem = pl.BlockSpec(memory_space=pltpu.VMEM)
+    wide = jax.ShapeDtypeStruct((rows, width), BF)
+    narrow = jax.ShapeDtypeStruct((rows, width // 2), BF)
+    quarter = width // 4
+    flat = jax.ShapeDtypeStruct((quarter, units), BF)
+    trades = 2 + 5 * FFN_GROUPS
+    return pl.pallas_call(
+        functools.partial(ffn_kernel, n_head),
+        out_shape=(wide, wide, narrow, narrow, jax.ShapeDtypeStruct((units, quarter), BF)) + (flat,) * 4,
+        in_specs=[vmem] * 11,
+        out_specs=(vmem,) * 5 + (pl.BlockSpec(memory_space=pl.ANY),) * 4,
+        scratch_shapes=[pltpu.VMEM((rows, units), BF)] * 3
+        + [pltpu.VMEM((rows, width // 2), BF)] * 2
+        + [pltpu.VMEM((rows, units), BF)] * 3
+        + [pltpu.VMEM((units, quarter), BF)] * 2
+        + [
+            pltpu.VMEM((2, 128, units), BF),
+            pltpu.SemaphoreType.DMA((2,)),
+            pltpu.SemaphoreType.DMA((trades,)),
+            pltpu.SemaphoreType.DMA((trades,)),
+            pltpu.SemaphoreType.DMA,
+            pltpu.SemaphoreType.DMA,
+        ]
+        + line_scratch(rows, width),
+        compiler_params=pltpu.CompilerParams(
+            collective_id=collective_id, has_side_effects=True, vmem_limit_bytes=66_000_000
+        ),
+        cost_estimate=pl.CostEstimate(
+            flops=50_000_000_000, bytes_accessed=8 * rows * width, transcendentals=0
+        ),
+        name="ffn_sum",
+    )(inputs, mixed, cot, gains, gains_other, gate, gate_o, up, up_o, down, down_o)
+
+
 def flip(array, axis, bit, size):
     return lax.ppermute(array, axis, [(i, i ^ bit) for i in range(size)])
 
@@ -900,41 +1180,33 @@
     attended, lse, mixed, gate_other, up_other, down_other = attend_sum(
         queries, pair, output_weight, out_other, gate_weight, up_weight, down_begun, n_ctx, n_head, 1
     )
+    low_sum, _, down_left, down_right, down_kept, gate_kept, gate_sent, up_kept, up_sent = ffn_sum(
+        inputs,
+        mixed,
+        cotangent,
+        gains_local,
+        gains_other,
+        gate_weight,
+        gate_other,
+        up_weight,
+        up_other,
+        down_weight,
+        down_other,
+        n_head,
+        2,
+    )
+    normed_two_grad = low_sum.astype(F32)
     gain_one = jnp.concatenate([gains_local[0], gains_other[0]])
     gain_two = jnp.concatenate([gains_local[1], gains_other[1]])
-    late_inputs, late_cot, normed_one, mixed = lax.optimization_barrier(
-        (inputs, cotangent, normed_one, mixed)
-    )
+    late_inputs, late_cot, normed_one, _ = lax.optimization_barrier((inputs, cotangent, normed_one, low_sum))
     in_float = own_first(late_inputs).astype(F32)
     cot = own_first(late_cot)
     scale_one = lax.rsqrt(jnp.mean(in_float * in_float, axis=-1, keepdims=True) + EPSILON)
     unit_one = in_float * scale_one
-    one_pair = trade_columns(normed_one)
-
     hidden = in_float + mixed.astype(F32)
     scale_two = lax.rsqrt(jnp.mean(hidden * hidden, axis=-1, keepdims=True) + EPSILON)
     unit_two = hidden * scale_two
-    normed_two = (unit_two * gain_two).astype(BF)
-
-    act_grad = mat_trans(cot[:, :half], down_weight) + mat_trans(cot[:, half:], down_other)
-    gate_pre = matmul(normed_two[:, :half], gate_weight) + matmul(normed_two[:, half:], gate_other)
-    up_pre = matmul(normed_two[:, :half], up_weight) + matmul(normed_two[:, half:], up_other)
-    sigma = jax.nn.sigmoid(gate_pre)
-    silu_gate = gate_pre * sigma
-    activated = (silu_gate * up_pre).astype(BF)
-    gate_in_grad = (act_grad * up_pre * sigma * (1.0 + gate_pre * (1.0 - sigma))).astype(BF)
-    up_in_grad = (act_grad * silu_gate).astype(BF)
-    low_left = (mat_trans(gate_in_grad, gate_weight) + mat_trans(up_in_grad, up_weight)).astype(BF)
-    low_right = (mat_trans(gate_in_grad, gate_other) + mat_trans(up_in_grad, up_other)).astype(BF)
-    cot_pair = trade_columns(cot)
-    two_pair = trade_columns(normed_two)
-    down_part = trans_mat(trade(activated), cot_pair).astype(BF)
-    gate_part = trans_mat(two_pair, trade(gate_in_grad)).astype(BF)
-    low_left, low_right, down_part, gate_part = lax.optimization_barrier(
-        (low_left, low_right, down_part, gate_part)
-    )
-    normed_two_grad = head_sum(low_left, low_right, n_head, 2).astype(F32)
-    up_part = trans_mat(two_pair, trade(up_in_grad)).astype(BF)
+    one_pair = trade_columns(normed_one)
     scaled_two = normed_two_grad * gain_two
     gain_two_part = jnp.sum(normed_two_grad * unit_two, axis=0)
     hidden_grad = cot.astype(F32) + scale_two * (
@@ -942,13 +1214,11 @@
     )
     hidden_low = hidden_grad.astype(BF)
 
-    down_left = matmul(activated, down_weight).astype(BF)
-    down_right = matmul(activated, down_other).astype(BF)
     attended_grad = (
         mat_trans(hidden_low[:, :half], output_weight) + mat_trans(hidden_low[:, half:], out_other)
     ).astype(BF)
     out_part = trans_mat(trade(attended), trade_columns(hidden_low)).astype(BF)
-    attended_grad, up_part, out_part = lax.optimization_barrier((attended_grad, up_part, out_part))
+    attended_grad, out_part = lax.optimization_barrier((attended_grad, out_part))
     query_acc, pair_acc, ffn_out = attend_back(
         queries, attended_grad, attended, lse, pair, down_left, down_right, n_head, 6
     )
@@ -980,7 +1250,8 @@
     )
 
     def total(kept, sent):
-        kept = (kept.astype(F32) + flip(sent, "fsdp", 1, 2).astype(F32)).astype(BF)
+        if sent is not None:
+            kept = (kept.astype(F32) + flip(sent, "fsdp", 1, 2).astype(F32)).astype(BF)
         for bit in every[:-1]:
             kept = (kept.astype(F32) + flip(kept, "ctx", bit, n_ctx).astype(F32)).astype(BF)
         return kept
@@ -991,26 +1262,19 @@
         second = jnp.where(core == 0, got, kept)
         return jnp.concatenate([first, second], axis=dim).astype(F32)
 
-    def by_rows(part):
-        return spread(total(part[:quarter], part[quarter:]), 0)
-
-    def by_columns(part):
-        return spread(total(part[:, :quarter], part[:, quarter:]), 1)
-
-    down_grad = by_columns(down_part)
-    gate_grad = by_rows(gate_part)
-    up_grad = by_rows(up_part)
-    output_grad = by_columns(out_part)
-    qkv_grad = by_rows(qkv_part)
+    down_grad = spread(total(down_kept, None), 1)
+    gate_grad = spread(total(gate_kept, gate_sent), 0)
+    up_grad = spread(total(up_kept, up_sent), 0)
+    output_grad = spread(total(out_part[:, :quarter], out_part[:, quarter:]), 1)
+    qkv_grad = spread(total(qkv_part[:quarter], qkv_part[quarter:]), 0)
     query_grad = qkv_grad[:, :q_width]
     key_grad = qkv_grad[:, q_width : q_width + HEAD_DIM]
     value_grad = qkv_grad[:, q_width + HEAD_DIM :]
 
-    def gain_total(part):
-        kept = part[:half].reshape(8, -1) + flip(part[half:].reshape(8, -1), "fsdp", 1, 2)
-        for bit in every:
-            kept = kept + flip(kept, "ctx", bit, n_ctx)
-        return kept.reshape(half)
+    gain_parts = jnp.stack([gain_one_part, gain_two_part])
+    gain_kept = gain_parts[:, :half] + flip(gain_parts[:, half:], "fsdp", 1, 2)
+    for bit in every:
+        gain_kept = gain_kept + flip(gain_kept, "ctx", bit, n_ctx)
 
     return (
         outputs,
@@ -1022,8 +1286,8 @@
         gate_grad,
         up_grad,
         down_grad,
-        gain_total(gain_one_part),
-        gain_total(gain_two_part),
+        gain_kept[0],
+        gain_kept[1],
     )
 
 

time: 603 us -> 518 us (0.86)
  matrix products: 66.5 us -> 12.6 us
  waiting for transfers between devices: 65.1 us -> 26 us
  Pallas kernels: 347 us -> 375 us
  local copies, waits for them, and re-layouts: 31 us -> 21.1 us
  other arithmetic: 69.9 us -> 62.9 us
    pallas_call x0 -> x1, Pallas kernels: none -> 90.3 us  [ffn_sum(): pl.pallas_call(functools.partial(ffn_kernel, n_head), out_shape=(wide, wi...]
    pallas_call x2 -> x1, Pallas kernels: 127 us -> 63.8 us  [head_sum(): pl.pallas_call(functools.partial(head_sum_kernel, n), out_shape=jax.Shape...]
    ppermute x30 -> x21, waiting for transfers between devices: 65.1 us -> 26 us  [flip(): return lax.ppermute(array, axis, [(i, i ^ bit) for i in range(size)])]
    dot_general x5 -> x2, matrix products: 26 us -> 6.38 us  [trans_mat(): lax.dot_general(left, right, (((0,), (0,)), ((), ())), preferred_element_...]
    dot_general x6 -> x0, matrix products: 18.4 us -> none  [matmul(): return jnp.dot(left, right, preferred_element_type=F32)]
    dot_general x10 -> x4, matrix products: 22.1 us -> 6.25 us  [mat_trans(): lax.dot_general(left, right, (((1,), (1,)), ((), ())), preferred_element_...]
    unnamed x136 -> x84, local copies, waits for them, and re-layouts: 15.3 us -> 9.19 us
    ppermute x30 -> x21, starting transfers between devices: 14.7 us -> 11.3 us  [flip(): return lax.ppermute(array, axis, [(i, i ^ bit) for i in range(size)])]
  transfers between devices with their start and end apart: 30 -> 21, of which waited for: 6 -> 4; matrix products, arithmetic and copies ran while one was open for 21% -> 13% of each run, Pallas kernels for 36% -> 30%
where the time goes in v3:
time: 518 us; the launch traced here: 511 us
  Pallas kernels  375 us (72%)
  other arithmetic  62.9 us (12%)
  waiting for transfers between devices  26 us (5%)
  local copies, waits for them, and re-layouts  21.1 us (4%)
  matrix products  12.6 us (2%)
  starting transfers between devices  11.3 us (2%)
    pallas_call x1, Pallas kernels, ffn_sum(): pl.pallas_call(functools.partial(ffn_kernel, n_head), out_shape=(wide, wi...  90.3 us
    pallas_call x1, Pallas kernels, attend_sum(): pl.pallas_call(functools.partial(forward_kernel, n_ctx, n_head, span), ou...  77.6 us
    pallas_call x1, Pallas kernels, attend_back(): pl.pallas_call(functools.partial(backward_kernel, n_head, group, span), o...  69.9 us
    pallas_call x1, Pallas kernels, head_sum(): pl.pallas_call(functools.partial(head_sum_kernel, n), out_shape=jax.Shape...  63.8 us
    pallas_call x1, Pallas kernels, project(): pl.pallas_call(functools.partial(project_kernel, n_ctx), out_shape=(jax.S...  51.7 us
    ppermute x21, waiting for transfers between devices, flip(): return lax.ppermute(array, axis, [(i, i ^ bit) for i in range(size)])  26 us
    pallas_call x1, Pallas kernels, scatter_pairs(): pl.pallas_call(functools.partial(scatter_kernel, n_ctx), out_shape=jax.Sh...  21.8 us
    ppermute x21, starting transfers between devices, flip(): return lax.ppermute(array, axis, [(i, i ^ bit) for i in range(size)])  11.3 us
  transfers between devices with their start and end apart: 21, of which 4 were waited for; matrix products, arithmetic and copies ran while one was open for 13% of the time, Pallas kernels for 30%

profile of v3, /device:TPU:0, one launch (start us, length us, event | category | flops | bytes accessed | tf_op | source)
XLA Modules:
  0.0 510.7 jit_solution(8179502447265068932)
XLA Ops:
  4.5 2.5 pad_maximum_fusion.w_ref
  6.9 1.8 negate_select_fusion
  8.8 51.7 %project.1 = (bf16[512,512]{1,0:T(8,128)(2,1)}, bf16[4096,128]{1,0:T(8,128)(2,1)}, bf16[512,2048]{1,0:T(8,128)(2,1)}, bf16[1024,640]{1,0:T(8,128)(2,1)}, f32[8,1...) custom-call(bf16[512,2048]{1,0:T(8,128)(2,1)} %x_ref.3, ...), custom_call_target="tpu_custom_call" | custom-call | tf_op jit(solution)/shard_map/project/pallas_call | solution.py:646
  61.4 77.6 %attend_sum.1 = (bf16[512,512]{1,0:T(8,128)(2,1)}, f32[8,1,512]{2,1,0:T(1,128)}, bf16[512,2048]{1,0:T(8,128)(2,1)}, bf16[1024,1408]{1,0:T(8,128)(2,1)}, bf16[102...) custom-call(bf16[512,512]{1,0:T(8,128)(2,1)} %get-tuple-element.44.q_ref, ...), custom_call_target="tpu_custom_call", output_to_operand_aliasing={{5}: (6, {})} | custom-call | flops 49999998976 | bytes 8388608 | tf_op jit(solution)/shard_map/attend_sum/pallas_call | solution.py:237
  139.0 90.3 %ffn_sum.1 = (bf16[512,2048]{1,0:T(8,128)(2,1)}, bf16[512,2048]{1,0:T(8,128)(2,1)}, bf16[512,1024]{1,0:T(8,128)(2,1)}, bf16[512,1024]{1,0:T(8,128)(2,1)}, bf16[1...) custom-call(bf16[512,2048]{1,0:T(8,128)(2,1)} %x_ref.3, ...), custom_call_target="tpu_custom_call" | custom-call | flops 49999998976 | bytes 8388608 | tf_op jit(solution)/shard_map/ffn_sum/pallas_call | solution.py:1092
  229.4 1.9 fusion.64
  232.2 1.3 multiply_reduce_fusion
  233.8 2.0 fusion.11
  236.1 2.9 fusion.58
  239.0 1.3 copy-done.8
  240.3 1.4 fusion.62
  241.6 2.2 broadcast_select_fusion.9
  244.7 1.8 broadcast_select_fusion.8
  249.4 1.5 fusion.35.g_ref
  251.0 1.3 collective-permute-start.16
  252.3 2.2 fusion.27
  254.5 69.9 %attend_backward.1 = (f32[512,512]{1,0:T(8,128)}, f32[4096,128]{1,0:T(8,128)}, bf16[512,2048]{1,0:T(8,128)(2,1)}) custom-call(bf16[512,512]{1,0:T(8,128)(2,1)} %get-tuple-element.44.q_ref, bf16[512,512]{1,0:T(8,128)(2,1)} %fusion.35.g_ref, bf16[512,512]{1,0:T(8,128)(2,1)} %get-tuple-element.56.o_ref, f32[8,1,512]{2,1,0:T(1,128)} %get-tuple-element.58.lse_ref, ...), custom_call_target="tpu_custom_call" | custom-call | flops 34359738368 | bytes 2097152 | tf_op jit(solution)/shard_map/attend_backward/pallas_call | solution.py:374
  324.4 21.8 %scatter_pairs.1 = f32[512,128]{1,0:T(8,128)} custom-call(f32[4096,128]{1,0:T(8,128)} %get-tuple-element.63.part_ref), custom_call_target="tpu_custom_call" | custom-call | tf_op jit(solution)/shard_map/scatter_pairs/pallas_call | solution.py:500
  346.2 1.2 fusion.67
  350.8 1.3 fusion.48
  352.3 2.0 convolution_convert_fusion.1.left_ref
  354.2 2.0 convolution_convert_fusion.right_ref
  356.2 2.9 add_convert_fusion.5
  359.9 2.8 add_convert_fusion.3
  362.7 1.3 collective-permute-start.14
  364.0 3.3 add_convert_fusion.1
  367.3 3.2 collective-permute-done.7
  371.5 4.1 fusion.24
  375.7 63.8 %head_sum.1 = bf16[512,2048]{1,0:T(8,128)(2,1)} custom-call(bf16[512,1024]{1,0:T(8,128)(2,1)} %convolution_convert_fusion.1.left_ref, bf16[512,1024]{1,0:T(8,128)(2,1)} %convolution_convert_fusion.right_ref), custom_call_target="tpu_custom_call" | custom-call | flops 40000000000 | bytes 4194304 | tf_op jit(solution)/shard_map/head_sum/pallas_call | solution.py:827
  439.5 3.1 fusion.13
  442.5 6.5 %fusion.7 = (f32[512,2048]{1,0:T(8,128)S(1)}, bf16[512,2048]{1,0:T(8,128)(2,1)S(1)}) fusion(bf16[512,2048]{1,0:T(8,128)(2,1)} %head_sum.1, bf16[512,2048]{1,0:T(8,128)(2,1)S(1)} %get-tuple-element.92, f32[512]{0:T(512)S(1)} %broadcast_multiply_fusion.1, f32[2048]{0:T(1024)S(1)} %pad_maximum_fusion.8, f32[512]{0:T(512)S(1)} %add_rsqrt_fusion, ...), kind=kLoop, calls=%fused_computation.13 | loop fusion | flops 27262976 | bytes 20996096 | tf_op jit(solution)/shard_map/add | solution.py:1247
  450.6 2.0 collective-permute-start.18
  452.6 3.1 maximum_select_fusion
  455.7 10.3 %collective-permute-done.18 = f32[2,1024]{1,0:T(2,128)S(1)} collective-permute-done((f32[2,1024]{1,0:T(2,128)S(1)}, f32[2,1024]{1,0:T(2,128)S(1)}, u32[]{:S(2)}, u32[]{:S(2)}) %collective-permute-start.18) | collective-permute-done | bytes 8224 | tf_op jit(solution)/shard_map/ppermute | solution.py:1121
  467.0 2.7 collective-permute-done.19
  469.8 1.3 add_convert_fusion.8
  471.7 2.2 maximum_select_fusion.3
  475.6 1.6 maximum_convert_fusion.4
  477.2 2.1 add_convert_fusion.4
  479.6 2.1 add_convert_fusion.2
  482.1 9.7 %collective-permute-done.5 = bf16[512,640]{1,0:T(8,128)(2,1)S(1)} collective-permute-done((bf16[512,640]{1,0:T(8,128)(2,1)S(1)}, bf16[512,640]{1,0:T(8,128)(2,1)S(1)}, u32[]{:S(2)}, u32[]{:S(2)}) %collective-permute-start.5) | collective-permute-done | bytes 655392 | tf_op jit(solution)/shard_map/ppermute | solution.py:1121
  492.5 3.3 maximum_convert_fusion.2
  496.1 1.6 slice.196
  498.6 1.9 copy.25
  501.4 1.6 broadcast_select_fusion.5
  503.0 2.9 maximum_convert_fusion
  506.0 1.6 broadcast_select_fusion.3
  507.6 2.9 maximum_convert_fusion.1
  (163 shorter events, 23.1 us)
Async XLA Ops:
  0.7 8.1 %copy-start.25 = (s32[128]{0:T(128)}, s32[128]{0:T(128)S(1)}, u32[]{:S(2)}) copy-start(s32[128]{0:T(128)S(1)} %get-tuple-element.145) | copy-start | bytes 1540
  0.7 8.1 %copy-start.27 = (s32[128]{0:T(128)}, s32[128]{0:T(128)S(1)}, u32[]{:S(2)}) copy-start(s32[128]{0:T(128)S(1)} %get-tuple-element.146) | copy-start | bytes 1540
  0.7 8.1 %copy-start.29 = (s32[128]{0:T(128)}, s32[128]{0:T(128)S(1)}, u32[]{:S(2)}) copy-start(s32[128]{0:T(128)S(1)} %get-tuple-element.147) | copy-start | bytes 1540
  0.7 8.1 %copy-start.31 = (s32[128]{0:T(128)}, s32[128]{0:T(128)S(1)}, u32[]{:S(2)}) copy-start(s32[128]{0:T(128)S(1)} %get-tuple-element.148) | copy-start | bytes 1540
  0.7 8.1 %copy-start.33 = (pred[128]{0:T(512)(128)(4,1)}, pred[128]{0:T(512)(128)(4,1)S(1)}, u32[]{:S(2)}) copy-start(pred[128]{0:T(512)(128)(4,1)S(1)} %get-tuple-element.143) | copy-start | bytes 388
  0.7 8.1 %copy-start.35 = (pred[128]{0:T(512)(128)(4,1)}, pred[128]{0:T(512)(128)(4,1)S(1)}, u32[]{:S(2)}) copy-start(pred[128]{0:T(512)(128)(4,1)S(1)} %get-tuple-element.144) | copy-start | bytes 388
  4.3 56.2 %copy-start.23 = (f32[512]{0:T(512)}, f32[512]{0:T(512)S(1)}, u32[]{:S(2)}) copy-start(f32[512]{0:T(512)S(1)} %add_convert_fusion.10) | copy-start | bytes 6148
  4.5 4.3 copy-start.22
  229.4 2.2 copy-start
  229.4 2.8 copy-start.4
  233.8 2.0 copy-start.5
  236.1 2.9 copy-start.7
  241.6 2.3 copy-start.39
  241.6 2.8 copy-start.15
  243.9 8.4 %collective-permute-start.1 = (bf16[512,1024]{1,0:T(8,128)(2,1)S(1)}, bf16[512,1024]{1,0:T(8,128)(2,1)S(1)}, u32[]{:S(2)}, u32[]{:S(2)}) collective-permute-start(bf16[512,1024]{1,0:T(8,128)(2,1)S(1)} %get-tuple-element.112), channel_id=1, source_target_pairs={{0,8},{8,0},{16,24},{24,16},{1,9},{9,1},{17,25},{25,17},{2,10},{10... | collective-permute-start | bytes 3145736 | tf_op jit(solution)/shard_map/ppermute | solution.py:1121
  243.9 7.0 %collective-permute-start = (bf16[512,512]{1,0:T(8,128)(2,1)S(1)}, bf16[512,512]{1,0:T(8,128)(2,1)S(1)}, u32[]{:S(2)}, u32[]{:S(2)}) collective-permute-start(bf16[512,512]{1,0:T(8,128)(2,1)S(1)} %copy-done.39), channel_id=1, source_target_pairs={{0,8},{8,0},{16,24},{24,16},{1,9},{9,1},{17,25},{25,17},{2,10},{10... | collective-permute-start | bytes 1572872 | tf_op jit(solution)/shard_map/ppermute | solution.py:1121
  244.6 4.0 copy-start.9
  244.6 4.0 copy-start.19
  246.5 2.9 copy-start.38
  246.5 125.0 %collective-permute-start.2 = (bf16[512,1024]{1,0:T(8,128)(2,1)}, bf16[512,1024]{1,0:T(8,128)(2,1)}, u32[]{:S(2)}, u32[]{:S(2)}) collective-permute-start(bf16[512,1024]{1,0:T(8,128)(2,1)} %get-tuple-element.104), channel_id=1, source_target_pairs={{0,8},{8,0},{16,24},{24,16},{1,9},{9,1},{17,25},{25,17},{2,10},{10... | collective-permute-start | bytes 3145736 | tf_op jit(solution)/shard_map/ppermute | solution.py:1121
  246.6 109.6 %collective-permute-start.10 = (bf16[512,1408]{1,0:T(8,128)(2,1)}, bf16[512,1408]{1,0:T(8,128)(2,1)}, u32[]{:S(2)}, u32[]{:S(2)}) collective-permute-start(bf16[512,1408]{1,0:T(8,128)(2,1)} %get-tuple-element.71), channel_id=1, source_target_pairs={{0,4},{4,0},{1,5},{5,1},{2,6},{6,2},{3,7},{7,3},{8,12},{12,8},{9,1... | collective-permute-start | bytes 4325384 | tf_op jit(solution)/shard_map/ppermute | solution.py:1121
  247.8 111.4 %collective-permute-start.13 = (bf16[512,1408]{1,0:T(8,128)(2,1)}, bf16[512,1408]{1,0:T(8,128)(2,1)}, u32[]{:S(2)}, u32[]{:S(2)}) collective-permute-start(bf16[512,1408]{1,0:T(8,128)(2,1)} %get-tuple-element.73), channel_id=1, source_target_pairs={{0,4},{4,0},{1,5},{5,1},{2,6},{6,2},{3,7},{7,3},{8,12},{12,8},{9,1... | collective-permute-start | bytes 4325384 | tf_op jit(solution)/shard_map/ppermute | solution.py:1121
  251.0 111.7 %collective-permute-start.16 = (bf16[1408,512]{1,0:T(8,128)(2,1)}, bf16[1408,512]{1,0:T(8,128)(2,1)}, u32[]{:S(2)}, u32[]{:S(2)}) collective-permute-start(bf16[1408,512]{1,0:T(8,128)(2,1)} %get-tuple-element.74), channel_id=1, source_target_pairs={{0,16},{8,24},{16,0},{24,8},{1,17},{9,25},{17,1},{25,9},{2,18},{10... | collective-permute-start | bytes 4325384 | tf_op jit(solution)/shard_map/ppermute | solution.py:1121
  346.2 2.4 copy-start.12
  350.4 1.8 copy-start.21
  350.4 1.8 copy-start.11
  352.1 19.4 %collective-permute-start.3 = (bf16[512,640]{1,0:T(8,128)(2,1)S(1)}, bf16[512,640]{1,0:T(8,128)(2,1)S(1)}, u32[]{:S(2)}, u32[]{:S(2)}) collective-permute-start(bf16[512,640]{1,0:T(8,128)(2,1)S(1)} %pad_maximum_fusion.5), channel_id=1, source_target_pairs={{0,8},{8,0},{16,24},{24,16},{1,9},{9,1},{17,25},{25,17},{2,10},{10... | collective-permute-start | bytes 1966088 | tf_op jit(solution)/shard_map/ppermute | solution.py:1121
  352.2 2.0 copy-start.37
  354.2 2.0 copy-start.17
  356.2 14.3 %collective-permute-start.7 = (bf16[512,512]{1,0:T(8,128)(2,1)S(1)}, bf16[512,512]{1,0:T(8,128)(2,1)S(1)}, u32[]{:S(2)}, u32[]{:S(2)}) collective-permute-start(bf16[512,512]{1,0:T(8,128)(2,1)S(1)} %slice.175), channel_id=1, source_target_pairs={{0,4},{4,0},{1,5},{5,1},{2,6},{6,2},{3,7},{7,3},{8,12},{12,8},{9,1... | collective-permute-start | bytes 1572872 | tf_op jit(solution)/shard_map/ppermute | solution.py:1121
  356.2 3.6 copy-start.16
  359.2 118.0 %collective-permute-start.11 = (bf16[512,1408]{1,0:T(8,128)(2,1)}, bf16[512,1408]{1,0:T(8,128)(2,1)}, u32[]{:S(2)}, u32[]{:S(2)}) collective-permute-start(bf16[512,1408]{1,0:T(8,128)(2,1)} %add_convert_fusion.5), channel_id=1, source_target_pairs={{0,16},{8,24},{16,0},{24,8},{1,17},{9,25},{17,1},{25,9},{2,18},{10... | collective-permute-start | bytes 4325384 | tf_op jit(solution)/shard_map/ppermute | solution.py:1121
  362.7 8.8 %copy-start.20 = (bf16[512,1024]{1,0:T(8,128)(2,1)S(1)}, bf16[512,1024]{1,0:T(8,128)(2,1)}, u32[]{:S(2)}) copy-start(bf16[512,1024]{1,0:T(8,128)(2,1)} %get-tuple-element.103) | copy-start | bytes 3145732
  362.7 116.9 %collective-permute-start.14 = (bf16[512,1408]{1,0:T(8,128)(2,1)}, bf16[512,1408]{1,0:T(8,128)(2,1)}, u32[]{:S(2)}, u32[]{:S(2)}) collective-permute-start(bf16[512,1408]{1,0:T(8,128)(2,1)} %add_convert_fusion.3), channel_id=1, source_target_pairs={{0,16},{8,24},{16,0},{24,8},{1,17},{9,25},{17,1},{25,9},{2,18},{10... | collective-permute-start | bytes 4325384 | tf_op jit(solution)/shard_map/ppermute | solution.py:1121
  371.5 98.3 %collective-permute-start.8 = (bf16[512,512]{1,0:T(8,128)(2,1)}, bf16[512,512]{1,0:T(8,128)(2,1)}, u32[]{:S(2)}, u32[]{:S(2)}) collective-permute-start(bf16[512,512]{1,0:T(8,128)(2,1)} %add_convert_fusion.9), channel_id=1, source_target_pairs={{0,16},{8,24},{16,0},{24,8},{1,17},{9,25},{17,1},{25,9},{2,18},{10... | collective-permute-start | bytes 1572872 | tf_op jit(solution)/shard_map/ppermute | solution.py:1121
  439.4 3.1 copy-start.1
  439.4 3.1 copy-start.3
  450.4 24.1 %collective-permute-start.4 = (bf16[512,640]{1,0:T(8,128)(2,1)S(1)}, bf16[512,640]{1,0:T(8,128)(2,1)S(1)}, u32[]{:S(2)}, u32[]{:S(2)}) collective-permute-start(bf16[512,640]{1,0:T(8,128)(2,1)S(1)} %slice.170), channel_id=1, source_target_pairs={{0,4},{4,0},{1,5},{5,1},{2,6},{6,2},{3,7},{7,3},{8,12},{12,8},{9,1... | collective-permute-start | bytes 1966088 | tf_op jit(solution)/shard_map/ppermute | solution.py:1121
  450.6 15.4 %collective-permute-start.18 = (f32[2,1024]{1,0:T(2,128)S(1)}, f32[2,1024]{1,0:T(2,128)S(1)}, u32[]{:S(2)}, u32[]{:S(2)}) collective-permute-start(f32[2,1024]{1,0:T(2,128)S(1)} %pad_maximum_fusion.6), channel_id=1, source_target_pairs={{0,4},{4,0},{1,5},{5,1},{2,6},{6,2},{3,7},{7,3},{8,12},{12,8},{9,1... | collective-permute-start | bytes 24584 | tf_op jit(solution)/shard_map/ppermute | solution.py:1121
  466.0 3.7 collective-permute-start.19
  469.7 4.1 collective-permute-start.20
  471.1 4.4 collective-permute-start.9
  471.7 2.2 copy-start.10
  473.8 18.2 %collective-permute-start.17 = (bf16[1408,512]{1,0:T(8,128)(2,1)S(1)}, bf16[1408,512]{1,0:T(8,128)(2,1)S(1)}, u32[]{:S(2)}, u32[]{:S(2)}) collective-permute-start(bf16[1408,512]{1,0:T(8,128)(2,1)S(1)} %copy-done.10), channel_id=1, source_target_pairs={{0,8},{8,0},{16,24},{24,16},{1,9},{9,1},{17,25},{25,17},{2,10},{10... | collective-permute-start | bytes 4325384 | tf_op jit(solution)/shard_map/ppermute | solution.py:1121
  474.6 17.2 %collective-permute-start.5 = (bf16[512,640]{1,0:T(8,128)(2,1)S(1)}, bf16[512,640]{1,0:T(8,128)(2,1)S(1)}, u32[]{:S(2)}, u32[]{:S(2)}) collective-permute-start(bf16[512,640]{1,0:T(8,128)(2,1)S(1)} %add_convert_fusion.7), channel_id=1, source_target_pairs={{0,16},{8,24},{16,0},{24,8},{1,17},{9,25},{17,1},{25,9},{2,18},{10... | collective-permute-start | bytes 1966088 | tf_op jit(solution)/shard_map/ppermute | solution.py:1121
  479.3 22.1 %collective-permute-start.12 = (bf16[512,1408]{1,0:T(8,128)(2,1)S(1)}, bf16[512,1408]{1,0:T(8,128)(2,1)}, u32[]{:S(2)}, u32[]{:S(2)}) collective-permute-start(bf16[512,1408]{1,0:T(8,128)(2,1)S(1)} %add_convert_fusion.4), channel_id=1, source_target_pairs={{0,8},{8,0},{16,24},{24,16},{1,9},{9,1},{17,25},{25,17},{2,10},{10... | collective-permute-start | bytes 4325384 | tf_op jit(solution)/shard_map/ppermute | solution.py:1121
  481.7 24.2 %collective-permute-start.15 = (bf16[512,1408]{1,0:T(8,128)(2,1)S(1)}, bf16[512,1408]{1,0:T(8,128)(2,1)}, u32[]{:S(2)}, u32[]{:S(2)}) collective-permute-start(bf16[512,1408]{1,0:T(8,128)(2,1)S(1)} %add_convert_fusion.2), channel_id=1, source_target_pairs={{0,8},{8,0},{16,24},{24,16},{1,9},{9,1},{17,25},{25,17},{2,10},{10... | collective-permute-start | bytes 4325384 | tf_op jit(solution)/shard_map/ppermute | solution.py:1121
  492.0 3.8 collective-permute-start.6
  (13 other events, 13.8 us)

commit v4 on v3

--- a/solution.py
+++ b/solution.py
@@ -30,6 +30,47 @@
 
 def trans_mat(left, right):
     return lax.dot_general(left, right, (((0,), (0,)), ((), ())), preferred_element_type=F32)
+
+
+def exchange(src, dst, axis, bit, send, recv):
+    return pltpu.make_async_remote_copy(
+        src_ref=src,
+        dst_ref=dst,
+        send_sem=send,
+        recv_sem=recv,
+        device_id={axis: lax.axis_index(axis) ^ bit},
+        device_id_type=MESH,
+    )
+
+
+def add_into(dst, left, right):
+    size = 64
+
+    def one(i, carry):
+        cut = pl.ds(pl.multiple_of(i * size, size), size)
+        dst[cut, :] = (left[cut, :].astype(F32) + right[cut, :].astype(F32)).astype(BF)
+        return carry
+
+    lax.fori_loop(0, dst.shape[0] // size, one, 0)
+
+
+class Chain:
+    def __init__(self, n_ctx, ref, land, send, recv):
+        self.ref, self.land, self.send, self.recv = ref, land, send, recv
+        self.bits = high_bits(n_ctx)[:-1]
+
+    def _copy(self, j):
+        return exchange(self.ref, self.land.at[j], "ctx", self.bits[j], self.send.at[j], self.recv.at[j])
+
+    def start(self):
+        self._copy(0).start()
+
+    def finish(self):
+        for j in range(len(self.bits)):
+            if j > 0:
+                self._copy(j).start()
+            self._copy(j).wait()
+            add_into(self.ref, self.ref, self.land.at[j])
 
 
 def high_bits(size):
@@ -263,6 +304,7 @@
 
 
 def backward_kernel(
+    n_ctx,
     n_head,
     group,
     span,
@@ -273,13 +315,26 @@
     p_ref,
     left_ref,
     right_ref,
+    gate_sent,
+    gate_kept,
+    up_sent,
+    up_kept,
     dq_ref,
     dp_ref,
     sum_ref,
+    gate_out,
+    up_out,
     q_pad,
     g_pad,
     acc_ref,
     dl_ref,
+    gate_land,
+    up_land,
+    far_land,
+    cross_send,
+    cross_recv,
+    far_send,
+    far_recv,
     work_l,
     work_r,
     from_lo,
@@ -291,6 +346,7 @@
     tiles = rows // span
     block = lax.axis_index("ctx") * 2 + lax.axis_index("fsdp")
     barrier = line_greet(n_head)
+    greet(n_ctx)
     dp_ref[...] = jnp.zeros_like(dp_ref)
     acc_ref[...] = jnp.zeros_like(acc_ref)
     for h in range(heads):
@@ -299,10 +355,23 @@
         g_pad[h] = head_lanes(g_ref, h, True)
         product = g_ref[:, cut].astype(F32) * o_ref[:, cut].astype(F32)
         dl_ref[h] = jnp.sum(product.T, axis=0, keepdims=True)
-    pl.semaphore_wait(barrier, line_peers(n_head))
+    pl.semaphore_wait(barrier, line_peers(n_head) + len(partners(n_ctx)))
+    crosses = [
+        exchange(sent, land, "fsdp", 1, cross_send.at[i], cross_recv.at[i])
+        for i, (sent, land) in enumerate(((gate_sent, gate_land), (up_sent, up_land)))
+    ]
+    for cross in crosses:
+        cross.start()
+    far = Chain(n_ctx, gate_out, far_land, far_send, far_recv)
+    hop_at = CHUNKS + 2
     step, steps, drain = line_sum(
         n_head, left_ref, right_ref, work_l, work_r, sum_ref, from_lo, from_hi, sems
     )
+
+    def hop():
+        crosses[0].wait_recv()
+        add_into(gate_out, gate_kept, gate_land)
+        far.start()
 
     def head_tile(h, pairs, start, masked):
         probs = jnp.exp(mat_trans(pairs, q_pad[h]) - lse_ref[h])
@@ -323,6 +392,10 @@
             def _():
                 step(2 * t + j)
 
+        @pl.when(2 * t == hop_at)
+        def _():
+            hop()
+
     def full(t, carry):
         two_steps(t)
         first = lax.rem(t, groups) * group
@@ -353,44 +426,67 @@
     for h in range(heads):
         dq_ref[:, h * HEAD_DIM : (h + 1) * HEAD_DIM] = acc_ref[h][:, :HEAD_DIM]
 
+    begun = 2 * (count + groups * tiles)
+
     def rest(s, carry):
         step(s)
-        return carry
-
-    lax.fori_loop(jnp.minimum(2 * (count + groups * tiles), steps), steps, rest, 0)
+
+        @pl.when(s == hop_at)
+        def _():
+            hop()
+
+        return carry
+
+    lax.fori_loop(jnp.minimum(begun, steps), steps, rest, 0)
     drain()
-
-
-def attend_back(queries, grads, attended, lse, pair, left, right, n_head, collective_id):
+    crosses[1].wait_recv()
+    add_into(up_out, up_kept, up_land)
+    for cross in crosses:
+        cross.wait_send()
+    far.finish()
+
+
+def attend_back(queries, grads, attended, lse, pair, left, right, parts, n_ctx, n_head, collective_id):
     rows, width = queries.shape
     heads = width // HEAD_DIM
     seq = pair.shape[0]
     group = 4 if heads % 4 == 0 else 2
     span = min(512, rows)
     vmem = pl.BlockSpec(memory_space=pltpu.VMEM)
+    flat = jax.ShapeDtypeStruct(parts[0].shape, BF)
+    n_far = len(high_bits(n_ctx)) - 1
     cost = pl.CostEstimate(
         flops=32 * rows * seq * width, bytes_accessed=8 * rows * width, transcendentals=0
     )
     return pl.pallas_call(
-        functools.partial(backward_kernel, n_head, group, span),
+        functools.partial(backward_kernel, n_ctx, n_head, group, span),
         out_shape=(
             jax.ShapeDtypeStruct((rows, width), F32),
             jax.ShapeDtypeStruct((seq, 2 * HEAD_DIM), F32),
             jax.ShapeDtypeStruct((rows, 2 * left.shape[1]), BF),
+            flat,
+            flat,
         ),
-        in_specs=[vmem] * 7,
-        out_specs=(vmem, vmem, vmem),
+        in_specs=[vmem] * 11,
+        out_specs=(vmem,) * 5,
         scratch_shapes=[
             pltpu.VMEM((heads, rows, 128), BF),
             pltpu.VMEM((heads, rows, 128), BF),
             pltpu.VMEM((heads, rows, 128), F32),
             pltpu.VMEM((heads, 1, rows), F32),
+            pltpu.VMEM(flat.shape, BF),
+            pltpu.VMEM(flat.shape, BF),
+            pltpu.VMEM((n_far,) + flat.shape, BF),
+            pltpu.SemaphoreType.DMA((2,)),
+            pltpu.SemaphoreType.DMA((2,)),
+            pltpu.SemaphoreType.DMA((n_far,)),
+            pltpu.SemaphoreType.DMA((n_far,)),
         ]
         + line_scratch(rows, 2 * left.shape[1]),
         compiler_params=pltpu.CompilerParams(collective_id=collective_id, has_side_effects=True),
         cost_estimate=cost,
         name="attend_backward",
-    )(queries, grads, attended, lse, pair, left, right)
+    )(queries, grads, attended, lse, pair, left, right, *parts)
 
 
 def partners(n_ctx):
@@ -447,70 +543,6 @@
             copy.wait_send()
 
     return finish
-
-
-def scatter_kernel(n_ctx, part_ref, o_ref, work, land, send, recv):
-    rows = o_ref.shape[0]
-    x = lax.axis_index("fsdp")
-    ctx = lax.axis_index("ctx")
-    barrier = greet(n_ctx)
-    work[...] = part_ref[...].astype(BF)
-    pl.semaphore_wait(barrier, len(partners(n_ctx)))
-    copies = []
-    used = [0]
-
-    def give(start, size, axis, bit):
-        e = len(copies)
-        cut = pl.ds(pl.multiple_of(start, rows), size)
-        copy = pltpu.make_async_remote_copy(
-            src_ref=work.at[cut],
-            dst_ref=land.at[pl.ds(used[0], size)],
-            send_sem=send.at[e],
-            recv_sem=recv.at[e],
-            device_id={axis: lax.axis_index(axis) ^ bit},
-            device_id_type=MESH,
-        )
-        copy.start()
-        copies.append(copy)
-        used[0] += size
-        return copy, used[0] - size
-
-    def take(start, size, at):
-        cut = pl.ds(pl.multiple_of(start, rows), size)
-        work[cut, :] = (work[cut, :].astype(F32) + land[at : at + size, :].astype(F32)).astype(BF)
-
-    bits = high_bits(n_ctx)
-    for j in range(len(bits)):
-        bit = bits[len(bits) - 1 - j]
-        masks = masks_of(bits[: len(bits) - 1 - j])
-        now = [give((ctx ^ bit ^ m) * 2 * rows, 2 * rows, "ctx", bit) for m in masks]
-        for (copy, at), m in zip(now, masks):
-            copy.wait_recv()
-            take((ctx ^ m) * 2 * rows, 2 * rows, at)
-    copy, at = give((ctx * 2 + 1 - x) * rows, rows, "fsdp", 1)
-    copy.wait_recv()
-    mine = pl.ds(pl.multiple_of((ctx * 2 + x) * rows, rows), rows)
-    o_ref[...] = work[mine, :].astype(F32) + land[at : at + rows, :].astype(F32)
-    for copy in copies:
-        copy.wait_send()
-
-
-def scatter_pairs(part, rows, n_ctx, collective_id):
-    vmem = pl.BlockSpec(memory_space=pltpu.VMEM)
-    return pl.pallas_call(
-        functools.partial(scatter_kernel, n_ctx),
-        out_shape=jax.ShapeDtypeStruct((rows, part.shape[1]), F32),
-        in_specs=[vmem],
-        out_specs=vmem,
-        scratch_shapes=[
-            pltpu.VMEM(part.shape, BF),
-            pltpu.VMEM(part.shape, BF),
-            pltpu.SemaphoreType.DMA((n_ctx,)),
-            pltpu.SemaphoreType.DMA((n_ctx,)),
-        ],
-        compiler_params=pltpu.CompilerParams(collective_id=collective_id, has_side_effects=True),
-        name="scatter_pairs",
-    )(part)
 
 
 def project_kernel(
@@ -809,33 +841,302 @@
     return [pltpu.VMEM((rows, width // 2), BF)] * 4 + [pltpu.SemaphoreType.DMA((CHUNKS,))] * 8
 
 
-def head_sum_kernel(n, left_ref, right_ref, o_ref, work_l, work_r, from_lo, from_hi, *sems):
-    barrier = line_greet(n)
-    pl.semaphore_wait(barrier, line_peers(n))
-    step, steps, drain = line_sum(n, left_ref, right_ref, work_l, work_r, o_ref, from_lo, from_hi, sems)
+def last_kernel(
+    n_ctx,
+    n_head,
+    dq_ref,
+    part_ref,
+    cos_ref,
+    sin_ref,
+    w_l,
+    w_r,
+    n_ref,
+    att_ref,
+    low_ref,
+    up_ref,
+    gate_ref,
+    down_ref,
+    sum_ref,
+    qkv_full,
+    out_full,
+    gate_full,
+    up_full,
+    down_full,
+    work,
+    land,
+    raw,
+    raw_land,
+    n_land,
+    low_land,
+    att_land,
+    up_sum,
+    out_sent,
+    out_kept,
+    out_land,
+    qkv_sent,
+    qkv_kept,
+    qkv_land,
+    up_far,
+    out_far,
+    qkv_far,
+    pair_send,
+    pair_recv,
+    trade_send,
+    trade_recv,
+    cross_send,
+    cross_recv,
+    far_send,
+    far_recv,
+    full_send,
+    full_recv,
+    full_local,
+    left,
+    right,
+    from_lo,
+    from_hi,
+    *sems,
+):
+    rows, q_width = dq_ref.shape
+    half = n_ref.shape[1] // 2
+    quarter = half // 2
+    x_at = lax.axis_index("fsdp")
+    ctx = lax.axis_index("ctx")
+    core = lax.rem(ctx, 2)
+    barrier = line_greet(n_head)
+    greet(n_ctx)
+    work[...] = part_ref[...].astype(BF)
+    up_sum[...] = up_ref[...]
+    pl.semaphore_wait(barrier, line_peers(n_head) + len(partners(n_ctx)))
+
+    def relative(side, c):
+        return pl.ds(pl.multiple_of(side * half + c * quarter, quarter), quarter)
+
+    def trade(src, dst, at):
+        return exchange(src, dst, "ctx", 1, trade_send.at[at], trade_recv.at[at])
+
+    pairs = []
+    used = [0]
+
+    def give(start, size, axis, bit):
+        e = len(pairs)
+        cut = pl.ds(pl.multiple_of(start, rows), size)
+        copy = exchange(
+            work.at[cut], land.at[pl.ds(used[0], size)], axis, bit, pair_send.at[e], pair_recv.at[e]
+        )
+        copy.start()
+        pairs.append(copy)
+        used[0] += size
+        return copy, used[0] - size
+
+    def take(start, size, at):
+        cut = pl.ds(pl.multiple_of(start, rows), size)
+        work[cut, :] = (work[cut, :].astype(F32) + land[at : at + size, :].astype(F32)).astype(BF)
+
+    up_chain = Chain(n_ctx, up_sum, up_far, far_send.at[0], far_recv.at[0])
+    out_chain = Chain(n_ctx, out_kept, out_far, far_send.at[1], far_recv.at[1])
+    qkv_chain = Chain(n_ctx, qkv_kept, qkv_far, far_send.at[2], far_recv.at[2])
+
+    def turned(wide, cut):
+        low = lax.rem(lanes(wide.shape), HEAD_DIM) < HEAD_DIM // 2
+        swapped = jnp.where(low, pltpu.roll(wide, 128 - HEAD_DIM // 2, 1), pltpu.roll(wide, HEAD_DIM // 2, 1))
+        return wide * cos_ref[cut, :] - swapped * sin_ref[cut, :]
+
+    def rotate_rows(i, carry):
+        cut = pl.ds(pl.multiple_of(i * 128, 128), 128)
+        for j in range(q_width // 128):
+            sl = slice(j * 128, (j + 1) * 128)
+            raw[cut, sl] = turned(dq_ref[cut, sl] * 0.125, cut).astype(BF)
+        return carry
+
+    bits = high_bits(n_ctx)
+    trades = []
+    for j in range(len(bits)):
+        bit = bits[len(bits) - 1 - j]
+        masks = masks_of(bits[: len(bits) - 1 - j])
+        now = [give((ctx ^ bit ^ m) * 2 * rows, 2 * rows, "ctx", bit) for m in masks]
+        if j == 0:
+            lax.fori_loop(0, rows // 128, rotate_rows, 0)
+        for (copy, at), m in zip(now, masks):
+            copy.wait_recv()
+            take((ctx ^ m) * 2 * rows, 2 * rows, at)
+    copy, at = give((ctx * 2 + 1 - x_at) * rows, rows, "fsdp", 1)
+    up_chain.start()
+    trades = [trade(att_ref, att_land, 0)]
+    for side in range(2):
+        trades.append(trade(low_ref.at[:, relative(side, 1 - core)], low_land.at[:, pl.ds(side * quarter, quarter)], 1 + side))
+        trades.append(trade(n_ref.at[:, relative(side, 1 - core)], n_land.at[:, pl.ds(side * quarter, quarter)], 3 + side))
+    for t in trades:
+        t.start()
+    copy.wait_recv()
+    base = pl.multiple_of((ctx * 2 + x_at) * rows, rows)
+
+    def finish_pair(i, carry):
+        cut = pl.ds(pl.multiple_of(i * 128, 128), 128)
+        mine = work[pl.ds(base + i * 128, 128), :].astype(F32) + land[pl.ds(at + i * 128, 128), :].astype(F32)
+        raw[cut, q_width:] = jnp.where(lanes(mine.shape) < HEAD_DIM, turned(mine, cut), mine).astype(BF)
+        left[cut, :] = mat_trans(raw[cut, :], w_l[...]).astype(BF)
+        right[cut, :] = mat_trans(raw[cut, :], w_r[...]).astype(BF)
+        return carry
+
+    lax.fori_loop(0, rows // 128, finish_pair, 0)
+    raw_trade = trade(raw, raw_land, 5)
+    raw_trade.start()
+    trades.append(raw_trade)
+    step, steps, drain = line_sum(n_head, left, right, left, right, sum_ref, from_lo, from_hi, sems)
 
     def run(s, carry):
         step(s)
         return carry
 
-    lax.fori_loop(0, steps, run, 0)
+    def spread(src, whole, by_rows, e):
+        size = src.shape[0 if by_rows else 1]
+        cut = pl.ds(pl.multiple_of(core * size, size), size)
+        dst = whole.at[cut] if by_rows else whole.at[:, cut]
+        return (
+            pltpu.make_async_copy(src, dst, full_local.at[e]),
+            exchange(src, dst, "ctx", 1, full_send.at[e], full_recv.at[e]),
+        )
+
+    spreads = [spread(gate_ref, gate_full, True, 0), spread(down_ref, down_full, False, 1)]
+    for pair in spreads:
+        for copy in pair:
+            copy.start()
+
+    def out_tiles(dst, side):
+        def one(t, carry):
+            cut = pl.ds(pl.multiple_of(t * 128, 128), 128)
+            dst[cut, :] = (
+                trans_mat(att_ref[:, cut], low_ref[:, relative(side, core)])
+                + trans_mat(att_land[:, cut], low_land[:, side * quarter : (side + 1) * quarter])
+            ).astype(BF)
+            step(steps_at + t)
+            return carry
+
+        lax.fori_loop(0, q_width // 128, one, 0)
+
+    def qkv_tiles(dst, side):
+        def one(t, carry):
+            cut = pl.ds(pl.multiple_of(t * 128, 128), 128)
+            there = pl.ds(pl.multiple_of(side * half + core * quarter + t * 128, 128), 128)
+            landing = pl.ds(pl.multiple_of(side * quarter + t * 128, 128), 128)
+            dst[cut, :] = (
+                trans_mat(n_ref[:, there], raw[...]) + trans_mat(n_land[:, landing], raw_land[...])
+            ).astype(BF)
+            step(steps_at + t)
+            return carry
+
+        lax.fori_loop(0, quarter // 128, one, 0)
+
+    lax.fori_loop(0, 2, run, 0)
+    for t in trades:
+        t.wait_recv()
+    steps_at = 2
+    out_tiles(out_sent, 1)
+    out_cross = exchange(out_sent, out_land, "fsdp", 1, cross_send.at[0], cross_recv.at[0])
+    out_cross.start()
+    steps_at += q_width // 128
+    qkv_tiles(qkv_sent, 1)
+    qkv_cross = exchange(qkv_sent, qkv_land, "fsdp", 1, cross_send.at[1], cross_recv.at[1])
+    qkv_cross.start()
+    steps_at += quarter // 128
+    out_tiles(out_kept, 0)
+    steps_at += q_width // 128
+    qkv_tiles(qkv_kept, 0)
+    steps_at += quarter // 128
+    out_cross.wait_recv()
+    add_into(out_kept, out_kept, out_land)
+    out_chain.start()
+    rest = steps - steps_at
+    lax.fori_loop(steps_at, steps_at + rest // 4, run, 0)
+    qkv_cross.wait_recv()
+    add_into(qkv_kept, qkv_kept, qkv_land)
+    qkv_chain.start()
+    lax.fori_loop(steps_at + rest // 4, steps_at + rest // 2, run, 0)
+    up_chain.finish()
+    spreads.append(spread(up_sum, up_full, True, 2))
+    for copy in spreads[-1]:
+        copy.start()
+    lax.fori_loop(steps_at + rest // 2, steps, run, 0)
+    out_chain.finish()
+    spreads.append(spread(out_kept, out_full, False, 3))
+    for copy in spreads[-1]:
+        copy.start()
+    qkv_chain.finish()
+    spreads.append(spread(qkv_kept, qkv_full, True, 4))
+    for copy in spreads[-1]:
+        copy.start()
     drain()
-
-
-def head_sum(left, right, n, collective_id):
-    rows, cols = left.shape
+    for t in pairs + trades + [out_cross, qkv_cross]:
+        t.wait_send()
+    for local, remote in spreads:
+        local.wait()
+        remote.wait()
+
+
+def last_sum(
+    dq, part, cosine, sine, w_left, w_right, normed, attended, low, up, gate, down, n_ctx, n_head, collective_id
+):
+    rows, q_width = dq.shape
+    width = normed.shape[1]
+    half = width // 2
+    quarter = half // 2
+    narrow = w_left.shape[1]
+    units = gate.shape[1]
+    n_far = len(high_bits(n_ctx)) - 1
+    vmem = pl.BlockSpec(memory_space=pltpu.VMEM)
+    anywhere = pl.BlockSpec(memory_space=pl.ANY)
+    dma = pltpu.SemaphoreType.DMA
     return pl.pallas_call(
-        functools.partial(head_sum_kernel, n),
-        out_shape=jax.ShapeDtypeStruct((rows, 2 * cols), BF),
-        in_specs=[pl.BlockSpec(memory_space=pltpu.VMEM)] * 2,
-        out_specs=pl.BlockSpec(memory_space=pltpu.VMEM),
-        scratch_shapes=line_scratch(rows, 2 * cols),
-        compiler_params=pltpu.CompilerParams(collective_id=collective_id, has_side_effects=True),
+        functools.partial(last_kernel, n_ctx, n_head),
+        out_shape=(
+            jax.ShapeDtypeStruct((rows, width), BF),
+            jax.ShapeDtypeStruct((half, narrow), BF),
+            jax.ShapeDtypeStruct((q_width, half), BF),
+            jax.ShapeDtypeStruct((half, units), BF),
+            jax.ShapeDtypeStruct((half, units), BF),
+            jax.ShapeDtypeStruct((units, half), BF),
+        ),
+        in_specs=[vmem] * 12,
+        out_specs=(vmem,) + (anywhere,) * 5,
+        scratch_shapes=[
+            pltpu.VMEM(part.shape, BF),
+            pltpu.VMEM(part.shape, BF),
+            pltpu.VMEM((rows, narrow), BF),
+            pltpu.VMEM((rows, narrow), BF),
+            pltpu.VMEM((rows, half), BF),
+            pltpu.VMEM((rows, half), BF),
+            pltpu.VMEM((rows, q_width), BF),
+            pltpu.VMEM(up.shape, BF),
+            pltpu.VMEM((q_width, quarter), BF),
+            pltpu.VMEM((q_width, quarter), BF),
+            pltpu.VMEM((q_width, quarter), BF),
+            pltpu.VMEM((quarter, narrow), BF),
+            pltpu.VMEM((quarter, narrow), BF),
+            pltpu.VMEM((quarter, narrow), BF),
+            pltpu.VMEM((n_far,) + up.shape, BF),
+            pltpu.VMEM((n_far, q_width, quarter), BF),
+            pltpu.VMEM((n_far, quarter, narrow), BF),
+            dma((n_ctx,)),
+            dma((n_ctx,)),
+            dma((6,)),
+            dma((6,)),
+            dma((2,)),
+            dma((2,)),
+            dma((3, n_far)),
+            dma((3, n_far)),
+            dma((5,)),
+            dma((5,)),
+            dma((5,)),
+        ]
+        + line_scratch(rows, width),
+        compiler_params=pltpu.CompilerParams(
+            collective_id=collective_id, has_side_effects=True, vmem_limit_bytes=66_000_000
+        ),
         cost_estimate=pl.CostEstimate(
-            flops=40_000_000_000, bytes_accessed=8 * rows * cols, transcendentals=0
+            flops=50_000_000_000, bytes_accessed=8 * rows * width, transcendentals=0
         ),
-        name="head_sum",
-    )(left, right)
+        name="last_sum",
+    )(dq, part, cosine, sine, w_left, w_right, normed, attended, low, up, gate, down)
 
 
 def ffn_kernel(
@@ -1138,7 +1439,6 @@
 ):
     rows, width = inputs.shape
     half = width // 2
-    quarter = half // 2
     x_at = lax.axis_index("fsdp")
     ctx_at = lax.axis_index("ctx")
     core = lax.rem(ctx_at, 2)
@@ -1150,18 +1450,6 @@
         return jnp.where(x_at == 0, array, swapped)
 
     every = high_bits(n_ctx)
-
-    def columns_of(array, which):
-        first = jnp.concatenate([array[:, :quarter], array[:, half : half + quarter]], axis=1)
-        second = jnp.concatenate([array[:, quarter:half], array[:, half + quarter :]], axis=1)
-        return jnp.where(which == 0, first, second)
-
-    def trade(array):
-        return jnp.concatenate([array, flip(array, "ctx", 1, n_ctx)], axis=0)
-
-    def trade_columns(array):
-        got = flip(columns_of(array, 1 - core), "ctx", 1, n_ctx)
-        return jnp.concatenate([columns_of(array, core), got], axis=0)
 
     q_width = query_weight.shape[1]
     half_dim = HEAD_DIM // 2
@@ -1206,7 +1494,6 @@
     hidden = in_float + mixed.astype(F32)
     scale_two = lax.rsqrt(jnp.mean(hidden * hidden, axis=-1, keepdims=True) + EPSILON)
     unit_two = hidden * scale_two
-    one_pair = trade_columns(normed_one)
     scaled_two = normed_two_grad * gain_two
     gain_two_part = jnp.sum(normed_two_grad * unit_two, axis=0)
     hidden_grad = cot.astype(F32) + scale_two * (
@@ -1217,30 +1504,41 @@
     attended_grad = (
         mat_trans(hidden_low[:, :half], output_weight) + mat_trans(hidden_low[:, half:], out_other)
     ).astype(BF)
-    out_part = trans_mat(trade(attended), trade_columns(hidden_low)).astype(BF)
-    attended_grad, out_part = lax.optimization_barrier((attended_grad, out_part))
-    query_acc, pair_acc, ffn_out = attend_back(
-        queries, attended_grad, attended, lse, pair, down_left, down_right, n_head, 6
+    down_far = down_kept
+    for bit in every[:-1]:
+        down_far = (down_far.astype(F32) + flip(down_far, "ctx", bit, n_ctx).astype(F32)).astype(BF)
+    query_acc, pair_acc, ffn_out, gate_far, up_kept = attend_back(
+        queries,
+        attended_grad,
+        attended,
+        lse,
+        pair,
+        down_left,
+        down_right,
+        (gate_sent, gate_kept, up_sent, up_kept),
+        n_ctx,
+        n_head,
+        6,
     )
     outputs = own_first((hidden + ffn_out.astype(F32)).astype(BF))
-    pair_mine = scatter_pairs(pair_acc, rows, n_ctx, 5)
-
-    def unrotate(values):
-        count = values.shape[1] // 128
-        cos = jnp.concatenate([cosine] * count, axis=1)
-        sin = jnp.concatenate([signed] * count, axis=1)
-        low = lax.broadcasted_iota(jnp.int32, values.shape, 1) % HEAD_DIM < half_dim
-        turned = jnp.where(low, jnp.roll(values, -half_dim, axis=1), jnp.roll(values, half_dim, axis=1))
-        return values * cos - turned * sin
-
-    q_raw = unrotate(query_acc * 0.125)
-    pair_raw = jnp.where(lane < HEAD_DIM, unrotate(pair_mine), pair_mine)
-    qkv_raw = jnp.concatenate([q_raw, pair_raw], axis=1).astype(BF)
-    last_left = mat_trans(qkv_raw, qkv_local).astype(BF)
-    last_right = mat_trans(qkv_raw, qkv_other).astype(BF)
-    qkv_part = trans_mat(one_pair, trade(qkv_raw)).astype(BF)
-    last_left, last_right, qkv_part = lax.optimization_barrier((last_left, last_right, qkv_part))
-    normed_one_grad = head_sum(last_left, last_right, n_head, 3).astype(F32)
+    last, qkv_full, out_full, gate_full, up_full, down_full = last_sum(
+        query_acc,
+        pair_acc,
+        cosine,
+        signed,
+        qkv_local,
+        qkv_other,
+        normed_one,
+        attended,
+        hidden_low,
+        up_kept,
+        gate_far,
+        down_far,
+        n_ctx,
+        n_head,
+        3,
+    )
+    normed_one_grad = last.astype(F32)
     gain_one_part = jnp.sum(normed_one_grad * unit_one, axis=0)
     scaled_one = normed_one_grad * gain_one
     input_grad = own_first(
@@ -1249,27 +1547,9 @@
         * (scaled_one - unit_one * jnp.mean(scaled_one * unit_one, axis=-1, keepdims=True))
     )
 
-    def total(kept, sent):
-        if sent is not None:
-            kept = (kept.astype(F32) + flip(sent, "fsdp", 1, 2).astype(F32)).astype(BF)
-        for bit in every[:-1]:
-            kept = (kept.astype(F32) + flip(kept, "ctx", bit, n_ctx).astype(F32)).astype(BF)
-        return kept
-
-    def spread(kept, dim):
-        got = flip(kept, "ctx", 1, n_ctx)
-        first = jnp.where(core == 0, kept, got)
-        second = jnp.where(core == 0, got, kept)
-        return jnp.concatenate([first, second], axis=dim).astype(F32)
-
-    down_grad = spread(total(down_kept, None), 1)
-    gate_grad = spread(total(gate_kept, gate_sent), 0)
-    up_grad = spread(total(up_kept, up_sent), 0)
-    output_grad = spread(total(out_part[:, :quarter], out_part[:, quarter:]), 1)
-    qkv_grad = spread(total(qkv_part[:quarter], qkv_part[quarter:]), 0)
-    query_grad = qkv_grad[:, :q_width]
-    key_grad = qkv_grad[:, q_width : q_width + HEAD_DIM]
-    value_grad = qkv_grad[:, q_width + HEAD_DIM :]
+    query_grad = qkv_full[:, :q_width].astype(F32)
+    key_grad = qkv_full[:, q_width : q_width + HEAD_DIM].astype(F32)
+    value_grad = qkv_full[:, q_width + HEAD_DIM :].astype(F32)
 
     gain_parts = jnp.stack([gain_one_part, gain_two_part])
     gain_kept = gain_parts[:, :half] + flip(gain_parts[:, half:], "fsdp", 1, 2)
@@ -1282,10 +1562,10 @@
         query_grad,
         key_grad,
         value_grad,
-        output_grad,
-        gate_grad,
-        up_grad,
-        down_grad,
+        out_full.astype(F32),
+        gate_full.astype(F32),
+        up_full.astype(F32),
+        down_full.astype(F32),
         gain_kept[0],
         gain_kept[1],
     )

time: 518 us -> 471 us (0.909)
  waiting for transfers between devices: 26 us -> 0.84 us
  Pallas kernels: 375 us -> 397 us
  other arithmetic: 62.9 us -> 43.4 us
  matrix products: 12.6 us -> 2.33 us
  starting transfers between devices: 11.3 us -> 4.49 us
  local copies, waits for them, and re-layouts: 21.1 us -> 14.8 us
    ppermute x21 -> x4, waiting for transfers between devices: 26 us -> 0.84 us  [flip(): return lax.ppermute(array, axis, [(i, i ^ bit) for i in range(size)])]
    pallas_call x3 -> x2, Pallas kernels: 155 us -> 168 us  [the longest x1 90 us: last_sum(): pl.pallas_call(functools.partial(last_kernel, n_ctx, n_head), out_shape=(...]
    convert_element_type x14 -> x7, other arithmetic: 26.8 us -> 14.6 us  [the longest x1 3.25 us: shards(): down_full.astype(F32)]
    pallas_call x1, Pallas kernels: 90.3 us -> 99.8 us  [ffn_sum(): pl.pallas_call(functools.partial(ffn_kernel, n_head), out_shape=(wide, wi...]
    select_n x7 -> x0, other arithmetic: 7.84 us -> none  [the longest x2 4.03 us: columns_of(): return jnp.where(which == 0, first, second)]
    ppermute x21 -> x4, starting transfers between devices: 11.3 us -> 4.49 us  [flip(): return lax.ppermute(array, axis, [(i, i ^ bit) for i in range(size)])]
    dot_general x2 -> x0, matrix products: 6.38 us -> none  [trans_mat(): lax.dot_general(left, right, (((0,), (0,)), ((), ())), preferred_element_...]
    slice x9 -> x0, local copies, waits for them, and re-layouts: 6.14 us -> none  [the longest x4 2.9 us: unrotate(): jnp.roll(values, half_dim, axis=1)]
  transfers between devices with their start and end apart: 21 -> 4, of which waited for: 4 -> 1; matrix products, arithmetic and copies ran while one was open for 13% -> 9% of each run, Pallas kernels for 30% -> 17%
where the time goes in v4:
time: 471 us; the launch traced here: 464 us
  Pallas kernels  397 us (84%)
  other arithmetic  43.4 us (9%)
  local copies, waits for them, and re-layouts  14.8 us (3%)
    pallas_call x1, Pallas kernels, ffn_sum(): pl.pallas_call(functools.partial(ffn_kernel, n_head), out_shape=(wide, wi...  99.8 us
    pallas_call x1, Pallas kernels, last_sum(): pl.pallas_call(functools.partial(last_kernel, n_ctx, n_head), out_shape=(...  90 us
    pallas_call x1, Pallas kernels, attend_sum(): pl.pallas_call(functools.partial(forward_kernel, n_ctx, n_head, span), ou...  77.7 us
    pallas_call x1, Pallas kernels, attend_back(): pl.pallas_call(functools.partial(backward_kernel, n_ctx, n_head, group, s...  77.7 us
    pallas_call x1, Pallas kernels, project(): pl.pallas_call(functools.partial(project_kernel, n_ctx), out_shape=(jax.S...  51.7 us
  transfers between devices with their start and end apart: 4, of which 1 were waited for; matrix products, arithmetic and copies ran while one was open for 9% of the time, Pallas kernels for 17%

profile of v4, /device:TPU:0, one launch (start us, length us, event | category | flops | bytes accessed | tf_op | source)
XLA Modules:
  0.0 464.1 jit_solution(9043458218081497327)
XLA Ops:
  0.7 0.7 broadcast_in_dim.6
  1.4 0.7 broadcast_in_dim.7
  2.1 1.1 copy.23
  3.1 1.1 copy.24
  4.3 0.7 maximum_convert_fusion.gain_ref
  5.0 2.5 pad_maximum_fusion.w_ref.w_l
  7.5 1.8 negate_select_fusion
  9.3 51.7 %project.1 = (bf16[512,512]{1,0:T(8,128)(2,1)}, bf16[4096,128]{1,0:T(8,128)(2,1)}, bf16[512,2048]{1,0:T(8,128)(2,1)}, bf16[1024,640]{1,0:T(8,128)(2,1)}, f32[8,1...) custom-call(bf16[512,2048]{1,0:T(8,128)(2,1)} %x_ref.3, ...), custom_call_target="tpu_custom_call" | custom-call | tf_op jit(solution)/shard_map/project/pallas_call | solution.py:678
  61.0 77.7 %attend_sum.1 = (bf16[512,512]{1,0:T(8,128)(2,1)}, f32[8,1,512]{2,1,0:T(1,128)}, bf16[512,2048]{1,0:T(8,128)(2,1)}, bf16[1024,1408]{1,0:T(8,128)(2,1)}, bf16[102...) custom-call(bf16[512,512]{1,0:T(8,128)(2,1)} %get-tuple-element.47.q_ref, ...), custom_call_target="tpu_custom_call", output_to_operand_aliasing={{5}: (6, {})} | custom-call | flops 49999998976 | bytes 8388608 | tf_op jit(solution)/shard_map/attend_sum/pallas_call | solution.py:278
  138.7 99.8 %ffn_sum.1 = (bf16[512,2048]{1,0:T(8,128)(2,1)}, bf16[512,2048]{1,0:T(8,128)(2,1)}, bf16[512,1024]{1,0:T(8,128)(2,1)}, bf16[512,1024]{1,0:T(8,128)(2,1)}, bf16[1...) custom-call(bf16[512,2048]{1,0:T(8,128)(2,1)} %x_ref.3, ...), custom_call_target="tpu_custom_call" | custom-call | flops 49999998976 | bytes 8388608 | tf_op jit(solution)/shard_map/ffn_sum/pallas_call | solution.py:1393
  238.5 1.4 collective-permute-start
  239.9 1.4 fusion.28
  241.3 1.4 fusion.29
  242.7 1.9 fusion.27
  244.6 0.3 copy-done.5
  244.9 1.3 multiply_reduce_fusion
  246.3 0.2 copy-done.4
  246.5 2.6 fusion.11
  249.1 0.2 fusion.26
  249.4 2.9 fusion.23.low_ref
  252.3 0.8 fusion.18
  253.1 1.2 copy-done.26
  254.3 1.6 fusion.16.g_ref
  255.9 77.7 %attend_backward.1 = (f32[512,512]{1,0:T(8,128)}, f32[4096,128]{1,0:T(8,128)}, bf16[512,2048]{1,0:T(8,128)(2,1)}, bf16[512,1408]{1,0:T(8,128)(2,1)}, bf16[512,1408]{1,0:T(8,128)(2,1)}) custom-call(bf16[512,512]{1,0:T(8,128)(2,1)} %get-tuple-element.47.q_ref, bf16[512,512]{1,0:T(8,128)(2,1)} %fusion.16.g_ref, ...), custom_call_target="tpu_custom_call" | custom-call | flops 34359738368 | bytes 2097152 | tf_op jit(solution)/shard_map/attend_backward/pallas_call | solution.py:461
  333.6 0.6 pad_maximum_fusion.3
  334.2 0.6 add_rsqrt_fusion
  334.8 1.5 add_convert_fusion.1.down_ref
  336.3 90.0 %last_sum.1 = (bf16[512,2048]{1,0:T(8,128)(2,1)}, bf16[1024,640]{1,0:T(8,128)(2,1)}, bf16[512,1024]{1,0:T(8,128)(2,1)}, bf16[1024,1408]{1,0:T(8,128)(2,1)}, bf16...) custom-call(f32[512,512]{1,0:T(8,128)} %get-tuple-element.68.dq_ref, f32[4096,128]{1,0:T(8,128)} %get-tuple-element.69.part_ref, ...), custom_call_target="tpu_custom_call" | custom-call | flops 49999998976 | bytes 8388608 | tf_op jit(solution)/shard_map/last_sum/pallas_call | solution.py:1089
  426.3 3.7 fusion.13
  430.0 1.8 collective-permute-start.1
  431.8 6.8 %fusion.7 = (f32[512,2048]{1,0:T(8,128)S(1)}, bf16[512,2048]{1,0:T(8,128)(2,1)S(1)}) fusion(bf16[512,2048]{1,0:T(8,128)(2,1)} %get-tuple-element.75, bf16[512,2048]{1,0:T(8,128)(2,1)S(1)} %copy-done.1, f32[512]{0:T(512)S(1)} %broadcast_multiply_fusion, f32[2048]{0:T(1024)S(1)} %copy-done.17, f32[512]{0:T(512)S(1)} %copy-done.20, f32[512]{0:T(512)S(1)} %copy-done.22, ...), kind=kLoop, calls=%fused_computation.13 | loop fusion | flops 27262976 | bytes 20996096 | tf_op jit(solution)/shard_map/add | solution.py:1545
  438.6 0.2 fusion.25
  438.9 0.6 fusion.24
  439.4 3.1 maximum_select_fusion
  442.6 2.2 maximum_select_fusion.3
  444.7 1.3 collective-permute-start.2
  446.0 1.6 slice_convert_fusion
  447.6 0.8 collective-permute-done.2
  448.6 0.9 slice_convert_fusion.1
  449.5 1.6 convert_element_type.88
  451.1 1.9 copy.26
  453.0 0.9 copy.25
  453.9 2.9 convert_element_type.89
  456.8 0.1 copy-done.10
  456.9 2.9 convert_element_type.90
  459.8 0.1 copy-done.9
  459.9 3.2 convert_element_type.91
  463.1 0.6 fusion.30
  (67 shorter events, 0.3 us)
Async XLA Ops:
  238.5 6.1 %copy-start.2 = (bf16[512,2048]{1,0:T(8,128)(2,1)S(1)}, bf16[512,2048]{1,0:T(8,128)(2,1)}, u32[]{:S(2)}) copy-start(bf16[512,2048]{1,0:T(8,128)(2,1)} %get-tuple-element.51.mix_ref) | copy-start | bytes 6291460
  238.5 96.3 %collective-permute-start = (bf16[1408,512]{1,0:T(8,128)(2,1)}, bf16[1408,512]{1,0:T(8,128)(2,1)S(1)}, u32[]{:S(2)}, u32[]{:S(2)}) collective-permute-start(bf16[1408,512]{1,0:T(8,128)(2,1)} %get-tuple-element.74), channel_id=1, source_target_pairs={{0,16},{8,24},{16,0},{24,8},{1,17},{9,25},{17,1},{25,9},{2,18},{10... | collective-permute-start | bytes 4325384 | tf_op jit(solution)/shard_map/ppermute | solution.py:1422
  242.7 2.2 copy-start.5
  244.9 1.6 copy-start.4
  246.2 3.1 copy-start
  246.3 3.1 copy-start.18
  246.5 2.6 copy-start.6
  249.1 3.1 copy-start.21
  249.3 2.9 copy-start.7
  249.3 2.9 copy-start.8
  249.4 2.9 copy-start.15
  252.3 3.6 copy-start.12
  252.3 2.0 copy-start.26
  255.9 77.7 %copy-start.23 = (f32[1,1024]{1,0:T(1,128)S(1)}, f32[1,1024]{1,0:T(1,128)}, u32[]{:S(2)}) copy-start(f32[1,1024]{1,0:T(1,128)} %get-tuple-element.111) | copy-start | bytes 12292
  255.9 77.7 %copy-start.24 = (f32[1,1024]{1,0:T(1,128)S(1)}, f32[1,1024]{1,0:T(1,128)}, u32[]{:S(2)}) copy-start(f32[1,1024]{1,0:T(1,128)} %get-tuple-element.113) | copy-start | bytes 12292
  255.9 78.3 %copy-start.25 = (f32[512]{0:T(512)S(1)}, f32[512]{0:T(512)}, u32[]{:S(2)}) copy-start(f32[512]{0:T(512)} %get-tuple-element.96) | copy-start | bytes 6148
  255.9 78.9 %copy-start.14 = (bf16[1408,512]{1,0:T(8,128)(2,1)S(1)}, bf16[1408,512]{1,0:T(8,128)(2,1)}, u32[]{:S(2)}) copy-start(bf16[1408,512]{1,0:T(8,128)(2,1)} %get-tuple-element.74) | copy-start | bytes 4325380
  336.2 90.0 %copy-start.17 = (f32[2048]{0:T(1024)S(1)}, f32[2048]{0:T(1024)}, u32[]{:S(2)}) copy-start(f32[2048]{0:T(1024)} %pad_maximum_fusion.3) | copy-start | bytes 24580
  336.3 90.1 %copy-start.20 = (f32[512]{0:T(512)S(1)}, f32[512]{0:T(512)}, u32[]{:S(2)}) copy-start(f32[512]{0:T(512)} %add_rsqrt_fusion) | copy-start | bytes 6148
  426.3 5.6 %copy-start.1 = (bf16[512,2048]{1,0:T(8,128)(2,1)S(1)}, bf16[512,2048]{1,0:T(8,128)(2,1)}, u32[]{:S(2)}) copy-start(bf16[512,2048]{1,0:T(8,128)(2,1)} %copy-done) | copy-start | bytes 6291460
  426.3 5.5 %copy-start.3 = (bf16[512,2048]{1,0:T(8,128)(2,1)S(1)}, bf16[512,2048]{1,0:T(8,128)(2,1)}, u32[]{:S(2)}) copy-start(bf16[512,2048]{1,0:T(8,128)(2,1)} %get-tuple-element.51.mix_ref) | copy-start | bytes 6291460
  426.3 5.5 %copy-start.19 = (f32[512]{0:T(512)S(1)}, f32[512]{0:T(512)}, u32[]{:S(2)}) copy-start(f32[512]{0:T(512)} %copy-done.18) | copy-start | bytes 6148
  426.3 5.5 %copy-start.22 = (f32[512]{0:T(512)S(1)}, f32[512]{0:T(512)}, u32[]{:S(2)}) copy-start(f32[512]{0:T(512)} %copy-done.21) | copy-start | bytes 6148
  430.0 14.7 %collective-permute-start.1 = (f32[2,1024]{1,0:T(2,128)S(1)}, f32[2,1024]{1,0:T(2,128)S(1)}, u32[]{:S(2)}, u32[]{:S(2)}) collective-permute-start(f32[2,1024]{1,0:T(2,128)S(1)} %pad_maximum_fusion.1), channel_id=1, source_target_pairs={{0,4},{4,0},{1,5},{5,1},{2,6},{6,2},{3,7},{7,3},{8,12},{12,8},{9,1... | collective-permute-start | bytes 24584 | tf_op jit(solution)/shard_map/ppermute | solution.py:1422
  442.6 3.5 copy-start.13
  444.7 4.8 %copy-start.16 = (bf16[512,1024]{1,0:T(8,128)(2,1)S(1)}, bf16[512,1024]{1,0:T(8,128)(2,1)}, u32[]{:S(2)}) copy-start(bf16[512,1024]{1,0:T(8,128)(2,1)} %get-tuple-element.77) | copy-start | bytes 3145732
  444.7 3.7 collective-permute-start.2
  448.5 5.4 %copy-start.11 = (bf16[1024,1408]{1,0:T(8,128)(2,1)S(1)}, bf16[1024,1408]{1,0:T(8,128)(2,1)}, u32[]{:S(2)}) copy-start(bf16[1024,1408]{1,0:T(8,128)(2,1)} %get-tuple-element.78) | copy-start | bytes 8650756
  448.5 14.7 %collective-permute-start.3 = (f32[2,1024]{1,0:T(2,128)S(1)}, f32[2,1024]{1,0:T(2,128)S(1)}, u32[]{:S(2)}, u32[]{:S(2)}) collective-permute-start(f32[2,1024]{1,0:T(2,128)S(1)} %fusion.33), channel_id=1, source_target_pairs={{0,8},{8,0},{16,24},{24,16},{1,9},{9,1},{17,25},{25,17},{2,10},{10... | collective-permute-start | bytes 24584 | tf_op jit(solution)/shard_map/ppermute | solution.py:1422
  453.9 3.0 copy-start.10
  456.9 3.0 copy-start.9

commit v5 on v4

--- a/solution.py
+++ b/solution.py
@@ -96,50 +96,41 @@
 
 class Relay:
     def __init__(self, n_ctx, src, dst, send, recv):
-        self.src, self.dst, self.send, self.recv = src, dst, send, recv
-        self.piece = src.shape[0] // n_ctx
-        self.ctx = lax.axis_index("ctx")
-        self.bits = high_bits(n_ctx)
-        self.count = 0
-        self.all = []
-        self.last = []
-
-    def _copy(self, src, dst, axis, bit):
-        e = self.count
-        self.count += 1
-        copy = pltpu.make_async_remote_copy(
-            src_ref=src,
-            dst_ref=dst,
-            send_sem=self.send.at[e],
-            recv_sem=self.recv.at[e],
-            device_id={axis: lax.axis_index(axis) ^ bit},
-            device_id_type=MESH,
-        )
-        copy.start()
-        self.all.append(copy)
-        return copy
-
-    def _cut(self, which):
-        return pl.ds(pl.multiple_of(which * self.piece, self.piece), self.piece)
+        piece = src.shape[0] // n_ctx
+        ctx = lax.axis_index("ctx")
+        bits = high_bits(n_ctx)
+
+        def cut(which):
+            return pl.ds(pl.multiple_of(which * piece, piece), piece)
+
+        self.levels = [[exchange(src.at[cut(ctx)], dst.at[cut(ctx)], "fsdp", 1, send.at[0], recv.at[0])]]
+        e = 1
+        for j, bit in enumerate(bits):
+            level = []
+            for m in masks_of(bits[:j]):
+                part = dst.at[cut(ctx ^ m)]
+                level.append(exchange(part, part, "ctx", bit, send.at[e], recv.at[e]))
+                e += 1
+            self.levels.append(level)
 
     def start(self):
-        mine = self._cut(self.ctx)
-        self.last = [self._copy(self.src.at[mine], self.dst.at[mine], "fsdp", 1)]
-
-    def hop(self, j):
-        self.landed()
-        bit = self.bits[j]
-        parts = [self.dst.at[self._cut(self.ctx ^ m)] for m in masks_of(self.bits[:j])]
-        self.last = [self._copy(part, part, "ctx", bit) for part in parts]
-
-    def landed(self):
-        for copy in self.last:
+        self.levels[0][0].start()
+
+    def hop(self, j, landed=True):
+        if landed:
+            for copy in self.levels[j]:
+                copy.wait_recv()
+        for copy in self.levels[j + 1]:
+            copy.start()
+
+    def landed(self, j=-1):
+        for copy in self.levels[j]:
             copy.wait_recv()
-        self.last = []
-
-    def drain(self):
-        for copy in self.all:
-            copy.wait_send()
+
+    def drain(self, levels=slice(None)):
+        for level in self.levels[levels]:
+            for copy in level:
+                copy.wait_send()
 
 
 def forward_kernel(
@@ -183,7 +174,7 @@
     down = Relay(n_ctx, down_ref, down_other, relay_send.at[2], relay_recv.at[2])
     gate.start()
     up.start()
-    down.hop(0)
+    down.hop(0, landed=False)
     step, steps, drain = line_sum(n_head, left, right, left, right, sum_ref, from_lo, from_hi, sems)
     size = rows // GROUPS
     stack = heads * size
@@ -210,6 +201,11 @@
         return carry
 
     def one_group(g, carry):
+        @pl.when(g == GROUPS - 1)
+        def _():
+            gate.hop(0)
+            down.hop(1)
+
         mine = pl.ds(pl.multiple_of(g * size, size), size)
         first_row = block * rows + g * size
         for h in range(heads):
@@ -243,10 +239,7 @@
         right[mine, :] = matmul(att, wr_ref[...]).astype(BF)
         return carry
 
-    lax.fori_loop(0, GROUPS - 1, one_group, 0)
-    gate.hop(0)
-    down.hop(1)
-    lax.fori_loop(GROUPS - 1, GROUPS, one_group, 0)
+    lax.fori_loop(0, GROUPS, one_group, 0)
     hops = len(high_bits(n_ctx))
     later = [(down, j) for j in range(2, hops)] + [(gate, 1), (up, 0)]
     for j in range(1, hops):
@@ -261,7 +254,9 @@
     lax.fori_loop(at, steps, run, 0)
     for relay in (gate, up, down):
         relay.landed()
-        relay.drain()
+    gate.drain()
+    up.drain()
+    down.drain(slice(1, None))
     drain()
 
 
@@ -315,10 +310,8 @@
     p_ref,
     left_ref,
     right_ref,
-    gate_sent,
-    gate_kept,
-    up_sent,
-    up_kept,
+    gate_both,
+    up_both,
     dq_ref,
     dp_ref,
     sum_ref,
@@ -358,7 +351,7 @@
     pl.semaphore_wait(barrier, line_peers(n_head) + len(partners(n_ctx)))
     crosses = [
         exchange(sent, land, "fsdp", 1, cross_send.at[i], cross_recv.at[i])
-        for i, (sent, land) in enumerate(((gate_sent, gate_land), (up_sent, up_land)))
+        for i, (sent, land) in enumerate(((gate_both.at[1], gate_land), (up_both.at[1], up_land)))
     ]
     for cross in crosses:
         cross.start()
@@ -370,7 +363,7 @@
 
     def hop():
         crosses[0].wait_recv()
-        add_into(gate_out, gate_kept, gate_land)
+        add_into(gate_out, gate_both.at[0], gate_land)
         far.start()
 
     def head_tile(h, pairs, start, masked):
@@ -440,7 +433,7 @@
     lax.fori_loop(jnp.minimum(begun, steps), steps, rest, 0)
     drain()
     crosses[1].wait_recv()
-    add_into(up_out, up_kept, up_land)
+    add_into(up_out, up_both.at[0], up_land)
     for cross in crosses:
         cross.wait_send()
     far.finish()
@@ -453,7 +446,7 @@
     group = 4 if heads % 4 == 0 else 2
     span = min(512, rows)
     vmem = pl.BlockSpec(memory_space=pltpu.VMEM)
-    flat = jax.ShapeDtypeStruct(parts[0].shape, BF)
+    flat = jax.ShapeDtypeStruct(parts[0].shape[1:], BF)
     n_far = len(high_bits(n_ctx)) - 1
     cost = pl.CostEstimate(
         flops=32 * rows * seq * width, bytes_accessed=8 * rows * width, transcendentals=0
@@ -467,7 +460,7 @@
             flat,
             flat,
         ),
-        in_specs=[vmem] * 11,
+        in_specs=[vmem] * 9,
         out_specs=(vmem,) * 5,
         scratch_shapes=[
             pltpu.VMEM((heads, rows, 128), BF),
@@ -665,9 +658,10 @@
     for j in range(1, len(high_bits(n_ctx))):
         second.hop(j)
     second.landed()
-    third.landed()
-    for relay in first + [second, third]:
+    third.landed(0)
+    for relay in first + [second]:
         relay.drain()
+    third.drain(slice(0, 1))
     gains.wait_send()
 
 
@@ -1146,21 +1140,26 @@
     cot_ref,
     gain_ref,
     gain_other,
+    gate_l_hbm,
+    gate_r_hbm,
+    up_l_hbm,
+    up_r_hbm,
+    down_l_hbm,
+    down_r_hbm,
+    sum_ref,
+    ffn_left,
+    ffn_right,
+    down_kept,
+    gate_both,
+    up_both,
     gate_l,
     gate_r,
     up_l,
     up_r,
     down_l,
     down_r,
-    sum_ref,
+    load_sem,
     n_ref,
-    ffn_left,
-    ffn_right,
-    down_kept,
-    gate_kept,
-    gate_sent,
-    up_kept,
-    up_sent,
     act_ref,
     gig_ref,
     uig_ref,
@@ -1195,6 +1194,21 @@
     barrier = line_greet(n_head)
     pl.semaphore_signal(barrier, inc=1, device_id={"fsdp": 1 - x_at}, device_id_type=MESH)
     pl.semaphore_signal(barrier, inc=1, device_id={"ctx": ctx_at ^ 1}, device_id_type=MESH)
+    loads = [
+        pltpu.make_async_copy(src, dst, load_sem.at[i])
+        for i, (src, dst) in enumerate(
+            (
+                (gate_l_hbm, gate_l),
+                (gate_r_hbm, gate_r),
+                (up_l_hbm, up_l),
+                (up_r_hbm, up_r),
+                (down_l_hbm, down_l),
+                (down_r_hbm, down_r),
+            )
+        )
+    ]
+    for load in loads:
+        load.start()
     pl.semaphore_wait(barrier, line_peers(n_head) + 2)
 
     def trade(src, dst, at):
@@ -1252,12 +1266,24 @@
         n_ref[mine, :half] = (hid_l * scale * gain_ref[1:2, :]).astype(BF)
         n_ref[mine, half:] = (hid_r * scale * gain_other[1:2, :]).astype(BF)
         lax.fori_loop(stops[0], stops[1], run, 0)
+
+        @pl.when(g == 0)
+        def _():
+            for load in loads[:4]:
+                load.wait()
+
         gate = matmul(n_ref[mine, :half], gate_l[...]) + matmul(n_ref[mine, half:], gate_r[...])
         up = matmul(n_ref[mine, :half], up_l[...]) + matmul(n_ref[mine, half:], up_r[...])
         lax.fori_loop(stops[1], stops[2], run, 0)
         sigma = jax.nn.sigmoid(gate)
         silu = gate * sigma
         act_ref[mine, :] = (silu * up).astype(BF)
+
+        @pl.when(g == 0)
+        def _():
+            for load in loads[4:]:
+                load.wait()
+
         grad = mat_trans(cot_ref[mine, own], down_l[...]) + mat_trans(cot_ref[mine, other], down_r[...])
         gig_ref[mine, :] = (grad * up * sigma * (1.0 + gate * (1.0 - sigma))).astype(BF)
         uig_ref[mine, :] = (grad * silu).astype(BF)
@@ -1319,22 +1345,18 @@
     done = down_tiles
 
     def out_copy(dst, t, slot):
-        cut = pl.ds(pl.multiple_of(t * tile, tile), tile)
-        return pltpu.make_async_copy(out_tile.at[slot], dst.at[cut], out_sem.at[slot])
-
-    outs = (
-        (gate_sent, 1, gig_ref, gig_land),
-        (gate_kept, 0, gig_ref, gig_land),
-        (up_sent, 1, uig_ref, uig_land),
-        (up_kept, 0, uig_ref, uig_land),
-    )
-    for dst, side, own_grad, their_grad in outs:
+        cut = pl.ds(pl.multiple_of(lax.rem(t, row_tiles) * tile, tile), tile)
+        return pltpu.make_async_copy(out_tile.at[slot], dst.at[1 - t // row_tiles, cut], out_sem.at[slot])
+
+    for dst, own_grad, their_grad in ((gate_both, gig_ref, gig_land), (up_both, uig_ref, uig_land)):
 
         def row_tile(t, carry):
             sums(done + t)
             slot = lax.rem(t, 2)
-            there = pl.ds(pl.multiple_of(side * half + core * quarter + t * tile, tile), tile)
-            landing = pl.ds(pl.multiple_of(side * quarter + t * tile, tile), tile)
+            side = 1 - t // row_tiles
+            row = lax.rem(t, row_tiles) * tile
+            there = pl.ds(pl.multiple_of(side * half + core * quarter + row, tile), tile)
+            landing = pl.ds(pl.multiple_of(side * quarter + row, tile), tile)
             value = (
                 trans_mat(n_ref[:, there], own_grad[...]) + trans_mat(n_land[:, landing], their_grad[...])
             ).astype(BF)
@@ -1347,10 +1369,10 @@
             out_copy(dst, t, slot).start()
             return carry
 
-        lax.fori_loop(0, row_tiles, row_tile, 0)
-        for t in range(max(row_tiles - 2, 0), row_tiles):
+        lax.fori_loop(0, 2 * row_tiles, row_tile, 0)
+        for t in range(2 * row_tiles - 2, 2 * row_tiles):
             out_copy(dst, t, t % 2).wait()
-        done += row_tiles
+        done += 2 * row_tiles
 
     def project_down(g, carry):
         mine = pl.ds(pl.multiple_of(g * size, size), size)
@@ -1388,14 +1410,17 @@
     wide = jax.ShapeDtypeStruct((rows, width), BF)
     narrow = jax.ShapeDtypeStruct((rows, width // 2), BF)
     quarter = width // 4
-    flat = jax.ShapeDtypeStruct((quarter, units), BF)
+    flat = jax.ShapeDtypeStruct((2, quarter, units), BF)
+    anywhere = pl.BlockSpec(memory_space=pl.ANY)
     trades = 2 + 5 * FFN_GROUPS
     return pl.pallas_call(
         functools.partial(ffn_kernel, n_head),
-        out_shape=(wide, wide, narrow, narrow, jax.ShapeDtypeStruct((units, quarter), BF)) + (flat,) * 4,
-        in_specs=[vmem] * 11,
-        out_specs=(vmem,) * 5 + (pl.BlockSpec(memory_space=pl.ANY),) * 4,
-        scratch_shapes=[pltpu.VMEM((rows, units), BF)] * 3
+        out_shape=(wide, narrow, narrow, jax.ShapeDtypeStruct((units, quarter), BF), flat, flat),
+        in_specs=[vmem] * 5 + [anywhere] * 6,
+        out_specs=(vmem,) * 4 + (anywhere,) * 2,
+        scratch_shapes=[pltpu.VMEM(w.shape, BF) for w in (gate, gate, up, up, down, down)]
+        + [pltpu.SemaphoreType.DMA((6,)), pltpu.VMEM((rows, width), BF)]
+        + [pltpu.VMEM((rows, units), BF)] * 3
         + [pltpu.VMEM((rows, width // 2), BF)] * 2
         + [pltpu.VMEM((rows, units), BF)] * 3
         + [pltpu.VMEM((units, quarter), BF)] * 2
@@ -1416,6 +1441,92 @@
         ),
         name="ffn_sum",
     )(inputs, mixed, cot, gains, gains_other, gate, gate_o, up, up_o, down, down_o)
+
+
+def halves(ref, x_at):
+    half = ref.shape[1] // 2
+    own = pl.ds(pl.multiple_of(x_at * half, half), half)
+    other = pl.ds(pl.multiple_of((1 - x_at) * half, half), half)
+    return ref[:, own].astype(F32), ref[:, other].astype(F32)
+
+
+def norm_back(values, grads, gains, width):
+    scale = lax.rsqrt(sum(jnp.sum(v * v, axis=1, keepdims=True) for v in values) / width + EPSILON)
+    units = [v * scale for v in values]
+    scaled = [g * gain for g, gain in zip(grads, gains)]
+    mean = sum(jnp.sum(s * u, axis=1, keepdims=True) for s, u in zip(scaled, units)) / width
+    return [scale * (s - u * mean) for s, u in zip(scaled, units)], [g * u for g, u in zip(grads, units)]
+
+
+def add_gain(gain_ref, products):
+    @pl.when(pl.program_id(0) == 0)
+    def _():
+        gain_ref[...] = jnp.zeros_like(gain_ref)
+
+    half = products[0].shape[1]
+    gain_ref[0:1, :half] += jnp.sum(products[0], axis=0, keepdims=True)
+    gain_ref[0:1, half:] += jnp.sum(products[1], axis=0, keepdims=True)
+
+
+def middle_kernel(at_ref, x_ref, mix_ref, grad_ref, cot_ref, gain_ref, other_ref, wl_ref, wr_ref, hid_ref, low_ref, att_ref, part_ref):
+    width = x_ref.shape[1]
+    half = width // 2
+    x_at = at_ref[0]
+    x_l, x_r = halves(x_ref, x_at)
+    cot_l, cot_r = halves(cot_ref, x_at)
+    values = (x_l + mix_ref[:, :half].astype(F32), x_r + mix_ref[:, half:].astype(F32))
+    grads = (grad_ref[:, :half].astype(F32), grad_ref[:, half:].astype(F32))
+    (d_l, d_r), products = norm_back(values, grads, (gain_ref[1:2, :], other_ref[1:2, :]), width)
+    add_gain(part_ref, products)
+    hid_l = cot_l + d_l
+    hid_r = cot_r + d_r
+    hid_ref[:, :half] = hid_l
+    hid_ref[:, half:] = hid_r
+    low_l = hid_l.astype(BF)
+    low_r = hid_r.astype(BF)
+    low_ref[:, :half] = low_l
+    low_ref[:, half:] = low_r
+    att_ref[...] = (mat_trans(low_l, wl_ref[...]) + mat_trans(low_r, wr_ref[...])).astype(BF)
+
+
+def end_kernel(at_ref, x_ref, mix_ref, ffn_ref, grad_ref, hid_ref, gain_ref, other_ref, out_ref, in_grad_ref, part_ref):
+    width = x_ref.shape[1]
+    half = width // 2
+    x_at = at_ref[0]
+    own = pl.ds(pl.multiple_of(x_at * half, half), half)
+    other = pl.ds(pl.multiple_of((1 - x_at) * half, half), half)
+    x_l, x_r = halves(x_ref, x_at)
+    out_ref[:, own] = (x_l + mix_ref[:, :half].astype(F32) + ffn_ref[:, :half].astype(F32)).astype(BF)
+    out_ref[:, other] = (x_r + mix_ref[:, half:].astype(F32) + ffn_ref[:, half:].astype(F32)).astype(BF)
+    grads = (grad_ref[:, :half].astype(F32), grad_ref[:, half:].astype(F32))
+    (d_l, d_r), products = norm_back((x_l, x_r), grads, (gain_ref[0:1, :], other_ref[0:1, :]), width)
+    add_gain(part_ref, products)
+    in_grad_ref[:, own] = hid_ref[:, :half] + d_l
+    in_grad_ref[:, other] = hid_ref[:, half:] + d_r
+
+
+def by_rows(kernel, x_at, arrays, whole, outs):
+    rows, width = arrays[0].shape
+    size = min(128, rows)
+
+    def block(shape):
+        return pl.BlockSpec((size, shape[1]), lambda i, *_: (i, 0))
+
+    def all_of(shape):
+        return pl.BlockSpec(shape, lambda i, *_: (0, 0))
+
+    gain = jax.ShapeDtypeStruct((8, width), F32)
+    return pl.pallas_call(
+        kernel,
+        out_shape=tuple(outs) + (gain,),
+        grid_spec=pltpu.PrefetchScalarGridSpec(
+            num_scalar_prefetch=1,
+            grid=(rows // size,),
+            in_specs=[block(a.shape) for a in arrays] + [all_of(a.shape) for a in whole],
+            out_specs=[block(o.shape) for o in outs] + [all_of(gain.shape)],
+        ),
+        cost_estimate=pl.CostEstimate(flops=4_000_000_000, bytes_accessed=24 * rows * width, transcendentals=0),
+    )(x_at, *arrays, *whole)
 
 
 def flip(array, axis, bit, size):
@@ -1445,10 +1556,6 @@
     block = ctx_at * 2 + x_at
     block_arr = jnp.reshape(block, (1,)).astype(jnp.int32)
 
-    def own_first(array):
-        swapped = jnp.concatenate([array[:, half:], array[:, :half]], axis=1)
-        return jnp.where(x_at == 0, array, swapped)
-
     every = high_bits(n_ctx)
 
     q_width = query_weight.shape[1]
@@ -1468,7 +1575,7 @@
     attended, lse, mixed, gate_other, up_other, down_other = attend_sum(
         queries, pair, output_weight, out_other, gate_weight, up_weight, down_begun, n_ctx, n_head, 1
     )
-    low_sum, _, down_left, down_right, down_kept, gate_kept, gate_sent, up_kept, up_sent = ffn_sum(
+    low_sum, down_left, down_right, down_kept, gate_both, up_both = ffn_sum(
         inputs,
         mixed,
         cotangent,
@@ -1483,31 +1590,20 @@
         n_head,
         2,
     )
-    normed_two_grad = low_sum.astype(F32)
-    gain_one = jnp.concatenate([gains_local[0], gains_other[0]])
-    gain_two = jnp.concatenate([gains_local[1], gains_other[1]])
-    late_inputs, late_cot, normed_one, _ = lax.optimization_barrier((inputs, cotangent, normed_one, low_sum))
-    in_float = own_first(late_inputs).astype(F32)
-    cot = own_first(late_cot)
-    scale_one = lax.rsqrt(jnp.mean(in_float * in_float, axis=-1, keepdims=True) + EPSILON)
-    unit_one = in_float * scale_one
-    hidden = in_float + mixed.astype(F32)
-    scale_two = lax.rsqrt(jnp.mean(hidden * hidden, axis=-1, keepdims=True) + EPSILON)
-    unit_two = hidden * scale_two
-    scaled_two = normed_two_grad * gain_two
-    gain_two_part = jnp.sum(normed_two_grad * unit_two, axis=0)
-    hidden_grad = cot.astype(F32) + scale_two * (
-        scaled_two - unit_two * jnp.mean(scaled_two * unit_two, axis=-1, keepdims=True)
+    x_arr = jnp.reshape(x_at, (1,)).astype(jnp.int32)
+    wide = jax.ShapeDtypeStruct((rows, width), F32)
+    flat = jax.ShapeDtypeStruct((rows, width), BF)
+    hidden_grad, hidden_low, attended_grad, gain_two_part = by_rows(
+        middle_kernel,
+        x_arr,
+        (inputs, mixed, low_sum, cotangent),
+        (gains_local, gains_other, output_weight, out_other),
+        (wide, flat, jax.ShapeDtypeStruct(attended.shape, BF)),
     )
-    hidden_low = hidden_grad.astype(BF)
-
-    attended_grad = (
-        mat_trans(hidden_low[:, :half], output_weight) + mat_trans(hidden_low[:, half:], out_other)
-    ).astype(BF)
     down_far = down_kept
     for bit in every[:-1]:
         down_far = (down_far.astype(F32) + flip(down_far, "ctx", bit, n_ctx).astype(F32)).astype(BF)
-    query_acc, pair_acc, ffn_out, gate_far, up_kept = attend_back(
+    query_acc, pair_acc, ffn_out, gate_far, up_crossed = attend_back(
         queries,
         attended_grad,
         attended,
@@ -1515,12 +1611,11 @@
         pair,
         down_left,
         down_right,
-        (gate_sent, gate_kept, up_sent, up_kept),
+        (gate_both, up_both),
         n_ctx,
         n_head,
         6,
     )
-    outputs = own_first((hidden + ffn_out.astype(F32)).astype(BF))
     last, qkv_full, out_full, gate_full, up_full, down_full = last_sum(
         query_acc,
         pair_acc,
@@ -1531,27 +1626,21 @@
         normed_one,
         attended,
         hidden_low,
-        up_kept,
+        up_crossed,
         gate_far,
         down_far,
         n_ctx,
         n_head,
         3,
     )
-    normed_one_grad = last.astype(F32)
-    gain_one_part = jnp.sum(normed_one_grad * unit_one, axis=0)
-    scaled_one = normed_one_grad * gain_one
-    input_grad = own_first(
-        hidden_grad
-        + scale_one
-        * (scaled_one - unit_one * jnp.mean(scaled_one * unit_one, axis=-1, keepdims=True))
+    outputs, input_grad, gain_one_part = by_rows(
+        end_kernel, x_arr, (inputs, mixed, ffn_out, last, hidden_grad), (gains_local, gains_other), (flat, wide)
     )
-
     query_grad = qkv_full[:, :q_width].astype(F32)
     key_grad = qkv_full[:, q_width : q_width + HEAD_DIM].astype(F32)
     value_grad = qkv_full[:, q_width + HEAD_DIM :].astype(F32)
 
-    gain_parts = jnp.stack([gain_one_part, gain_two_part])
+    gain_parts = jnp.stack([gain_one_part[0], gain_two_part[0]])
     gain_kept = gain_parts[:, :half] + flip(gain_parts[:, half:], "fsdp", 1, 2)
     for bit in every:
         gain_kept = gain_kept + flip(gain_kept, "ctx", bit, n_ctx)

time: 471 us -> 440 us (0.934); the launches traced: 464 us -> 439 us
  other arithmetic: 43.4 us -> 20.2 us
  Pallas kernels: 397 us -> 404 us
  local copies, waits for them, and re-layouts: 14.8 us -> 7.87 us
    reduce_sum x3 -> x0, other arithmetic: 7.55 us -> none  [the longest x1 3.7 us: shards(): gain_one_part = jnp.sum(normed_one_grad * unit_one, axis=0)]
    add x1 -> x0, other arithmetic: 6.82 us -> none  [shards(): hidden_grad + scale_one * (scaled_one - unit_one * jnp.mean(scaled_one *...]
    pallas_call x1 -> x3, Pallas kernels: 99.8 us -> 106 us  [the longest x1 86.9 us: ffn_sum(): pl.pallas_call(functools.partial(ffn_kernel, n_head), out_shape=(wide, na...]
    select_n x2 -> x0, other arithmetic: 5.27 us -> none  [own_first(): return jnp.where(x_at == 0, array, swapped)]
  transfers between devices with their start and end apart: 4 -> 4, of which waited for: 1 -> 2; matrix products, arithmetic and copies ran while one was open for 9% -> 4% of each run, Pallas kernels for 17% -> 20%
where the time goes in v5:
time: 440 us; the launch traced here: 439 us
  Pallas kernels  404 us (92%)
  other arithmetic  20.2 us (5%)
  local copies, waits for them, and re-layouts  7.87 us (2%)
  starting transfers between devices  4.44 us (1%)
    pallas_call x1, Pallas kernels, last_sum(): pl.pallas_call(functools.partial(last_kernel, n_ctx, n_head), out_shape=(...  90.6 us
    pallas_call x1, Pallas kernels, ffn_sum(): pl.pallas_call(functools.partial(ffn_kernel, n_head), out_shape=(wide, na...  86.9 us
    pallas_call x1, Pallas kernels, attend_back(): pl.pallas_call(functools.partial(backward_kernel, n_ctx, n_head, group, s...  78.6 us
    pallas_call x1, Pallas kernels, attend_sum(): pl.pallas_call(functools.partial(forward_kernel, n_ctx, n_head, span), ou...  77.5 us
    pallas_call x1, Pallas kernels, project(): pl.pallas_call(functools.partial(project_kernel, n_ctx), out_shape=(jax.S...  51.7 us
    pallas_call x2, Pallas kernels, by_rows(): pl.pallas_call(kernel, out_shape=tuple(outs) + (gain,), grid_spec=pltpu.P...  18.8 us
  transfers between devices with their start and end apart: 4, of which 2 were waited for; matrix products, arithmetic and copies ran while one was open for 4% of the time, Pallas kernels for 20%

profile of v5, /device:TPU:0, one launch (start us, length us, event | category | flops | bytes accessed | tf_op | source)
XLA Modules:
  0.0 439.5 jit_solution(7227278185294796957)
XLA Ops:
  0.7 0.7 broadcast_in_dim.10
  1.4 0.7 broadcast_in_dim.11
  2.1 1.1 copy.23
  3.1 1.1 copy.24
  4.2 0.1 pad.4.clone
  4.3 0.7 maximum_convert_fusion.gain_ref
  5.0 2.5 pad_maximum_fusion.w_ref.w_l
  7.5 1.8 negate_select_fusion
  9.3 51.7 %project.1 = (bf16[512,512]{1,0:T(8,128)(2,1)}, bf16[4096,128]{1,0:T(8,128)(2,1)}, bf16[512,2048]{1,0:T(8,128)(2,1)}, bf16[1024,640]{1,0:T(8,128)(2,1)}, f32[8,1...) custom-call(bf16[512,2048]{1,0:T(8,128)(2,1)} %x_ref.7, ...), custom_call_target="tpu_custom_call" | custom-call | tf_op jit(solution)/shard_map/project/pallas_call | solution.py:672
  61.0 77.5 %attend_sum.1 = (bf16[512,512]{1,0:T(8,128)(2,1)}, f32[8,1,512]{2,1,0:T(1,128)}, bf16[512,2048]{1,0:T(8,128)(2,1)}, bf16[1024,1408]{1,0:T(8,128)(2,1)}, bf16[102...) custom-call(bf16[512,512]{1,0:T(8,128)(2,1)} %get-tuple-element.48.q_ref, ...), custom_call_target="tpu_custom_call", output_to_operand_aliasing={{5}: (6, {})} | custom-call | flops 49999998976 | bytes 8388608 | tf_op jit(solution)/shard_map/attend_sum/pallas_call | solution.py:273
  138.4 86.9 %ffn_sum.1 = (bf16[512,2048]{1,0:T(8,128)(2,1)}, bf16[512,1024]{1,0:T(8,128)(2,1)}, bf16[512,1024]{1,0:T(8,128)(2,1)}, bf16[1408,512]{1,0:T(8,128)(2,1)}, bf16[2...) custom-call(bf16[512,2048]{1,0:T(8,128)(2,1)} %x_ref.7, bf16[512,2048]{1,0:T(8,128)(2,1)} %get-tuple-element.52.mix_ref, ...), custom_call_target="tpu_custom_call" | custom-call | flops 49999998976 | bytes 8388608 | tf_op jit(solution)/shard_map/ffn_sum/pallas_call | solution.py:1416
  225.3 0.4 collective-permute-start
  225.7 9.8 %shard_map.194 = (f32[512,2048]{1,0:T(8,128)}, bf16[512,2048]{1,0:T(8,128)(2,1)}, bf16[512,512]{1,0:T(8,128)(2,1)}, f32[8,2048]{1,0:T(8,128)}) custom-call(s32[1]{0:T(128)} %bitcast.at_ref, bf16[512,2048]{1,0:T(8,128)(2,1)} %x_ref.7, bf16[512,2048]{1,0:T(8,128)(2,1)} %get-tuple-element.52.mix_ref, bf16[512,2048]{1,0:T(8,128)(2,1)} %get-tuple-element.57.grad_ref, ...), custom_call_target="tpu_custom_call" | custom-call | flops 4000000000 | bytes 25165824 | tf_op jit(solution)/shard_map/pallas_call | solution.py:1519
  235.5 0.0 copy-start.4
  235.5 78.6 %attend_backward.1 = (f32[512,512]{1,0:T(8,128)}, f32[4096,128]{1,0:T(8,128)}, bf16[512,2048]{1,0:T(8,128)(2,1)}, bf16[512,1408]{1,0:T(8,128)(2,1)}, bf16[512,1408]{1,0:T(8,128)(2,1)}) custom-call(bf16[512,512]{1,0:T(8,128)(2,1)} %get-tuple-element.48.q_ref, bf16[512,512]{1,0:T(8,128)(2,1)} %get-tuple-element.58.g_ref, ...), custom_call_target="tpu_custom_call" | custom-call | flops 34359738368 | bytes 2097152 | tf_op jit(solution)/shard_map/attend_backward/pallas_call | solution.py:454
  314.1 0.8 slice.31
  315.0 0.0 collective-permute-done
  315.0 0.0 copy-done.4
  315.0 1.5 add_convert_fusion.down_ref
  316.5 90.6 %last_sum.1 = (bf16[512,2048]{1,0:T(8,128)(2,1)}, bf16[1024,640]{1,0:T(8,128)(2,1)}, bf16[512,1024]{1,0:T(8,128)(2,1)}, bf16[1024,1408]{1,0:T(8,128)(2,1)}, bf16...) custom-call(f32[512,512]{1,0:T(8,128)} %get-tuple-element.66.dq_ref, f32[4096,128]{1,0:T(8,128)} %get-tuple-element.67.part_ref, ...), custom_call_target="tpu_custom_call" | custom-call | flops 49999998976 | bytes 8388608 | tf_op jit(solution)/shard_map/last_sum/pallas_call | solution.py:1083
  407.1 0.0 copy-start.3
  407.1 9.0 %shard_map.195 = (bf16[512,2048]{1,0:T(8,128)(2,1)}, f32[512,2048]{1,0:T(8,128)}, f32[8,2048]{1,0:T(8,128)}) custom-call(s32[1]{0:T(128)} %bitcast.at_ref, bf16[512,2048]{1,0:T(8,128)(2,1)} %x_ref.7, bf16[512,2048]{1,0:T(8,128)(2,1)} %get-tuple-element.52.mix_ref, bf16[512,2048]{1,0:T(8,128)(2,1)} %get-tuple-element.65.ffn_ref, ...), custom_call_target="tpu_custom_call" | custom-call | flops 4000000000 | bytes 25165824 | tf_op jit(solution)/shard_map/pallas_call | solution.py:1519
  416.0 0.8 slice.30
  416.9 2.5 collective-permute-start.1
  419.4 1.6 collective-permute-done.1
  421.0 1.5 collective-permute-start.2
  422.5 0.0 copy-done.3
  422.5 1.6 slice_convert_fusion
  424.1 0.6 collective-permute-done.2
  424.7 0.1 collective-permute-start.3
  424.8 0.1 slice_convert_fusion.1
  425.0 0.9 copy.26
  425.8 0.0 copy-start.2
  425.9 0.9 copy.25
  426.7 2.9 convert_element_type.52
  429.6 0.0 copy-done.2
  429.6 0.0 copy-start.1
  429.6 2.9 convert_element_type.53
  432.5 0.1 copy-done.1
  432.6 0.0 copy-start
  432.6 2.9 convert_element_type.54
  435.5 0.1 copy-done
  435.6 3.2 convert_element_type.55
  438.9 0.0 collective-permute-done.3
  438.9 0.6 fusion.3
  (9 shorter events, 0.1 us)
Async XLA Ops:
  225.3 89.7 %collective-permute-start = (bf16[1408,512]{1,0:T(8,128)(2,1)}, bf16[1408,512]{1,0:T(8,128)(2,1)S(1)}, u32[]{:S(2)}, u32[]{:S(2)}) collective-permute-start(bf16[1408,512]{1,0:T(8,128)(2,1)} %get-tuple-element.73), channel_id=1, source_target_pairs={{0,16},{8,24},{16,0},{24,8},{1,17},{9,25},{17,1},{25,9},{2,18},{10... | collective-permute-start | bytes 4325384 | tf_op jit(solution)/shard_map/ppermute | solution.py:1533
  235.5 79.5 %copy-start.4 = (bf16[1408,512]{1,0:T(8,128)(2,1)S(1)}, bf16[1408,512]{1,0:T(8,128)(2,1)}, u32[]{:S(2)}) copy-start(bf16[1408,512]{1,0:T(8,128)(2,1)} %get-tuple-element.73) | copy-start | bytes 4325380
  407.1 15.4 %copy-start.3 = (bf16[1024,640]{1,0:T(8,128)(2,1)S(1)}, bf16[1024,640]{1,0:T(8,128)(2,1)}, u32[]{:S(2)}) copy-start(bf16[1024,640]{1,0:T(8,128)(2,1)} %get-tuple-element.78) | copy-start | bytes 3932164
  416.9 4.1 collective-permute-start.1
  421.0 3.7 collective-permute-start.2
  424.7 14.1 %collective-permute-start.3 = (f32[2,1024]{1,0:T(2,128)S(1)}, f32[2,1024]{1,0:T(2,128)S(1)}, u32[]{:S(2)}, u32[]{:S(2)}) collective-permute-start(f32[2,1024]{1,0:T(2,128)S(1)} %fusion.4), channel_id=1, source_target_pairs={{0,8},{8,0},{16,24},{24,16},{1,9},{9,1},{17,25},{25,17},{2,10},{10... | collective-permute-start | bytes 24584 | tf_op jit(solution)/shard_map/ppermute | solution.py:1533
  425.8 3.8 copy-start.2
  429.6 3.0 copy-start.1
  432.6 3.0 copy-start

commit v6 on v5

--- a/solution.py
+++ b/solution.py
@@ -175,7 +175,7 @@
     gate.start()
     up.start()
     down.hop(0, landed=False)
-    step, steps, drain = line_sum(n_head, left, right, left, right, sum_ref, from_lo, from_hi, sems)
+    step, steps, drain = line_sum(n_head, left, right, left, right, sum_ref, from_lo, from_hi, sems, 2)
     size = rows // GROUPS
     stack = heads * size
     sub = min(512, stack)
@@ -340,6 +340,32 @@
     block = lax.axis_index("ctx") * 2 + lax.axis_index("fsdp")
     barrier = line_greet(n_head)
     greet(n_ctx)
+    pl.semaphore_wait(barrier, line_peers(n_head) + len(partners(n_ctx)))
+    part = gate_out.shape[0] // 2
+    tops = [pl.ds(i * part, part) for i in range(2)]
+    crosses = [
+        exchange(gate_both.at[1, top], gate_land.at[top], "fsdp", 1, cross_send.at[i], cross_recv.at[i])
+        for i, top in enumerate(tops)
+    ] + [exchange(up_both.at[1], up_land, "fsdp", 1, cross_send.at[2], cross_recv.at[2])]
+    for cross in crosses:
+        cross.start()
+    fars = [
+        Chain(n_ctx, gate_out.at[top], far_land.at[i], far_send.at[i], far_recv.at[i])
+        for i, top in enumerate(tops)
+    ]
+    hops = (11, 19)
+    step, steps, drain = line_sum(
+        n_head, left_ref, right_ref, work_l, work_r, sum_ref, from_lo, from_hi, sems
+    )
+
+    def hop(i):
+        crosses[i].wait_recv()
+        add_into(gate_out.at[tops[i]], gate_both.at[0, tops[i]], gate_land.at[tops[i]])
+        fars[i].start()
+
+    ahead = 3
+    for s in range(ahead):
+        step(s)
     dp_ref[...] = jnp.zeros_like(dp_ref)
     acc_ref[...] = jnp.zeros_like(acc_ref)
     for h in range(heads):
@@ -348,23 +374,6 @@
         g_pad[h] = head_lanes(g_ref, h, True)
         product = g_ref[:, cut].astype(F32) * o_ref[:, cut].astype(F32)
         dl_ref[h] = jnp.sum(product.T, axis=0, keepdims=True)
-    pl.semaphore_wait(barrier, line_peers(n_head) + len(partners(n_ctx)))
-    crosses = [
-        exchange(sent, land, "fsdp", 1, cross_send.at[i], cross_recv.at[i])
-        for i, (sent, land) in enumerate(((gate_both.at[1], gate_land), (up_both.at[1], up_land)))
-    ]
-    for cross in crosses:
-        cross.start()
-    far = Chain(n_ctx, gate_out, far_land, far_send, far_recv)
-    hop_at = CHUNKS + 2
-    step, steps, drain = line_sum(
-        n_head, left_ref, right_ref, work_l, work_r, sum_ref, from_lo, from_hi, sems
-    )
-
-    def hop():
-        crosses[0].wait_recv()
-        add_into(gate_out, gate_both.at[0], gate_land)
-        far.start()
 
     def head_tile(h, pairs, start, masked):
         probs = jnp.exp(mat_trans(pairs, q_pad[h]) - lse_ref[h])
@@ -381,13 +390,15 @@
     def two_steps(t):
         for j in range(2):
 
-            @pl.when(2 * t + j < steps)
+            @pl.when(ahead + 2 * t + j < steps)
             def _():
-                step(2 * t + j)
-
-        @pl.when(2 * t == hop_at)
-        def _():
-            hop()
+                step(ahead + 2 * t + j)
+
+        for i in range(2):
+
+            @pl.when(ahead + 2 * t == hops[i])
+            def _():
+                hop(i)
 
     def full(t, carry):
         two_steps(t)
@@ -404,39 +415,42 @@
     lax.fori_loop(0, count, full, 0)
 
     def last(t, carry):
-        h = lax.rem(t, heads)
-
-        @pl.when(lax.rem(t, group) == 0)
+        h = lax.rem(2 * t, heads)
+
+        @pl.when(lax.rem(2 * t, group) == 0)
         def _():
-            two_steps(count + t // group)
-
-        start = pl.multiple_of(block * rows + (t // heads) * span, span)
+            two_steps(count + 2 * t // group)
+
+        start = pl.multiple_of(block * rows + (2 * t // heads) * span, span)
         cut = pl.ds(start, span)
-        dp_ref[cut, :] += head_tile(h, p_ref[cut, :], start, True)
-        return carry
-
-    lax.fori_loop(0, heads * tiles, last, 0)
+        dp_ref[cut, :] += head_tile(h, p_ref[cut, :], start, True) + head_tile(h + 1, p_ref[cut, :], start, True)
+        return carry
+
+    lax.fori_loop(0, heads * tiles // 2, last, 0)
     for h in range(heads):
         dq_ref[:, h * HEAD_DIM : (h + 1) * HEAD_DIM] = acc_ref[h][:, :HEAD_DIM]
 
-    begun = 2 * (count + groups * tiles)
+    begun = ahead + 2 * (count + groups * tiles)
 
     def rest(s, carry):
         step(s)
 
-        @pl.when(s == hop_at)
-        def _():
-            hop()
+        for i in range(2):
+
+            @pl.when(s == hops[i])
+            def _():
+                hop(i)
 
         return carry
 
     lax.fori_loop(jnp.minimum(begun, steps), steps, rest, 0)
     drain()
-    crosses[1].wait_recv()
+    crosses[2].wait_recv()
     add_into(up_out, up_both.at[0], up_land)
     for cross in crosses:
         cross.wait_send()
-    far.finish()
+    for far in fars:
+        far.finish()
 
 
 def attend_back(queries, grads, attended, lse, pair, left, right, parts, n_ctx, n_head, collective_id):
@@ -469,11 +483,11 @@
             pltpu.VMEM((heads, 1, rows), F32),
             pltpu.VMEM(flat.shape, BF),
             pltpu.VMEM(flat.shape, BF),
-            pltpu.VMEM((n_far,) + flat.shape, BF),
-            pltpu.SemaphoreType.DMA((2,)),
-            pltpu.SemaphoreType.DMA((2,)),
-            pltpu.SemaphoreType.DMA((n_far,)),
-            pltpu.SemaphoreType.DMA((n_far,)),
+            pltpu.VMEM((2, n_far, flat.shape[0] // 2, flat.shape[1]), BF),
+            pltpu.SemaphoreType.DMA((3,)),
+            pltpu.SemaphoreType.DMA((3,)),
+            pltpu.SemaphoreType.DMA((2, n_far)),
+            pltpu.SemaphoreType.DMA((2, n_far)),
         ]
         + line_scratch(rows, 2 * left.shape[1]),
         compiler_params=pltpu.CompilerParams(collective_id=collective_id, has_side_effects=True),
@@ -616,7 +630,6 @@
     lax.fori_loop(0, parts, norm, 0)
     for relay in first:
         relay.hop(0)
-    third.start()
     second.hop(0)
 
     def local(i, carry):
@@ -653,6 +666,7 @@
 
     lax.fori_loop(0, parts, pairs, 0)
     finish = gather_pairs(n_ctx, rows, p_ref, send, recv)
+    third.start()
     lax.fori_loop(0, parts, queries, 0)
     finish()
     for j in range(1, len(high_bits(n_ctx))):
@@ -696,7 +710,7 @@
     )(inputs, w_local, gains, cosine, sine, w_out, w_down)
 
 
-def line_sum(n, left, right, work_l, work_r, o_ref, from_lo, from_hi, sems):
+def line_sum(n, left, right, work_l, work_r, o_ref, from_lo, from_hi, sems, lag=LAG):
     s_up, r_up, s_dn, r_dn, s_a, r_a, s_b, r_b = sems
     me = lax.axis_index("head")
     rows, cols = left.shape
@@ -739,10 +753,10 @@
         return (mine[at(k), :].astype(F32) + there[at(k), :].astype(F32)).astype(BF)
 
     def step(s):
-        k1 = s - LAG * me
-        k2 = s - LAG * (n - 1 - me)
-        k3 = s - LAG * (n - 1 + me)
-        k4 = s - LAG * (2 * (n - 1) - me)
+        k1 = s - lag * me
+        k2 = s - lag * (n - 1 - me)
+        k3 = s - lag * (n - 1 + me)
+        k4 = s - lag * (2 * (n - 1) - me)
 
         @pl.when(jnp.logical_and(valid(k1), me == 0))
         def _():
@@ -808,7 +822,7 @@
 
         lax.fori_loop(0, CHUNKS, one, 0)
 
-    return step, CHUNKS + 2 * LAG * (n - 1), drain
+    return step, CHUNKS + 2 * lag * (n - 1), drain
 
 
 def line_greet(n):
@@ -942,25 +956,47 @@
             raw[cut, sl] = turned(dq_ref[cut, sl] * 0.125, cut).astype(BF)
         return carry
 
+    trades = [trade(att_ref, att_land, 0)]
+    for side in range(2):
+        landing = pl.ds(side * quarter, quarter)
+        trades.append(trade(low_ref.at[:, relative(side, 1 - core)], low_land.at[:, landing], 1 + side))
+    late = []
+    for side in range(2):
+        landing = pl.ds(side * quarter, quarter)
+        late.append(trade(n_ref.at[:, relative(side, 1 - core)], n_land.at[:, landing], 3 + side))
+
+    def out_tiles(dst, side):
+        def one(t, carry):
+            cut = pl.ds(pl.multiple_of(t * 128, 128), 128)
+            dst[cut, :] = (
+                trans_mat(att_ref[:, cut], low_ref[:, relative(side, core)])
+                + trans_mat(att_land[:, cut], low_land[:, side * quarter : (side + 1) * quarter])
+            ).astype(BF)
+            return carry
+
+        lax.fori_loop(0, q_width // 128, one, 0)
+
     bits = high_bits(n_ctx)
-    trades = []
     for j in range(len(bits)):
         bit = bits[len(bits) - 1 - j]
         masks = masks_of(bits[: len(bits) - 1 - j])
         now = [give((ctx ^ bit ^ m) * 2 * rows, 2 * rows, "ctx", bit) for m in masks]
         if j == 0:
+            for t in trades + late:
+                t.start()
             lax.fori_loop(0, rows // 128, rotate_rows, 0)
+        if j == 1:
+            for t in trades:
+                t.wait_recv()
+            out_tiles(out_sent, 1)
         for (copy, at), m in zip(now, masks):
             copy.wait_recv()
             take((ctx ^ m) * 2 * rows, 2 * rows, at)
     copy, at = give((ctx * 2 + 1 - x_at) * rows, rows, "fsdp", 1)
+    out_cross = exchange(out_sent, out_land, "fsdp", 1, cross_send.at[0], cross_recv.at[0])
+    out_cross.start()
     up_chain.start()
-    trades = [trade(att_ref, att_land, 0)]
-    for side in range(2):
-        trades.append(trade(low_ref.at[:, relative(side, 1 - core)], low_land.at[:, pl.ds(side * quarter, quarter)], 1 + side))
-        trades.append(trade(n_ref.at[:, relative(side, 1 - core)], n_land.at[:, pl.ds(side * quarter, quarter)], 3 + side))
-    for t in trades:
-        t.start()
+    out_tiles(out_kept, 0)
     copy.wait_recv()
     base = pl.multiple_of((ctx * 2 + x_at) * rows, rows)
 
@@ -975,7 +1011,7 @@
     lax.fori_loop(0, rows // 128, finish_pair, 0)
     raw_trade = trade(raw, raw_land, 5)
     raw_trade.start()
-    trades.append(raw_trade)
+    late.append(raw_trade)
     step, steps, drain = line_sum(n_head, left, right, left, right, sum_ref, from_lo, from_hi, sems)
 
     def run(s, carry):
@@ -995,18 +1031,6 @@
     for pair in spreads:
         for copy in pair:
             copy.start()
-
-    def out_tiles(dst, side):
-        def one(t, carry):
-            cut = pl.ds(pl.multiple_of(t * 128, 128), 128)
-            dst[cut, :] = (
-                trans_mat(att_ref[:, cut], low_ref[:, relative(side, core)])
-                + trans_mat(att_land[:, cut], low_land[:, side * quarter : (side + 1) * quarter])
-            ).astype(BF)
-            step(steps_at + t)
-            return carry
-
-        lax.fori_loop(0, q_width // 128, one, 0)
 
     def qkv_tiles(dst, side):
         def one(t, carry):
@@ -1022,45 +1046,41 @@
         lax.fori_loop(0, quarter // 128, one, 0)
 
     lax.fori_loop(0, 2, run, 0)
-    for t in trades:
+    for t in late:
         t.wait_recv()
     steps_at = 2
-    out_tiles(out_sent, 1)
-    out_cross = exchange(out_sent, out_land, "fsdp", 1, cross_send.at[0], cross_recv.at[0])
-    out_cross.start()
-    steps_at += q_width // 128
     qkv_tiles(qkv_sent, 1)
     qkv_cross = exchange(qkv_sent, qkv_land, "fsdp", 1, cross_send.at[1], cross_recv.at[1])
     qkv_cross.start()
     steps_at += quarter // 128
-    out_tiles(out_kept, 0)
-    steps_at += q_width // 128
     qkv_tiles(qkv_kept, 0)
     steps_at += quarter // 128
     out_cross.wait_recv()
     add_into(out_kept, out_kept, out_land)
     out_chain.start()
     rest = steps - steps_at
-    lax.fori_loop(steps_at, steps_at + rest // 4, run, 0)
+    stops = [steps_at + (rest * i) // 8 for i in range(9)]
+    lax.fori_loop(stops[0], stops[2], run, 0)
     qkv_cross.wait_recv()
     add_into(qkv_kept, qkv_kept, qkv_land)
     qkv_chain.start()
-    lax.fori_loop(steps_at + rest // 4, steps_at + rest // 2, run, 0)
+    lax.fori_loop(stops[2], stops[4], run, 0)
     up_chain.finish()
     spreads.append(spread(up_sum, up_full, True, 2))
     for copy in spreads[-1]:
         copy.start()
-    lax.fori_loop(steps_at + rest // 2, steps, run, 0)
+    lax.fori_loop(stops[4], stops[6], run, 0)
     out_chain.finish()
     spreads.append(spread(out_kept, out_full, False, 3))
     for copy in spreads[-1]:
         copy.start()
+    lax.fori_loop(stops[6], stops[8], run, 0)
     qkv_chain.finish()
     spreads.append(spread(qkv_kept, qkv_full, True, 4))
     for copy in spreads[-1]:
         copy.start()
     drain()
-    for t in pairs + trades + [out_cross, qkv_cross]:
+    for t in pairs + trades + late + [out_cross, qkv_cross]:
         t.wait_send()
     for local, remote in spreads:
         local.wait()
@@ -1568,7 +1588,7 @@
     sine = jnp.sin(angles)
     signed = jnp.where(lane % HEAD_DIM < half_dim, -sine, sine)
     qkv_local = jnp.concatenate([query_weight, key_weight, value_weight], axis=1)
-    gains_local = jnp.concatenate([attn_gain[None], ffn_gain[None], jnp.zeros((6, half), BF)]).astype(F32)
+    gains_local = jnp.stack([attn_gain.astype(F32), ffn_gain.astype(F32)])
     queries, pair, normed_one, qkv_other, gains_other, out_other, down_begun = project(
         inputs, qkv_local, gains_local, cosine, signed, output_weight, down_weight, q_width, n_ctx, 4
     )

time: 440 us -> 435 us (0.989)
    pallas_call x1, Pallas kernels: 78.6 us -> 73.7 us  [attend_back(): pl.pallas_call(functools.partial(backward_kernel, n_ctx, n_head, group, s...]
  transfers between devices with their start and end apart: 4 -> 4, of which waited for: 2 -> 2; matrix products, arithmetic and copies ran while one was open for 4% -> 4% of each run, Pallas kernels for 20% -> 19%
where the time goes in v6:
time: 435 us; the launch traced here: 434 us
  Pallas kernels  400 us (92%)
  other arithmetic  20.1 us (5%)
  local copies, waits for them, and re-layouts  7.79 us (2%)
    pallas_call x1, Pallas kernels, last_sum(): pl.pallas_call(functools.partial(last_kernel, n_ctx, n_head), out_shape=(...  91.8 us
    pallas_call x1, Pallas kernels, ffn_sum(): pl.pallas_call(functools.partial(ffn_kernel, n_head), out_shape=(wide, na...  86.9 us
    pallas_call x1, Pallas kernels, attend_sum(): pl.pallas_call(functools.partial(forward_kernel, n_ctx, n_head, span), ou...  81 us
    pallas_call x1, Pallas kernels, attend_back(): pl.pallas_call(functools.partial(backward_kernel, n_ctx, n_head, group, s...  73.7 us
    pallas_call x1, Pallas kernels, project(): pl.pallas_call(functools.partial(project_kernel, n_ctx), out_shape=(jax.S...  47.5 us
    pallas_call x2, Pallas kernels, by_rows(): pl.pallas_call(kernel, out_shape=tuple(outs) + (gain,), grid_spec=pltpu.P...  18.7 us
  transfers between devices with their start and end apart: 4, of which 2 were waited for; matrix products, arithmetic and copies ran while one was open for 4% of the time, Pallas kernels for 19%

profile of v6, /device:TPU:0, one launch (start us, length us, event | category | flops | bytes accessed | tf_op | source)
XLA Modules:
  0.0 434.4 jit_solution(10115854534068865813)
XLA Ops:
  0.7 0.7 stack.16
  1.4 0.7 stack.17
  2.1 1.1 copy.23
  3.1 1.1 copy.24
  4.2 0.6 maximum_convert_fusion.gain_ref
  4.8 2.5 pad_maximum_fusion.w_ref.w_l
  7.3 1.8 negate_select_fusion
  9.1 47.5 %project.1 = (bf16[512,512]{1,0:T(8,128)(2,1)}, bf16[4096,128]{1,0:T(8,128)(2,1)}, bf16[512,2048]{1,0:T(8,128)(2,1)}, bf16[1024,640]{1,0:T(8,128)(2,1)}, f32[2,1...) custom-call(bf16[512,2048]{1,0:T(8,128)(2,1)} %x_ref.7, ...), custom_call_target="tpu_custom_call" | custom-call | tf_op jit(solution)/shard_map/project/pallas_call | solution.py:686
  56.7 81.0 %attend_sum.1 = (bf16[512,512]{1,0:T(8,128)(2,1)}, f32[8,1,512]{2,1,0:T(1,128)}, bf16[512,2048]{1,0:T(8,128)(2,1)}, bf16[1024,1408]{1,0:T(8,128)(2,1)}, bf16[102...) custom-call(bf16[512,512]{1,0:T(8,128)(2,1)} %get-tuple-element.48.q_ref, ...), custom_call_target="tpu_custom_call", output_to_operand_aliasing={{5}: (6, {})} | custom-call | flops 49999998976 | bytes 8388608 | tf_op jit(solution)/shard_map/attend_sum/pallas_call | solution.py:273
  137.7 86.9 %ffn_sum.1 = (bf16[512,2048]{1,0:T(8,128)(2,1)}, bf16[512,1024]{1,0:T(8,128)(2,1)}, bf16[512,1024]{1,0:T(8,128)(2,1)}, bf16[1408,512]{1,0:T(8,128)(2,1)}, bf16[2...) custom-call(bf16[512,2048]{1,0:T(8,128)(2,1)} %x_ref.7, bf16[512,2048]{1,0:T(8,128)(2,1)} %get-tuple-element.52.mix_ref, ...), custom_call_target="tpu_custom_call" | custom-call | flops 49999998976 | bytes 8388608 | tf_op jit(solution)/shard_map/ffn_sum/pallas_call | solution.py:1436
  224.6 0.2 collective-permute-start
  224.8 9.9 %shard_map.194 = (f32[512,2048]{1,0:T(8,128)}, bf16[512,2048]{1,0:T(8,128)(2,1)}, bf16[512,512]{1,0:T(8,128)(2,1)}, f32[8,2048]{1,0:T(8,128)}) custom-call(s32[1]{0:T(128)} %bitcast.at_ref, bf16[512,2048]{1,0:T(8,128)(2,1)} %x_ref.7, bf16[512,2048]{1,0:T(8,128)(2,1)} %get-tuple-element.52.mix_ref, bf16[512,2048]{1,0:T(8,128)(2,1)} %get-tuple-element.57.grad_ref, ...), custom_call_target="tpu_custom_call" | custom-call | flops 4000000000 | bytes 25165824 | tf_op jit(solution)/shard_map/pallas_call | solution.py:1539
  234.7 0.0 copy-start.4
  234.7 73.7 %attend_backward.1 = (f32[512,512]{1,0:T(8,128)}, f32[4096,128]{1,0:T(8,128)}, bf16[512,2048]{1,0:T(8,128)(2,1)}, bf16[512,1408]{1,0:T(8,128)(2,1)}, bf16[512,1408]{1,0:T(8,128)(2,1)}) custom-call(bf16[512,512]{1,0:T(8,128)(2,1)} %get-tuple-element.48.q_ref, bf16[512,512]{1,0:T(8,128)(2,1)} %get-tuple-element.58.g_ref, ...), custom_call_target="tpu_custom_call" | custom-call | flops 34359738368 | bytes 2097152 | tf_op jit(solution)/shard_map/attend_backward/pallas_call | solution.py:468
  308.4 0.8 slice.31
  309.3 0.0 collective-permute-done
  309.3 0.0 copy-done.4
  309.3 1.5 add_convert_fusion.down_ref
  310.8 91.8 %last_sum.1 = (bf16[512,2048]{1,0:T(8,128)(2,1)}, bf16[1024,640]{1,0:T(8,128)(2,1)}, bf16[512,1024]{1,0:T(8,128)(2,1)}, bf16[1024,1408]{1,0:T(8,128)(2,1)}, bf16...) custom-call(f32[512,512]{1,0:T(8,128)} %get-tuple-element.66.dq_ref, f32[4096,128]{1,0:T(8,128)} %get-tuple-element.67.part_ref, ...), custom_call_target="tpu_custom_call" | custom-call | flops 49999998976 | bytes 8388608 | tf_op jit(solution)/shard_map/last_sum/pallas_call | solution.py:1103
  402.6 0.0 copy-start.3
  402.6 8.8 %shard_map.195 = (bf16[512,2048]{1,0:T(8,128)(2,1)}, f32[512,2048]{1,0:T(8,128)}, f32[8,2048]{1,0:T(8,128)}) custom-call(s32[1]{0:T(128)} %bitcast.at_ref, bf16[512,2048]{1,0:T(8,128)(2,1)} %x_ref.7, bf16[512,2048]{1,0:T(8,128)(2,1)} %get-tuple-element.52.mix_ref, bf16[512,2048]{1,0:T(8,128)(2,1)} %get-tuple-element.65.ffn_ref, ...), custom_call_target="tpu_custom_call" | custom-call | flops 4000000000 | bytes 25165824 | tf_op jit(solution)/shard_map/pallas_call | solution.py:1539
  411.4 0.8 slice.30
  412.2 1.9 collective-permute-start.1
  414.2 1.8 collective-permute-done.1
  416.0 0.8 collective-permute-start.2
  416.8 0.0 copy-done.3
  416.8 1.6 slice_convert_fusion
  418.4 1.3 collective-permute-done.2
  419.7 0.1 collective-permute-start.3
  419.8 0.1 slice_convert_fusion.1
  419.9 0.9 copy.26
  420.8 0.0 copy-start.2
  420.8 0.9 copy.25
  421.7 2.9 convert_element_type.50
  424.6 0.0 copy-done.2
  424.6 0.0 copy-start.1
  424.6 2.9 convert_element_type.51
  427.5 0.1 copy-done.1
  427.6 0.0 copy-start
  427.6 2.9 convert_element_type.52
  430.5 0.1 copy-done
  430.6 3.2 convert_element_type.53
  433.8 0.0 collective-permute-done.3
  433.8 0.6 fusion.3
  (8 shorter events, 0.1 us)
Async XLA Ops:
  224.6 84.7 %collective-permute-start = (bf16[1408,512]{1,0:T(8,128)(2,1)}, bf16[1408,512]{1,0:T(8,128)(2,1)S(1)}, u32[]{:S(2)}, u32[]{:S(2)}) collective-permute-start(bf16[1408,512]{1,0:T(8,128)(2,1)} %get-tuple-element.73), channel_id=1, source_target_pairs={{0,16},{8,24},{16,0},{24,8},{1,17},{9,25},{17,1},{25,9},{2,18},{10... | collective-permute-start | bytes 4325384 | tf_op jit(solution)/shard_map/ppermute | solution.py:1553
  234.7 74.6 %copy-start.4 = (bf16[1408,512]{1,0:T(8,128)(2,1)S(1)}, bf16[1408,512]{1,0:T(8,128)(2,1)}, u32[]{:S(2)}) copy-start(bf16[1408,512]{1,0:T(8,128)(2,1)} %get-tuple-element.73) | copy-start | bytes 4325380
  402.6 14.2 %copy-start.3 = (bf16[1024,640]{1,0:T(8,128)(2,1)S(1)}, bf16[1024,640]{1,0:T(8,128)(2,1)}, u32[]{:S(2)}) copy-start(bf16[1024,640]{1,0:T(8,128)(2,1)} %get-tuple-element.78) | copy-start | bytes 3932164
  412.2 3.7 collective-permute-start.1
  416.0 3.7 collective-permute-start.2
  419.7 14.1 %collective-permute-start.3 = (f32[2,1024]{1,0:T(2,128)S(1)}, f32[2,1024]{1,0:T(2,128)S(1)}, u32[]{:S(2)}, u32[]{:S(2)}) collective-permute-start(f32[2,1024]{1,0:T(2,128)S(1)} %fusion.4), channel_id=1, source_target_pairs={{0,8},{8,0},{16,24},{24,16},{1,9},{9,1},{17,25},{25,17},{2,10},{10... | collective-permute-start | bytes 24584 | tf_op jit(solution)/shard_map/ppermute | solution.py:1553
  420.8 3.8 copy-start.2
  424.6 3.0 copy-start.1
  427.6 3.0 copy-start

commit v7 on v6

--- a/solution.py
+++ b/solution.py
@@ -201,7 +201,7 @@
         return carry
 
     def one_group(g, carry):
-        @pl.when(g == GROUPS - 1)
+        @pl.when(jnp.logical_and(g == GROUPS - 1, block >= n_ctx))
         def _():
             gate.hop(0)
             down.hop(1)
@@ -240,14 +240,21 @@
         return carry
 
     lax.fori_loop(0, GROUPS, one_group, 0)
+    lax.fori_loop(CHUNKS - per_group, CHUNKS, run, 0)
+
+    @pl.when(block < n_ctx)
+    def _():
+        gate.hop(0)
+        down.hop(1)
+
     hops = len(high_bits(n_ctx))
     later = [(down, j) for j in range(2, hops)] + [(gate, 1), (up, 0)]
     for j in range(1, hops):
         later += [(up, j)] + ([(gate, j + 1)] if j + 1 < hops else [])
-    at = CHUNKS - per_group
+    at = CHUNKS
     rest = steps - at
     for i, (relay, j) in enumerate(later):
-        to = CHUNKS - per_group + (rest * (2 * i + 1)) // (2 * len(later))
+        to = CHUNKS + (rest * (2 * i + 1)) // (2 * len(later))
         lax.fori_loop(at, to, run, 0)
         at = to
         relay.hop(j)

time: 435 us -> 442 us (1.016)
  Pallas kernels: 400 us -> 407 us
    pallas_call x1, Pallas kernels: 81 us -> 86.6 us  [attend_sum(): pl.pallas_call(functools.partial(forward_kernel, n_ctx, n_head, span), ou...]
where the time goes in v7:
time: 442 us
  Pallas kernels  407 us (92%)
  other arithmetic  20.1 us (5%)
  local copies, waits for them, and re-layouts  7.79 us (2%)
    pallas_call x1, Pallas kernels, last_sum(): pl.pallas_call(functools.partial(last_kernel, n_ctx, n_head), out_shape=(...  91.9 us
    pallas_call x1, Pallas kernels, ffn_sum(): pl.pallas_call(functools.partial(ffn_kernel, n_head), out_shape=(wide, na...  86.9 us
    pallas_call x1, Pallas kernels, attend_sum(): pl.pallas_call(functools.partial(forward_kernel, n_ctx, n_head, span), ou...  86.6 us
    pallas_call x1, Pallas kernels, attend_back(): pl.pallas_call(functools.partial(backward_kernel, n_ctx, n_head, group, s...  75.4 us
    pallas_call x1, Pallas kernels, project(): pl.pallas_call(functools.partial(project_kernel, n_ctx), out_shape=(jax.S...  47.5 us
    pallas_call x2, Pallas kernels, by_rows(): pl.pallas_call(kernel, out_shape=tuple(outs) + (gain,), grid_spec=pltpu.P...  18.7 us
  transfers between devices with their start and end apart: 4, of which 2 were waited for; matrix products, arithmetic and copies ran while one was open for 4% of the time, Pallas kernels for 19%

profile of v7, /device:TPU:0, one launch (start us, length us, event | category | flops | bytes accessed | tf_op | source)
XLA Modules:
  0.0 441.8 jit_solution(6549879575453281490)
XLA Ops:
  0.7 0.7 stack.16
  1.4 0.7 stack.17
  2.1 1.1 copy.23
  3.1 1.1 copy.24
  4.2 0.6 maximum_convert_fusion.gain_ref
  4.8 2.5 pad_maximum_fusion.w_ref.w_l
  7.3 1.8 negate_select_fusion
  9.1 47.5 %project.1 = (bf16[512,512]{1,0:T(8,128)(2,1)}, bf16[4096,128]{1,0:T(8,128)(2,1)}, bf16[512,2048]{1,0:T(8,128)(2,1)}, bf16[1024,640]{1,0:T(8,128)(2,1)}, f32[2,1...) custom-call(bf16[512,2048]{1,0:T(8,128)(2,1)} %x_ref.7, ...), custom_call_target="tpu_custom_call" | custom-call | tf_op jit(solution)/shard_map/project/pallas_call | solution.py:693
  56.7 86.6 %attend_sum.1 = (bf16[512,512]{1,0:T(8,128)(2,1)}, f32[8,1,512]{2,1,0:T(1,128)}, bf16[512,2048]{1,0:T(8,128)(2,1)}, bf16[1024,1408]{1,0:T(8,128)(2,1)}, bf16[102...) custom-call(bf16[512,512]{1,0:T(8,128)(2,1)} %get-tuple-element.48.q_ref, ...), custom_call_target="tpu_custom_call", output_to_operand_aliasing={{5}: (6, {})} | custom-call | flops 49999998976 | bytes 8388608 | tf_op jit(solution)/shard_map/attend_sum/pallas_call | solution.py:280
  143.3 86.9 %ffn_sum.1 = (bf16[512,2048]{1,0:T(8,128)(2,1)}, bf16[512,1024]{1,0:T(8,128)(2,1)}, bf16[512,1024]{1,0:T(8,128)(2,1)}, bf16[1408,512]{1,0:T(8,128)(2,1)}, bf16[2...) custom-call(bf16[512,2048]{1,0:T(8,128)(2,1)} %x_ref.7, bf16[512,2048]{1,0:T(8,128)(2,1)} %get-tuple-element.52.mix_ref, ...), custom_call_target="tpu_custom_call" | custom-call | flops 49999998976 | bytes 8388608 | tf_op jit(solution)/shard_map/ffn_sum/pallas_call | solution.py:1443
  230.2 0.1 collective-permute-start
  230.3 9.9 %shard_map.194 = (f32[512,2048]{1,0:T(8,128)}, bf16[512,2048]{1,0:T(8,128)(2,1)}, bf16[512,512]{1,0:T(8,128)(2,1)}, f32[8,2048]{1,0:T(8,128)}) custom-call(s32[1]{0:T(128)} %bitcast.at_ref, bf16[512,2048]{1,0:T(8,128)(2,1)} %x_ref.7, bf16[512,2048]{1,0:T(8,128)(2,1)} %get-tuple-element.52.mix_ref, bf16[512,2048]{1,0:T(8,128)(2,1)} %get-tuple-element.57.grad_ref, ...), custom_call_target="tpu_custom_call" | custom-call | flops 4000000000 | bytes 25165824 | tf_op jit(solution)/shard_map/pallas_call | solution.py:1546
  240.2 0.0 copy-start.4
  240.2 75.4 %attend_backward.1 = (f32[512,512]{1,0:T(8,128)}, f32[4096,128]{1,0:T(8,128)}, bf16[512,2048]{1,0:T(8,128)(2,1)}, bf16[512,1408]{1,0:T(8,128)(2,1)}, bf16[512,1408]{1,0:T(8,128)(2,1)}) custom-call(bf16[512,512]{1,0:T(8,128)(2,1)} %get-tuple-element.48.q_ref, bf16[512,512]{1,0:T(8,128)(2,1)} %get-tuple-element.58.g_ref, ...), custom_call_target="tpu_custom_call" | custom-call | flops 34359738368 | bytes 2097152 | tf_op jit(solution)/shard_map/attend_backward/pallas_call | solution.py:475
  315.6 0.8 slice.31
  316.5 0.0 collective-permute-done
  316.5 0.0 copy-done.4
  316.5 1.5 add_convert_fusion.down_ref
  318.0 91.9 %last_sum.1 = (bf16[512,2048]{1,0:T(8,128)(2,1)}, bf16[1024,640]{1,0:T(8,128)(2,1)}, bf16[512,1024]{1,0:T(8,128)(2,1)}, bf16[1024,1408]{1,0:T(8,128)(2,1)}, bf16...) custom-call(f32[512,512]{1,0:T(8,128)} %get-tuple-element.66.dq_ref, f32[4096,128]{1,0:T(8,128)} %get-tuple-element.67.part_ref, ...), custom_call_target="tpu_custom_call" | custom-call | flops 49999998976 | bytes 8388608 | tf_op jit(solution)/shard_map/last_sum/pallas_call | solution.py:1110
  409.9 0.0 copy-start.3
  409.9 8.8 %shard_map.195 = (bf16[512,2048]{1,0:T(8,128)(2,1)}, f32[512,2048]{1,0:T(8,128)}, f32[8,2048]{1,0:T(8,128)}) custom-call(s32[1]{0:T(128)} %bitcast.at_ref, bf16[512,2048]{1,0:T(8,128)(2,1)} %x_ref.7, bf16[512,2048]{1,0:T(8,128)(2,1)} %get-tuple-element.52.mix_ref, bf16[512,2048]{1,0:T(8,128)(2,1)} %get-tuple-element.65.ffn_ref, ...), custom_call_target="tpu_custom_call" | custom-call | flops 4000000000 | bytes 25165824 | tf_op jit(solution)/shard_map/pallas_call | solution.py:1546
  418.7 0.8 slice.30
  419.6 2.0 collective-permute-start.1
  421.6 1.7 collective-permute-done.1
  423.3 0.8 collective-permute-start.2
  424.1 0.0 copy-done.3
  424.1 1.6 slice_convert_fusion
  425.7 1.3 collective-permute-done.2
  427.1 0.1 collective-permute-start.3
  427.1 0.1 slice_convert_fusion.1
  427.3 0.9 copy.26
  428.2 0.0 copy-start.2
  428.2 0.9 copy.25
  429.1 2.9 convert_element_type.50
  431.9 0.0 copy-done.2
  431.9 0.0 copy-start.1
  431.9 2.9 convert_element_type.51
  434.8 0.1 copy-done.1
  434.9 0.0 copy-start
  434.9 2.9 convert_element_type.52
  437.8 0.1 copy-done
  437.9 3.2 convert_element_type.53
  441.2 0.0 collective-permute-done.3
  441.2 0.6 fusion.3
  (8 shorter events, 0.1 us)
Async XLA Ops:
  230.2 86.3 %collective-permute-start = (bf16[1408,512]{1,0:T(8,128)(2,1)}, bf16[1408,512]{1,0:T(8,128)(2,1)S(1)}, u32[]{:S(2)}, u32[]{:S(2)}) collective-permute-start(bf16[1408,512]{1,0:T(8,128)(2,1)} %get-tuple-element.73), channel_id=1, source_target_pairs={{0,16},{8,24},{16,0},{24,8},{1,17},{9,25},{17,1},{25,9},{2,18},{10... | collective-permute-start | bytes 4325384 | tf_op jit(solution)/shard_map/ppermute | solution.py:1560
  240.2 76.3 %copy-start.4 = (bf16[1408,512]{1,0:T(8,128)(2,1)S(1)}, bf16[1408,512]{1,0:T(8,128)(2,1)}, u32[]{:S(2)}) copy-start(bf16[1408,512]{1,0:T(8,128)(2,1)} %get-tuple-element.73) | copy-start | bytes 4325380
  409.9 14.2 %copy-start.3 = (bf16[1024,640]{1,0:T(8,128)(2,1)S(1)}, bf16[1024,640]{1,0:T(8,128)(2,1)}, u32[]{:S(2)}) copy-start(bf16[1024,640]{1,0:T(8,128)(2,1)} %get-tuple-element.78) | copy-start | bytes 3932164
  419.6 3.7 collective-permute-start.1
  423.3 3.7 collective-permute-start.2
  427.1 14.1 %collective-permute-start.3 = (f32[2,1024]{1,0:T(2,128)S(1)}, f32[2,1024]{1,0:T(2,128)S(1)}, u32[]{:S(2)}, u32[]{:S(2)}) collective-permute-start(f32[2,1024]{1,0:T(2,128)S(1)} %fusion.4), channel_id=1, source_target_pairs={{0,8},{8,0},{16,24},{24,16},{1,9},{9,1},{17,25},{25,17},{2,10},{10... | collective-permute-start | bytes 24584 | tf_op jit(solution)/shard_map/ppermute | solution.py:1560
  428.2 3.8 copy-start.2
  431.9 3.0 copy-start.1
  434.9 3.0 copy-start
